TPU v7x, 32 devices: a whole 2x2x4 slice. The times are simulated.
32 devices in a mesh: bank: 4 (over z), zero: 8 (over y, x, core).
Axes of the slice: x: 2, y: 2, z: 4, core: 2. Of those that a mesh axis runs over, the one named last changes fastest.
Arguments:
- w_gate: float32 [128, 2048, 768], P('bank', 'zero'), may hold values from -0.1875 to 0.1875
- w_up: float32 [128, 2048, 768], P('bank', 'zero'), may hold values from -0.1875 to 0.1875
- router_weight: float32 [2048, 128], P('zero', 'bank'), may hold values from -0.125 to 0.125
- router_gain: float32 [2048], P('zero'), may hold values from 0.25 to 1.75
Outputs:
- serve_gate: bfloat16 [128, 2048, 768], P('bank', None, 'zero')
- serve_up: bfloat16 [128, 2048, 768], P('bank', None, 'zero')
- scale_gate: float32 [128, 768], P('bank', 'zero')
- scale_up: float32 [128, 768], P('bank', 'zero')
- serve_router: bfloat16 [2048, 128], replicated
All inputs are finite; a program needn't handle non-finite values.
Results may differ from a plain program's by a relative error of at most 0.001.
Values may be sent and summed in bfloat16 or wider, within the bound.
No kernel may reach another device: no remote copies, remote signals or barrier semaphores. Data moves between devices by JAX's collectives and lax.ppermute only.
A program may use at most 192 MiB of HBM per device.

v0:
```python
import jax
import jax.numpy as jnp
from jax import lax
from jax.sharding import PartitionSpec as P


def shards(w_gate, w_up, router_weight, router_gain):
    total_gate, total_up = lax.psum(
        (jnp.sum(w_gate * w_gate, axis=1), jnp.sum(w_up * w_up, axis=1)), "zero"
    )
    scale_gate = jnp.sqrt(total_gate)
    scale_up = jnp.sqrt(total_up)
    narrow_gate, narrow_up = (
        (w_gate / jnp.expand_dims(scale_gate, 1)).astype(jnp.bfloat16),
        (w_up / jnp.expand_dims(scale_up, 1)).astype(jnp.bfloat16),
    )
    serve_gate, serve_up = (
        lax.all_to_all(narrow_gate, "zero", split_axis=2, concat_axis=1, tiled=True),
        lax.all_to_all(narrow_up, "zero", split_axis=2, concat_axis=1, tiled=True),
    )
    scale_gate = lax.dynamic_slice_in_dim(
        scale_gate, lax.axis_index("zero") * serve_gate.shape[2], serve_gate.shape[2], axis=1
    )
    scale_up = lax.dynamic_slice_in_dim(
        scale_up, lax.axis_index("zero") * serve_up.shape[2], serve_up.shape[2], axis=1
    )
    part_router = (router_weight * router_gain[:, None]).astype(jnp.bfloat16)
    row_router = lax.all_gather(part_router, "zero", axis=0, tiled=True)
    serve_router = lax.all_gather(row_router, "bank", axis=1, tiled=True)
    return (serve_gate, serve_up, scale_gate, scale_up, serve_router)


def solution(mesh):
    placed = (P("bank", "zero", None), P("bank", "zero", None), P("zero", "bank"), P("zero"))
    return jax.shard_map(
        shards,
        mesh=mesh,
        in_specs=placed,
        out_specs=(
            P("bank", None, "zero"),
            P("bank", None, "zero"),
            P("bank", "zero"),
            P("bank", "zero"),
            P(),
        ),
        check_vma=False,
    )
```

profile of v0, /device:TPU:0, one launch (start us, length us, event | category | flops | bytes accessed | tf_op | source)
XLA Modules:
  0.0 481.0 jit_solution(10650282860068963028)
XLA Ops:
  7.2 0.0 all-reduce.3.cloned.1.call-start
  7.2 17.3 %multiply_reduce_fusion = (f32[32,768]{1,0:T(8,128)}, f32[32,768]{1,0:T(8,128)}) fusion(f32[32,256,768]{2,1,0:T(8,128)} %param.5, f32[32,256,768]{2,1,0:T(8,128)} %param.4), kind=kLoop, calls=%fused_computation.1 | loop fusion | flops 25116672 | bytes 50528256 | tf_op jit(solution)/shard_map/reduce_sum | solution.py:9
  24.5 0.0 all-reduce.3.cloned.1.call-update
  24.5 25.1 %copy.25 = f32[32,256,768]{1,0,2:T(8,128)} copy(f32[32,256,768]{2,1,0:T(8,128)} %param.5) | data formatting | bytes 50331648 | tf_op args[1]
  49.6 31.5 %all-reduce.3.cloned.1.call-done = (f32[32,768]{1,0:T(8,128)}, f32[32,768]{1,0:T(8,128)}) async-done(((f32[32,768]{1,0:T(8,128)}, f32[32,768]{1,0:T(8,128)}), (f32[32,768]{1,0:T(8,128)}, f32[32,768]{1,0:T(8,128)})) %all-reduce.3.cloned.1.call-update) | async-done | bytes 196624 | tf_op jit(solution)/shard_map/psum | solution.py:8
  81.1 0.9 sqrt.7
  82.1 0.2 copy.24
  82.2 14.1 %divide_convert_fusion = bf16[32,256,768]{1,0,2:T(8,128)(2,1)} fusion(f32[32,256,768]{1,0,2:T(8,128)} %copy.25, f32[32,768]{0,1:T(8,128)S(1)} %copy.24), kind=kLoop, calls=%fused_computation | loop fusion | flops 12582912 | bytes 37847040 | tf_op jit(solution)/shard_map/convert_element_type | solution.py:15
  96.4 5.4 %all-to-all-start.1 = ((bf16[32,256,768]{1,0,2:T(8,128)(2,1)}), bf16[32,256,768]{1,0,2:T(8,128)(2,1)}, u32[]{:S(2)}, u32[]{:S(2)}) async-start(bf16[32,256,768]{1,0,2:T(8,128)(2,1)} %divide_convert_fusion), calls=%async_computation.1 | async-start | bytes 25165824 | tf_op jit(solution)/shard_map/all_to_all | solution.py:19
  101.8 0.0 copy-start
  101.8 25.1 %copy.21 = f32[32,256,768]{1,0,2:T(8,128)} copy(f32[32,256,768]{2,1,0:T(8,128)} %param.4) | data formatting | bytes 50331648 | tf_op args[0]
  126.9 0.0 copy-done
  126.9 0.2 copy.20
  127.1 0.0 copy-start.1
  127.1 0.0 copy-start.2
  127.1 14.1 %divide_convert_fusion.1 = bf16[32,256,768]{1,0,2:T(8,128)(2,1)} fusion(f32[32,256,768]{1,0,2:T(8,128)} %copy.21, f32[32,768]{0,1:T(8,128)S(1)} %copy.20), kind=kLoop, calls=%fused_computation.2 | loop fusion | flops 12582912 | bytes 37847040 | tf_op jit(solution)/shard_map/convert_element_type | solution.py:14
  141.3 99.5 %all-to-all-done.1 = bf16[32,256,768]{1,0,2:T(8,128)(2,1)} async-done(((bf16[32,256,768]{1,0,2:T(8,128)(2,1)}), bf16[32,256,768]{1,0,2:T(8,128)(2,1)}, u32[]{:S(2)}, u32[]{:S(2)}) %all-to-all-start.1) | async-done | bytes 12582944 | tf_op jit(solution)/shard_map/all_to_all | solution.py:19
  240.8 5.4 %all-to-all-start = ((bf16[32,256,768]{1,0,2:T(8,128)(2,1)}), bf16[32,256,768]{1,0,2:T(8,128)(2,1)}, u32[]{:S(2)}, u32[]{:S(2)}) async-start(bf16[32,256,768]{1,0,2:T(8,128)(2,1)} %divide_convert_fusion.1), calls=%async_computation | async-start | bytes 25165824 | tf_op jit(solution)/shard_map/all_to_all | solution.py:18
  246.1 0.0 copy-done.1
  246.1 0.0 copy-done.2
  246.2 142.4 %all_gather.6 = bf16[2048,32]{0,1:T(8,128)(2,1)S(1)} all-gather(bf16[256,32]{0,1:T(8,128)(2,1)S(1)} %multiply_convert_fusion), channel_id=1, replica_groups=mesh['bank'=4,'zero'=8] {'zero'}, dimensions={0}, use_global_device_ids=true | all-gather | bytes 147456 | tf_op jit(solution)/shard_map/all_gather | solution.py:28
  388.6 16.1 %all_gather.7 = bf16[2048,128]{0,1:T(8,128)(2,1)S(1)} all-gather(bf16[2048,32]{0,1:T(8,128)(2,1)S(1)} %all_gather.6), channel_id=1, replica_groups=mesh['bank'=4,'zero'=8] {'bank'}, dimensions={1}, use_global_device_ids=true | all-gather | bytes 655360 | tf_op jit(solution)/shard_map/all_gather | solution.py:29
  404.6 1.0 copy.28
  405.6 0.7 constant_dynamic-slice_fusion
  406.3 0.7 constant_dynamic-slice_fusion.1
  407.0 14.1 %copy.27 = bf16[32,8,256,96]{2,1,3,0:T(8,128)(2,1)} copy(bf16[32,8,256,96]{2,0,3,1:T(8,128)(2,1)} %bitcast.5) | data formatting | bytes 25165824 | tf_op jit(solution)/shard_map/all_to_all | solution.py:19
  421.1 19.5 %all_to_all.33 = bf16[32,2048,96]{1,2,0:T(8,128)(2,1)} reshape(bf16[32,8,256,96]{2,1,3,0:T(8,128)(2,1)} %copy.27) | data formatting | bytes 25165824 | tf_op jit(solution)/shard_map/all_to_all | solution.py:19
  440.6 0.0 all-to-all-done
  440.6 14.1 %copy.23 = bf16[32,8,256,96]{2,1,3,0:T(8,128)(2,1)} copy(bf16[32,8,256,96]{2,0,3,1:T(8,128)(2,1)} %bitcast.2) | data formatting | bytes 25165824 | tf_op jit(solution)/shard_map/all_to_all | solution.py:18
  454.7 19.5 %all_to_all.29 = bf16[32,2048,96]{1,2,0:T(8,128)(2,1)} reshape(bf16[32,8,256,96]{2,1,3,0:T(8,128)(2,1)} %copy.23) | data formatting | bytes 25165824 | tf_op jit(solution)/shard_map/all_to_all | solution.py:18
  (2 shorter events, 0.0 us)
Async XLA Ops:
  7.2 74.0 %all-reduce.3.cloned.1.call-start = ((), (), s32[]{:S(2)}) async-start(), calls=%async_computation.2 | async-start | bytes 393216 | tf_op jit(solution)/shard_map/psum | solution.py:8
  96.4 144.4 %all-to-all-start.1 = ((bf16[32,256,768]{1,0,2:T(8,128)(2,1)}), bf16[32,256,768]{1,0,2:T(8,128)(2,1)}, u32[]{:S(2)}, u32[]{:S(2)}) async-start(bf16[32,256,768]{1,0,2:T(8,128)(2,1)} %divide_convert_fusion), calls=%async_computation.1 | async-start | bytes 25165824 | tf_op jit(solution)/shard_map/all_to_all | solution.py:19
  101.8 25.1 %copy-start = (f32[32,768]{1,0:T(8,128)S(1)}, f32[32,768]{1,0:T(8,128)}, u32[]{:S(2)}) copy-start(f32[32,768]{1,0:T(8,128)} %get-tuple-element.10) | copy-start | bytes 294916
  127.1 119.0 %copy-start.1 = (f32[256,32]{0,1:T(8,128)S(1)}, f32[256,32]{0,1:T(8,128)}, u32[]{:S(2)}) copy-start(f32[256,32]{0,1:T(8,128)} %param.6) | copy-start | bytes 98308
  127.1 119.0 %copy-start.2 = (f32[256]{0:T(256)S(1)}, f32[256]{0:T(256)}, u32[]{:S(2)}) copy-start(f32[256]{0:T(256)} %param.7) | copy-start | bytes 3076
  240.8 199.8 %all-to-all-start = ((bf16[32,256,768]{1,0,2:T(8,128)(2,1)}), bf16[32,256,768]{1,0,2:T(8,128)(2,1)}, u32[]{:S(2)}, u32[]{:S(2)}) async-start(bf16[32,256,768]{1,0,2:T(8,128)(2,1)} %divide_convert_fusion.1), calls=%async_computation | async-start | bytes 25165824 | tf_op jit(solution)/shard_map/all_to_all | solution.py:18
Sparse Core Ops, SparseCore 0:
  24.6 56.4 all-reduce.2
where the time goes:
time: 483 us; the launch traced here: 481 us
  blocking collectives  158 us (33%)
  waiting for transfers between devices  131 us (27%)
  local copies, waits for them, and re-layouts  121 us (25%)
  other arithmetic  45.5 us (9%)
  between operations  14.1 us (3%)
  starting transfers between devices  10.8 us (2%)
    all_gather x1, blocking collectives, shards(): row_router = lax.all_gather(part_router, 'zero', axis=0, tiled=True)  142 us
    all_to_all x1, waiting for transfers between devices, shards(): lax.all_to_all(narrow_up, 'zero', split_axis=2, concat_axis=1, tiled=True)  99.5 us
    unnamed x9, local copies, waits for them, and re-layouts  51.3 us
    all_to_all x2, local copies, waits for them, and re-layouts, shards(): lax.all_to_all(narrow_gate, 'zero', split_axis=2, concat_axis=1, tiled=True)  33.6 us
    all_to_all x2, local copies, waits for them, and re-layouts, shards(): lax.all_to_all(narrow_up, 'zero', split_axis=2, concat_axis=1, tiled=True)  33.6 us
    psum x1, waiting for transfers between devices, shards(): lax.psum((jnp.sum(w_gate * w_gate, axis=1), jnp.sum(w_up * w_up, axis=1))...  31.5 us
    reduce_sum x1, other arithmetic, shards(): jnp.sum(w_up * w_up, axis=1)  17.3 us
    all_gather x1, blocking collectives, shards(): serve_router = lax.all_gather(row_router, 'bank', axis=1, tiled=True)  16.1 us
  transfers between devices with their start and end apart: 3, of which 2 were waited for; matrix products, arithmetic and copies ran while one was open for 17% of the time, Pallas kernels for 0%

commit v1 on v0

v1 whole, which is shorter than its diff:
```python
import jax
import jax.numpy as jnp
from jax import lax
from jax.experimental import pallas as pl
from jax.experimental.pallas import tpu as pltpu
from jax.sharding import PartitionSpec as P


def xor_pairs(size, k):
    return [(i, i ^ k) for i in range(size)]


def cost(flops, moved):
    return pl.CostEstimate(flops=flops, bytes_accessed=moved, transcendentals=0)


def square_sums(w_gate, w_up, first, count):
    _, rows, cols = w_gate.shape
    per_step = 2 if count % 2 == 0 and first % 2 == 0 else 1

    def kernel(gate_ref, up_ref, out_ref):
        step = pl.program_id(0)
        for n in range(per_step):
            for side, ref in enumerate((gate_ref, up_ref)):
                w = ref[n]
                out_ref[side, pl.ds(step * per_step + n, 1), :] = jnp.sum(w * w, axis=0, keepdims=True)

    weights = pl.BlockSpec((per_step, rows, cols), lambda i: (first // per_step + i, 0, 0))
    return pl.pallas_call(
        kernel,
        grid=(count // per_step,),
        in_specs=[weights, weights],
        out_specs=pl.BlockSpec((2, count, cols), lambda i: (0, 0, 0)),
        out_shape=jax.ShapeDtypeStruct((2, count, cols), jnp.float32),
        cost_estimate=cost(4 * count * rows * cols, 8 * count * rows * cols),
    )(w_gate, w_up)


def scaled_pieces(w_gate, w_up, total, first, count, start, size):
    _, rows, cols = w_gate.shape
    width = cols // size

    def kernel(gate_ref, up_ref, total_ref, *refs):
        outs, held = refs[:size], refs[size]
        me = lax.axis_index("zero")
        step = pl.program_id(0)
        for side, ref in enumerate((gate_ref, up_ref)):
            inverse = 1.0 / jnp.sqrt(total_ref[side, pl.ds(start + step, 1), :])
            held[side] = (ref[0] * inverse).astype(jnp.bfloat16).T
            for k in range(size):
                offset = pl.multiple_of(lax.bitwise_xor(me, k) * width, width)
                outs[k][side, 0] = held[side, pl.ds(offset, width), :]

    weights = pl.BlockSpec((1, rows, cols), lambda i: (first + i, 0, 0))
    piece = pl.BlockSpec((2, 1, width, rows), lambda i: (0, i, 0, 0))
    return pl.pallas_call(
        kernel,
        grid=(count,),
        in_specs=[weights, weights, pl.BlockSpec(total.shape, lambda i: (0, 0, 0))],
        out_specs=[piece] * size,
        out_shape=[jax.ShapeDtypeStruct((2, count, width, rows), jnp.bfloat16)] * size,
        scratch_shapes=[pltpu.VMEM((2, cols, rows), jnp.bfloat16)],
        cost_estimate=cost(4 * count * rows * cols, 12 * count * rows * cols),
    )(w_gate, w_up, total)


def assembled(pieces, outputs, first, experts):
    size = len(pieces)
    _, count, width, rows = pieces[0].shape

    def kernel(*refs):
        ins, outs = refs[:size], refs[-2:]
        me = lax.axis_index("zero")
        for k in range(size):
            offset = pl.multiple_of(lax.bitwise_xor(me, k) * rows, rows)
            for side in range(2):
                outs[side][0, :, pl.ds(offset, rows)] = ins[k][side, 0]

    piece = pl.BlockSpec((2, 1, width, rows), lambda i: (0, i, 0, 0))
    whole = pl.BlockSpec((1, width, size * rows), lambda i: (first + i, 0, 0))
    kept = () if outputs is None else tuple(outputs)
    return pl.pallas_call(
        kernel,
        grid=(count,),
        in_specs=[piece] * size + [pl.BlockSpec(memory_space=pl.ANY)] * len(kept),
        out_specs=[whole, whole],
        out_shape=[jax.ShapeDtypeStruct((experts, width, size * rows), jnp.bfloat16)] * 2,
        input_output_aliases={size + n: n for n in range(len(kept))},
        cost_estimate=cost(count * width * rows * size, 8 * count * width * rows * size),
    )(*pieces, *kept)


def joined_rows(pieces):
    size = len(pieces)
    height, rows = pieces[0].shape

    def kernel(*refs):
        me = lax.axis_index("zero")
        for k in range(size):
            offset = pl.multiple_of(lax.bitwise_xor(me, k) * rows, rows)
            refs[size][:, pl.ds(offset, rows)] = refs[k][...]

    return pl.pallas_call(
        kernel,
        out_shape=jax.ShapeDtypeStruct((height, size * rows), pieces[0].dtype),
        cost_estimate=cost(size * height * rows, 4 * size * height * rows),
    )(*pieces)


def joined_columns(pieces):
    banks = len(pieces)
    height, rows = pieces[0].shape

    def kernel(*refs):
        out_ref, held = refs[banks], refs[banks + 1]
        me = lax.axis_index("bank")
        for k in range(banks):
            offset = pl.multiple_of(lax.bitwise_xor(me, k) * height, height)
            held[pl.ds(offset, height), :] = refs[k][...]
        out_ref[...] = held[...].T

    return pl.pallas_call(
        kernel,
        out_shape=jax.ShapeDtypeStruct((rows, banks * height), pieces[0].dtype),
        scratch_shapes=[pltpu.VMEM((banks * height, rows), pieces[0].dtype)],
        cost_estimate=cost(banks * height * rows, 4 * banks * height * rows),
    )(*pieces)


def chunk_sizes(experts):
    sizes, left = [], experts
    for part in (16, 8, 4, 4, 4, 8, 16):
        take = max(1, experts // part)
        sizes.append(min(take, left))
        left -= sizes[-1]
    if left:
        sizes[len(sizes) // 2] += left
    return [n for n in sizes if n]


def piped(w_gate, w_up, router_weight, router_gain, size, banks):
    experts, _, cols = w_gate.shape
    width = cols // size

    def send(x, k, axis="zero", count=size):
        return lax.ppermute(x, axis, xor_pairs(count, k))

    total = square_sums(w_gate, w_up, 0, experts)
    k = 1
    while k < size:
        total = total + send(total, k)
        k *= 2

    sizes = chunk_sizes(experts)
    chunks = range(len(sizes))
    firsts = [sum(sizes[:c]) for c in chunks]
    sent, got = [], [dict() for _ in chunks]
    for c in chunks:
        sent.append(scaled_pieces(w_gate, w_up, total, firsts[c], sizes[c], firsts[c], size))
        got[c] = [sent[c][0]] + [send(sent[c][k], k) for k in range(1, size)]

    part = (router_weight * router_gain[:, None]).astype(jnp.bfloat16).T
    row = joined_rows([part] + [send(part, k) for k in range(1, size)])
    columns = [row] + [send(row, k, "bank", banks) for k in range(1, banks)]
    serve_router = joined_columns(columns)

    outputs = None
    for c in chunks:
        outputs = assembled(got[c], outputs, firsts[c], experts)
    serve_gate, serve_up = (jnp.swapaxes(x, 1, 2) for x in outputs)

    mine = lax.dynamic_slice_in_dim(total, lax.axis_index("zero") * width, width, axis=2)
    scale = jnp.sqrt(mine)
    return (serve_gate, serve_up, scale[0], scale[1], serve_router)


def plain(w_gate, w_up, router_weight, router_gain):
    total_gate, total_up = lax.psum(
        (jnp.sum(w_gate * w_gate, axis=1), jnp.sum(w_up * w_up, axis=1)), "zero"
    )
    scale_gate, scale_up = jnp.sqrt(total_gate), jnp.sqrt(total_up)
    served = [
        lax.all_to_all(
            (w / jnp.expand_dims(scale, 1)).astype(jnp.bfloat16), "zero", split_axis=2, concat_axis=1, tiled=True
        )
        for w, scale in ((w_gate, scale_gate), (w_up, scale_up))
    ]
    width = served[0].shape[2]
    start = lax.axis_index("zero") * width
    scales = [lax.dynamic_slice_in_dim(s, start, width, axis=1) for s in (scale_gate, scale_up)]
    part = (router_weight * router_gain[:, None]).astype(jnp.bfloat16)
    row = lax.all_gather(part, "zero", axis=0, tiled=True)
    return (*served, *scales, lax.all_gather(row, "bank", axis=1, tiled=True))


def solution(mesh):
    size, banks = mesh.shape["zero"], mesh.shape["bank"]
    placed = (P("bank", "zero", None), P("bank", "zero", None), P("zero", "bank"), P("zero"))

    def placed_over(shards):
        return jax.shard_map(
            shards,
            mesh=mesh,
            in_specs=placed,
            out_specs=(
                P("bank", None, "zero"),
                P("bank", None, "zero"),
                P("bank", "zero"),
                P("bank", "zero"),
                P(),
            ),
            check_vma=False,
        )

    def whole(w_gate, w_up, router_weight, router_gain):
        _, rows, cols = w_gate.shape
        powers = size & (size - 1) == 0 and banks & (banks - 1) == 0
        aligned = rows % (128 * size) == 0 and cols % (16 * size) == 0 and router_weight.shape[1] % (16 * banks) == 0
        if not (powers and aligned and size >= 8):
            return placed_over(plain)(w_gate, w_up, router_weight, router_gain)

        def shards(*args):
            return piped(*args, size, banks)

        return placed_over(shards)(w_gate, w_up, router_weight, router_gain)

    return whole
```

time: 483 us -> 402 us (0.83)
  blocking collectives: 158 us -> 0 us
  local copies, waits for them, and re-layouts: 121 us -> 8.04 us
  Pallas kernels: 0 us -> 99.1 us
  waiting for transfers between devices: 131 us -> 225 us
  starting transfers between devices: 10.8 us -> 64.1 us
  other arithmetic: 45.5 us -> 1.69 us
  between operations: 14.1 us -> 1.1 us
    ppermute x0 -> x55, waiting for transfers between devices: none -> 225 us  [send(): return lax.ppermute(x, axis, xor_pairs(count, k))]
    all_gather x2 -> x0, blocking collectives: 158 us -> none  [the longest x1 142 us: shards(): row_router = lax.all_gather(part_router, 'zero', axis=0, tiled=True)]
    all_to_all x2 -> x0, waiting for transfers between devices: 99.5 us -> none  [the longest x1 99.5 us: shards(): lax.all_to_all(narrow_up, 'zero', split_axis=2, concat_axis=1, tiled=True)]
    pallas_call x0 -> x15, Pallas kernels: none -> 99.1 us  [the longest x6 41.7 us: scaled_pieces(): pl.pallas_call(kernel, grid=(count,), in_specs=[weights, weights, pl.Bloc...]
    all_to_all x4 -> x0, local copies, waits for them, and re-layouts: 67.1 us -> none  [the longest x2 33.6 us: shards(): lax.all_to_all(narrow_gate, 'zero', split_axis=2, concat_axis=1, tiled=True)]
    ppermute x0 -> x55, starting transfers between devices: none -> 64.1 us  [send(): return lax.ppermute(x, axis, xor_pairs(count, k))]
    unnamed x9 -> x86, local copies, waits for them, and re-layouts: 51.3 us -> 6.51 us
    psum x1 -> x0, waiting for transfers between devices: 31.5 us -> none  [shards(): lax.psum((jnp.sum(w_gate * w_gate, axis=1), jnp.sum(w_up * w_up, axis=1))...]
  transfers between devices with their start and end apart: 3 -> 55, of which waited for: 2 -> 20; matrix products, arithmetic and copies ran while one was open for 17% -> 0% of each run, Pallas kernels for 0% -> 18%
where the time goes in v1:
time: 402 us; the launch traced here: 399 us
  waiting for transfers between devices  225 us (56%)
  Pallas kernels  99.1 us (25%)
  starting transfers between devices  64.1 us (16%)
  local copies, waits for them, and re-layouts  8.04 us (2%)
    ppermute x55, waiting for transfers between devices, send(): return lax.ppermute(x, axis, xor_pairs(count, k))  225 us
    ppermute x55, starting transfers between devices, send(): return lax.ppermute(x, axis, xor_pairs(count, k))  64.1 us
    pallas_call x6, Pallas kernels, scaled_pieces(): pl.pallas_call(kernel, grid=(count,), in_specs=[weights, weights, pl.Bloc...  41.7 us
    pallas_call x6, Pallas kernels, assembled(): pl.pallas_call(kernel, grid=(count,), in_specs=[piece] * size + [pl.Block...  33.4 us
    pallas_call x1, Pallas kernels, square_sums(): pl.pallas_call(kernel, grid=(count // per_step,), in_specs=[weights, weig...  20.4 us
  transfers between devices with their start and end apart: 55, of which 20 were waited for; matrix products, arithmetic and copies ran while one was open for 0% of the time, Pallas kernels for 18%

profile of v1, /device:TPU:0, one launch (start us, length us, event | category | flops | bytes accessed | tf_op | source)
XLA Modules:
  0.0 399.1 jit_solution(7363522919678620299)
XLA Ops:
  0.6 20.4 %shard_map.83 = f32[2,32,768]{2,1,0:T(8,128)} custom-call(f32[32,256,768]{2,1,0:T(8,128)} %gate_ref.13, f32[32,256,768]{2,1,0:T(8,128)} %up_ref.13), custom_call_target="tpu_custom_call" | custom-call | flops 25165824 | bytes 50331648 | tf_op jit(solution)/shard_map/pallas_call | solution.py:29
  21.5 1.3 collective-permute-done
  23.8 2.9 collective-permute-start.1
  26.7 5.2 %collective-permute-done.1 = f32[2,32,768]{2,1,0:T(8,128)S(1)} collective-permute-done((f32[2,32,768]{2,1,0:T(8,128)S(1)}, f32[2,32,768]{2,1,0:T(8,128)S(1)}, u32[]{:S(2)}, u32[]{:S(2)}) %collective-permute-start.1) | collective-permute-done | bytes 196640 | tf_op jit(solution)/shard_map/ppermute | solution.py:146
  31.9 1.8 collective-permute-start.2
  33.7 4.6 %collective-permute-done.2 = f32[2,32,768]{2,1,0:T(8,128)S(1)} collective-permute-done((f32[2,32,768]{2,1,0:T(8,128)S(1)}, f32[2,32,768]{2,1,0:T(8,128)S(1)}, u32[]{:S(2)}, u32[]{:S(2)}) %collective-permute-start.2) | collective-permute-done | bytes 196640 | tf_op jit(solution)/shard_map/ppermute | solution.py:146
  39.0 3.1 shard_map.89
  42.2 1.5 collective-permute-start.39
  44.6 1.1 collective-permute-start.47
  45.7 1.5 collective-permute-start.48
  47.2 3.0 collective-permute-done.46.refs_2_
  50.8 2.0 collective-permute-start.50
  52.8 1.4 collective-permute-start.51
  54.1 1.3 collective-permute-done.50.refs_6_
  55.4 1.4 collective-permute-done.51.refs_7_
  57.5 1.5 shard_map.96.refs_0_
  59.0 1.6 collective-permute-start.52
  60.6 2.6 collective-permute-start.53
  63.4 3.5 collective-permute-done.52.refs_1_
  66.9 6.8 %collective-permute-done.53.refs_2_ = bf16[32,2048]{1,0:T(8,128)(2,1)S(1)} collective-permute-done((bf16[32,2048]{1,0:T(8,128)(2,1)}, bf16[32,2048]{1,0:T(8,128)(2,1)S(1)}, u32[]{:S(2)}, u32[]{:S(2)}) %collective-permute-start.53) | collective-permute-done | bytes 131104 | tf_op jit(solution)/shard_map/ppermute | solution.py:146
  74.7 1.2 collective-permute-start.43
  75.9 2.3 collective-permute-start.44
  78.2 3.2 shard_map.84
  81.4 5.4 %shard_map.88 = (bf16[2,4,96,256]{3,2,1,0:T(8,128)(2,1)}, bf16[2,4,96,256]{3,2,1,0:T(8,128)(2,1)}, bf16[2,4,96,256]{3,2,1,0:T(8,128)(2,1)}, bf16[2,4,96,256]{3,2...) custom-call(f32[32,256,768]{2,1,0:T(8,128)} %gate_ref.13, ...), custom_call_target="tpu_custom_call" | custom-call | flops 3145728 | bytes 9437184 | tf_op jit(solution)/shard_map/pallas_call | solution.py:56
  86.9 2.8 collective-permute-done.41.refs_4_
  90.8 1.2 collective-permute-start.3
  93.6 10.0 %shard_map.87 = (bf16[2,8,96,256]{3,2,1,0:T(8,128)(2,1)}, bf16[2,8,96,256]{3,2,1,0:T(8,128)(2,1)}, bf16[2,8,96,256]{3,2,1,0:T(8,128)(2,1)}, bf16[2,8,96,256]{3,2...) custom-call(f32[32,256,768]{2,1,0:T(8,128)} %gate_ref.13, ...), custom_call_target="tpu_custom_call" | custom-call | flops 6291456 | bytes 18874368 | tf_op jit(solution)/shard_map/pallas_call | solution.py:56
  104.3 1.4 collective-permute-start.4
  105.8 5.5 %collective-permute-done.4.refs_2_ = bf16[2,2,96,256]{3,2,1,0:T(8,128)(2,1)S(1)} collective-permute-done((bf16[2,2,96,256]{3,2,1,0:T(8,128)(2,1)}, bf16[2,2,96,256]{3,2,1,0:T(8,128)(2,1)S(1)}, u32[]{:S(2)}, u32[]{:S(2)}) %collective-permute-start.4) | collective-permute-done | bytes 196640 | tf_op jit(solution)/shard_map/ppermute | solution.py:146
  113.2 1.8 collective-permute-start.36
  115.1 1.5 collective-permute-start.37
  116.5 24.3 %collective-permute-done.34.refs_4_ = bf16[2,4,96,256]{3,2,1,0:T(8,128)(2,1)S(1)} collective-permute-done((bf16[2,4,96,256]{3,2,1,0:T(8,128)(2,1)S(1)}, bf16[2,4,96,256]{3,2,1,0:T(8,128)(2,1)S(1)}, u32[]{:S(2)}, u32[]{:S(2)}) %collective-permute-start.34) | collective-permute-done | bytes 393248 | tf_op jit(solution)/shard_map/ppermute | solution.py:146
  140.9 1.5 collective-permute-start.25
  142.3 3.7 collective-permute-done.35.refs_5_
  146.8 2.5 collective-permute-start.26
  152.9 10.0 %shard_map.86 = (bf16[2,8,96,256]{3,2,1,0:T(8,128)(2,1)}, bf16[2,8,96,256]{3,2,1,0:T(8,128)(2,1)}, bf16[2,8,96,256]{3,2,1,0:T(8,128)(2,1)}, bf16[2,8,96,256]{3,2...) custom-call(f32[32,256,768]{2,1,0:T(8,128)} %gate_ref.13, ...), custom_call_target="tpu_custom_call" | custom-call | flops 6291456 | bytes 18874368 | tf_op jit(solution)/shard_map/pallas_call | solution.py:56
  163.0 1.7 collective-permute-start.30
  164.7 12.8 %collective-permute-done.26.refs_3_ = bf16[2,8,96,256]{3,2,1,0:T(8,128)(2,1)S(1)} collective-permute-done((bf16[2,8,96,256]{3,2,1,0:T(8,128)(2,1)}, bf16[2,8,96,256]{3,2,1,0:T(8,128)(2,1)S(1)}, u32[]{:S(2)}, u32[]{:S(2)}) %collective-permute-start.26) | collective-permute-done | bytes 786464 | tf_op jit(solution)/shard_map/ppermute | solution.py:146
  177.4 1.2 collective-permute-start.17
  178.6 1.4 collective-permute-start.18
  180.0 38.0 %collective-permute-done.28.refs_5_ = bf16[2,8,96,256]{3,2,1,0:T(8,128)(2,1)} collective-permute-done((bf16[2,8,96,256]{3,2,1,0:T(8,128)(2,1)}, bf16[2,8,96,256]{3,2,1,0:T(8,128)(2,1)}, u32[]{:S(2)}, u32[]{:S(2)}) %collective-permute-start.28) | collective-permute-done | bytes 786464 | tf_op jit(solution)/shard_map/ppermute | solution.py:146
  218.0 2.5 collective-permute-start.19
  221.5 10.0 %shard_map.85 = (bf16[2,8,96,256]{3,2,1,0:T(8,128)(2,1)}, bf16[2,8,96,256]{3,2,1,0:T(8,128)(2,1)}, bf16[2,8,96,256]{3,2,1,0:T(8,128)(2,1)}, bf16[2,8,96,256]{3,2...) custom-call(f32[32,256,768]{2,1,0:T(8,128)} %gate_ref.13, ...), custom_call_target="tpu_custom_call" | custom-call | flops 6291456 | bytes 18874368 | tf_op jit(solution)/shard_map/pallas_call | solution.py:56
  231.6 1.2 collective-permute-start.22
  232.8 2.2 collective-permute-start.23
  235.0 8.3 %collective-permute-done.19.refs_3_ = bf16[2,8,96,256]{3,2,1,0:T(8,128)(2,1)} collective-permute-done((bf16[2,8,96,256]{3,2,1,0:T(8,128)(2,1)}, bf16[2,8,96,256]{3,2,1,0:T(8,128)(2,1)}, u32[]{:S(2)}, u32[]{:S(2)}) %collective-permute-start.19) | collective-permute-done | bytes 786464 | tf_op jit(solution)/shard_map/ppermute | solution.py:146
  243.8 2.0 collective-permute-start.11
  245.8 42.6 %collective-permute-done.21.refs_5_ = bf16[2,8,96,256]{3,2,1,0:T(8,128)(2,1)S(1)} collective-permute-done((bf16[2,8,96,256]{3,2,1,0:T(8,128)(2,1)}, bf16[2,8,96,256]{3,2,1,0:T(8,128)(2,1)S(1)}, u32[]{:S(2)}, u32[]{:S(2)}) %collective-permute-start.21) | collective-permute-done | bytes 786464 | tf_op jit(solution)/shard_map/ppermute | solution.py:146
  288.5 2.5 collective-permute-start.12
  292.8 1.3 collective-permute-start.15
  294.2 1.3 collective-permute-start.16
  295.4 2.1 shard_map.97
  298.5 10.7 %collective-permute-done.12.refs_3_ = bf16[2,8,96,256]{3,2,1,0:T(8,128)(2,1)} collective-permute-done((bf16[2,8,96,256]{3,2,1,0:T(8,128)(2,1)}, bf16[2,8,96,256]{3,2,1,0:T(8,128)(2,1)}, u32[]{:S(2)}, u32[]{:S(2)}) %collective-permute-start.12) | collective-permute-done | bytes 786464 | tf_op jit(solution)/shard_map/ppermute | solution.py:146
  309.2 2.2 collective-permute-start.5
  311.4 34.0 %collective-permute-done.13.refs_4_ = bf16[2,8,96,256]{3,2,1,0:T(8,128)(2,1)} collective-permute-done((bf16[2,8,96,256]{3,2,1,0:T(8,128)(2,1)}, bf16[2,8,96,256]{3,2,1,0:T(8,128)(2,1)}, u32[]{:S(2)}, u32[]{:S(2)}) %collective-permute-start.13) | collective-permute-done | bytes 786464 | tf_op jit(solution)/shard_map/ppermute | solution.py:146
  346.4 14.4 %collective-permute-done.14.refs_5_ = bf16[2,8,96,256]{3,2,1,0:T(8,128)(2,1)} collective-permute-done((bf16[2,8,96,256]{3,2,1,0:T(8,128)(2,1)}, bf16[2,8,96,256]{3,2,1,0:T(8,128)(2,1)}, u32[]{:S(2)}, u32[]{:S(2)}) %collective-permute-start.14) | collective-permute-done | bytes 786464 | tf_op jit(solution)/shard_map/ppermute | solution.py:146
  360.7 1.9 collective-permute-start.7
  362.6 1.3 collective-permute-start.8
  364.9 2.5 shard_map.90
  367.4 4.4 %shard_map.91 = (bf16[32,96,2048]{2,1,0:T(8,128)(2,1)}, bf16[32,96,2048]{2,1,0:T(8,128)(2,1)}) custom-call(bf16[2,4,96,256]{3,2,1,0:T(8,128)(2,1)} %get-tuple-element.97.refs_0_, bf16[2,4,96,256]{3,2,1,0:T(8,128)(2,1)} %copy-done.9, bf16[2,4,96,256]{3,2,1,0:T(8,128)(2,1)} %copy-done.10, ...), custom_call_target="tpu_custom_call", output_to_operand_aliasing={{0}: (8, {}), {1}: (9, {})} | custom-call | flops 786432 | bytes 6291456 | tf_op jit(solution)/shard_map/pallas_call | solution.py:82
  371.8 8.0 %shard_map.92 = (bf16[32,96,2048]{2,1,0:T(8,128)(2,1)}, bf16[32,96,2048]{2,1,0:T(8,128)(2,1)}) custom-call(bf16[2,8,96,256]{3,2,1,0:T(8,128)(2,1)} %get-tuple-element.89.refs_0_, bf16[2,8,96,256]{3,2,1,0:T(8,128)(2,1)} %copy-done, bf16[2,8,96,256]{3,2,1,0:T(8,128)(2,1)} %copy-done.1, ...), custom_call_target="tpu_custom_call", output_to_operand_aliasing={{0}: (8, {}), {1}: (9, {})} | custom-call | flops 1572864 | bytes 12582912 | tf_op jit(solution)/shard_map/pallas_call | solution.py:82
  379.9 8.0 %shard_map.93 = (bf16[32,96,2048]{2,1,0:T(8,128)(2,1)}, bf16[32,96,2048]{2,1,0:T(8,128)(2,1)}) custom-call(bf16[2,8,96,256]{3,2,1,0:T(8,128)(2,1)} %get-tuple-element.81.refs_0_, bf16[2,8,96,256]{3,2,1,0:T(8,128)(2,1)} %copy-done.4, bf16[2,8,96,256]{3,2,1,0:T(8,128)(2,1)} %collective-permute-done.18.refs_2_, ...), custom_call_target="tpu_custom_call", output_to_operand_aliasing={{0}: (8, {}), {1}: (9, {})} | custom-call | flops 1572864 | bytes 12582912 | tf_op jit(solution)/shard_map/pallas_call | solution.py:82
  387.9 8.0 %shard_map.94 = (bf16[32,96,2048]{2,1,0:T(8,128)(2,1)}, bf16[32,96,2048]{2,1,0:T(8,128)(2,1)}) custom-call(bf16[2,8,96,256]{3,2,1,0:T(8,128)(2,1)} %get-tuple-element.73.refs_0_, bf16[2,8,96,256]{3,2,1,0:T(8,128)(2,1)} %copy-done.7, bf16[2,8,96,256]{3,2,1,0:T(8,128)(2,1)} %collective-permute-done.11.refs_2_, ...), custom_call_target="tpu_custom_call", output_to_operand_aliasing={{0}: (8, {}), {1}: (9, {})} | custom-call | flops 1572864 | bytes 12582912 | tf_op jit(solution)/shard_map/pallas_call | solution.py:82
  396.7 2.5 shard_map.95
  (153 shorter events, 22.0 us)
Async XLA Ops:
  21.0 1.8 collective-permute-start
  23.8 8.1 %collective-permute-start.1 = (f32[2,32,768]{2,1,0:T(8,128)S(1)}, f32[2,32,768]{2,1,0:T(8,128)S(1)}, u32[]{:S(2)}, u32[]{:S(2)}) collective-permute-start(f32[2,32,768]{2,1,0:T(8,128)S(1)} %add.12), channel_id=1, source_target_pairs={{0,2},{1,3},{2,0},{3,1},{4,6},{5,7},{6,4},{7,5},{8,10},{9,11},{10,... | collective-permute-start | bytes 589832 | tf_op jit(solution)/shard_map/ppermute | solution.py:146
  31.9 6.4 %collective-permute-start.2 = (f32[2,32,768]{2,1,0:T(8,128)S(1)}, f32[2,32,768]{2,1,0:T(8,128)S(1)}, u32[]{:S(2)}, u32[]{:S(2)}) collective-permute-start(f32[2,32,768]{2,1,0:T(8,128)S(1)} %add.13), channel_id=1, source_target_pairs={{0,4},{1,5},{2,6},{3,7},{4,0},{5,1},{6,2},{7,3},{8,12},{9,13},{10,... | collective-permute-start | bytes 589832 | tf_op jit(solution)/shard_map/ppermute | solution.py:146
  42.2 32.5 %collective-permute-start.38 = (bf16[2,2,96,256]{3,2,1,0:T(8,128)(2,1)}, bf16[2,2,96,256]{3,2,1,0:T(8,128)(2,1)S(1)}, u32[]{:S(2)}, u32[]{:S(2)}) collective-permute-start(bf16[2,2,96,256]{3,2,1,0:T(8,128)(2,1)} %get-tuple-element.106), channel_id=1, source_target_pairs={{0,1},{1,0},{2,3},{3,2},{4,5},{5,4},{6,7},{7,6},{8,9},{9,8},{10,11... | collective-permute-start | bytes 589832 | tf_op jit(solution)/shard_map/ppermute | solution.py:146
  42.2 33.7 %collective-permute-start.39 = (bf16[2,2,96,256]{3,2,1,0:T(8,128)(2,1)}, bf16[2,2,96,256]{3,2,1,0:T(8,128)(2,1)S(1)}, u32[]{:S(2)}, u32[]{:S(2)}) collective-permute-start(bf16[2,2,96,256]{3,2,1,0:T(8,128)(2,1)} %get-tuple-element.107), channel_id=1, source_target_pairs={{0,2},{1,3},{2,0},{3,1},{4,6},{5,7},{6,4},{7,5},{8,10},{9,11},{10,... | collective-permute-start | bytes 589832 | tf_op jit(solution)/shard_map/ppermute | solution.py:146
  43.8 1.9 collective-permute-start.45
  44.0 6.3 %collective-permute-start.46 = (bf16[32,256]{1,0:T(8,128)(2,1)S(1)}, bf16[32,256]{1,0:T(8,128)(2,1)S(1)}, u32[]{:S(2)}, u32[]{:S(2)}) collective-permute-start(bf16[32,256]{1,0:T(8,128)(2,1)S(1)} %fusion.refs_0_), channel_id=1, source_target_pairs={{0,2},{1,3},{2,0},{3,1},{4,6},{5,7},{6,4},{7,5},{8,10},{9,11},{10,... | collective-permute-start | bytes 49160 | tf_op jit(solution)/shard_map/ppermute | solution.py:146
  44.6 6.2 %collective-permute-start.47 = (bf16[32,256]{1,0:T(8,128)(2,1)S(1)}, bf16[32,256]{1,0:T(8,128)(2,1)S(1)}, u32[]{:S(2)}, u32[]{:S(2)}) collective-permute-start(bf16[32,256]{1,0:T(8,128)(2,1)S(1)} %fusion.refs_0_), channel_id=1, source_target_pairs={{0,3},{1,2},{2,1},{3,0},{4,7},{5,6},{6,5},{7,4},{8,11},{9,10},{10,... | collective-permute-start | bytes 49160 | tf_op jit(solution)/shard_map/ppermute | solution.py:146
  45.7 7.1 %collective-permute-start.48 = (bf16[32,256]{1,0:T(8,128)(2,1)S(1)}, bf16[32,256]{1,0:T(8,128)(2,1)S(1)}, u32[]{:S(2)}, u32[]{:S(2)}) collective-permute-start(bf16[32,256]{1,0:T(8,128)(2,1)S(1)} %fusion.refs_0_), channel_id=1, source_target_pairs={{0,4},{1,5},{2,6},{3,7},{4,0},{5,1},{6,2},{7,3},{8,12},{9,13},{10,... | collective-permute-start | bytes 49160 | tf_op jit(solution)/shard_map/ppermute | solution.py:146
  50.3 3.9 collective-permute-start.49
  50.8 4.7 %collective-permute-start.50 = (bf16[32,256]{1,0:T(8,128)(2,1)S(1)}, bf16[32,256]{1,0:T(8,128)(2,1)S(1)}, u32[]{:S(2)}, u32[]{:S(2)}) collective-permute-start(bf16[32,256]{1,0:T(8,128)(2,1)S(1)} %fusion.refs_0_), channel_id=1, source_target_pairs={{0,6},{1,7},{2,4},{3,5},{4,2},{5,3},{6,0},{7,1},{8,14},{9,15},{10,... | collective-permute-start | bytes 49160 | tf_op jit(solution)/shard_map/ppermute | solution.py:146
  52.8 4.1 %collective-permute-start.51 = (bf16[32,256]{1,0:T(8,128)(2,1)S(1)}, bf16[32,256]{1,0:T(8,128)(2,1)S(1)}, u32[]{:S(2)}, u32[]{:S(2)}) collective-permute-start(bf16[32,256]{1,0:T(8,128)(2,1)S(1)} %fusion.refs_0_), channel_id=1, source_target_pairs={{0,7},{1,6},{2,5},{3,4},{4,3},{5,2},{6,1},{7,0},{8,15},{9,14},{10,... | collective-permute-start | bytes 49160 | tf_op jit(solution)/shard_map/ppermute | solution.py:146
  59.0 7.9 %collective-permute-start.52 = (bf16[32,2048]{1,0:T(8,128)(2,1)}, bf16[32,2048]{1,0:T(8,128)(2,1)S(1)}, u32[]{:S(2)}, u32[]{:S(2)}) collective-permute-start(bf16[32,2048]{1,0:T(8,128)(2,1)} %shard_map.96.refs_0_), channel_id=1, source_target_pairs={{0,8},{8,0},{16,24},{24,16},{1,9},{9,1},{17,25},{25,17},{2,10},{10... | collective-permute-start | bytes 393224 | tf_op jit(solution)/shard_map/ppermute | solution.py:146
  60.6 13.1 %collective-permute-start.53 = (bf16[32,2048]{1,0:T(8,128)(2,1)}, bf16[32,2048]{1,0:T(8,128)(2,1)S(1)}, u32[]{:S(2)}, u32[]{:S(2)}) collective-permute-start(bf16[32,2048]{1,0:T(8,128)(2,1)} %shard_map.96.refs_0_), channel_id=1, source_target_pairs={{0,16},{8,24},{16,0},{24,8},{1,17},{9,25},{17,1},{25,9},{2,18},{10... | collective-permute-start | bytes 393224 | tf_op jit(solution)/shard_map/ppermute | solution.py:146
  63.2 11.5 %collective-permute-start.54 = (bf16[32,2048]{1,0:T(8,128)(2,1)}, bf16[32,2048]{1,0:T(8,128)(2,1)S(1)}, u32[]{:S(2)}, u32[]{:S(2)}) collective-permute-start(bf16[32,2048]{1,0:T(8,128)(2,1)} %shard_map.96.refs_0_), channel_id=1, source_target_pairs={{0,24},{8,16},{16,8},{24,0},{1,25},{9,17},{17,9},{25,1},{2,26},{10... | collective-permute-start | bytes 393224 | tf_op jit(solution)/shard_map/ppermute | solution.py:146
  66.9 19.9 %collective-permute-start.40 = (bf16[2,2,96,256]{3,2,1,0:T(8,128)(2,1)}, bf16[2,2,96,256]{3,2,1,0:T(8,128)(2,1)S(1)}, u32[]{:S(2)}, u32[]{:S(2)}) collective-permute-start(bf16[2,2,96,256]{3,2,1,0:T(8,128)(2,1)} %get-tuple-element.108), channel_id=1, source_target_pairs={{0,3},{1,2},{2,1},{3,0},{4,7},{5,6},{6,5},{7,4},{8,11},{9,10},{10,... | collective-permute-start | bytes 589832 | tf_op jit(solution)/shard_map/ppermute | solution.py:146
  73.7 16.0 %collective-permute-start.41 = (bf16[2,2,96,256]{3,2,1,0:T(8,128)(2,1)}, bf16[2,2,96,256]{3,2,1,0:T(8,128)(2,1)S(1)}, u32[]{:S(2)}, u32[]{:S(2)}) collective-permute-start(bf16[2,2,96,256]{3,2,1,0:T(8,128)(2,1)} %get-tuple-element.109), channel_id=1, source_target_pairs={{0,4},{1,5},{2,6},{3,7},{4,0},{5,1},{6,2},{7,3},{8,12},{9,13},{10,... | collective-permute-start | bytes 589832 | tf_op jit(solution)/shard_map/ppermute | solution.py:146
  74.7 16.1 %collective-permute-start.42 = (bf16[2,2,96,256]{3,2,1,0:T(8,128)(2,1)}, bf16[2,2,96,256]{3,2,1,0:T(8,128)(2,1)S(1)}, u32[]{:S(2)}, u32[]{:S(2)}) collective-permute-start(bf16[2,2,96,256]{3,2,1,0:T(8,128)(2,1)} %get-tuple-element.110), channel_id=1, source_target_pairs={{0,5},{1,4},{2,7},{3,6},{4,1},{5,0},{6,3},{7,2},{8,13},{9,12},{10,... | collective-permute-start | bytes 589832 | tf_op jit(solution)/shard_map/ppermute | solution.py:146
  74.7 17.4 %collective-permute-start.43 = (bf16[2,2,96,256]{3,2,1,0:T(8,128)(2,1)}, bf16[2,2,96,256]{3,2,1,0:T(8,128)(2,1)S(1)}, u32[]{:S(2)}, u32[]{:S(2)}) collective-permute-start(bf16[2,2,96,256]{3,2,1,0:T(8,128)(2,1)} %get-tuple-element.111), channel_id=1, source_target_pairs={{0,6},{1,7},{2,4},{3,5},{4,2},{5,3},{6,0},{7,1},{8,14},{9,15},{10,... | collective-permute-start | bytes 589832 | tf_op jit(solution)/shard_map/ppermute | solution.py:146
  75.9 27.7 %collective-permute-start.44 = (bf16[2,2,96,256]{3,2,1,0:T(8,128)(2,1)}, bf16[2,2,96,256]{3,2,1,0:T(8,128)(2,1)S(1)}, u32[]{:S(2)}, u32[]{:S(2)}) collective-permute-start(bf16[2,2,96,256]{3,2,1,0:T(8,128)(2,1)} %get-tuple-element.112), channel_id=1, source_target_pairs={{0,7},{1,6},{2,5},{3,4},{4,3},{5,2},{6,1},{7,0},{8,15},{9,14},{10,... | collective-permute-start | bytes 589832 | tf_op jit(solution)/shard_map/ppermute | solution.py:146
  86.8 26.3 %collective-permute-start.31 = (bf16[2,4,96,256]{3,2,1,0:T(8,128)(2,1)}, bf16[2,4,96,256]{3,2,1,0:T(8,128)(2,1)S(1)}, u32[]{:S(2)}, u32[]{:S(2)}) collective-permute-start(bf16[2,4,96,256]{3,2,1,0:T(8,128)(2,1)} %get-tuple-element.98), channel_id=1, source_target_pairs={{0,1},{1,0},{2,3},{3,2},{4,5},{5,4},{6,7},{7,6},{8,9},{9,8},{10,11... | collective-permute-start | bytes 1179656 | tf_op jit(solution)/shard_map/ppermute | solution.py:146
  89.7 23.5 %collective-permute-start.32 = (bf16[2,4,96,256]{3,2,1,0:T(8,128)(2,1)}, bf16[2,4,96,256]{3,2,1,0:T(8,128)(2,1)S(1)}, u32[]{:S(2)}, u32[]{:S(2)}) collective-permute-start(bf16[2,4,96,256]{3,2,1,0:T(8,128)(2,1)} %get-tuple-element.99), channel_id=1, source_target_pairs={{0,2},{1,3},{2,0},{3,1},{4,6},{5,7},{6,4},{7,5},{8,10},{9,11},{10,... | collective-permute-start | bytes 1179656 | tf_op jit(solution)/shard_map/ppermute | solution.py:146
  90.8 12.9 %collective-permute-start.3 = (bf16[2,2,96,256]{3,2,1,0:T(8,128)(2,1)}, bf16[2,2,96,256]{3,2,1,0:T(8,128)(2,1)S(1)}, u32[]{:S(2)}, u32[]{:S(2)}) collective-permute-start(bf16[2,2,96,256]{3,2,1,0:T(8,128)(2,1)} %get-tuple-element.66), channel_id=1, source_target_pairs={{0,1},{1,0},{2,3},{3,2},{4,5},{5,4},{6,7},{7,6},{8,9},{9,8},{10,11... | collective-permute-start | bytes 589832 | tf_op jit(solution)/shard_map/ppermute | solution.py:146
  92.8 22.3 %collective-permute-start.33 = (bf16[2,4,96,256]{3,2,1,0:T(8,128)(2,1)}, bf16[2,4,96,256]{3,2,1,0:T(8,128)(2,1)S(1)}, u32[]{:S(2)}, u32[]{:S(2)}) collective-permute-start(bf16[2,4,96,256]{3,2,1,0:T(8,128)(2,1)} %get-tuple-element.100), channel_id=1, source_target_pairs={{0,3},{1,2},{2,1},{3,0},{4,7},{5,6},{6,5},{7,4},{8,11},{9,10},{10,... | collective-permute-start | bytes 1179656 | tf_op jit(solution)/shard_map/ppermute | solution.py:146
  103.6 47.4 %collective-permute-start.24 = (bf16[2,8,96,256]{3,2,1,0:T(8,128)(2,1)}, bf16[2,8,96,256]{3,2,1,0:T(8,128)(2,1)S(1)}, u32[]{:S(2)}, u32[]{:S(2)}) collective-permute-start(bf16[2,8,96,256]{3,2,1,0:T(8,128)(2,1)} %get-tuple-element.90), channel_id=1, source_target_pairs={{0,1},{1,0},{2,3},{3,2},{4,5},{5,4},{6,7},{7,6},{8,9},{9,8},{10,11... | collective-permute-start | bytes 2359304 | tf_op jit(solution)/shard_map/ppermute | solution.py:146
  104.3 7.0 %collective-permute-start.4 = (bf16[2,2,96,256]{3,2,1,0:T(8,128)(2,1)}, bf16[2,2,96,256]{3,2,1,0:T(8,128)(2,1)S(1)}, u32[]{:S(2)}, u32[]{:S(2)}) collective-permute-start(bf16[2,2,96,256]{3,2,1,0:T(8,128)(2,1)} %get-tuple-element.67), channel_id=1, source_target_pairs={{0,2},{1,3},{2,0},{3,1},{4,6},{5,7},{6,4},{7,5},{8,10},{9,11},{10,... | collective-permute-start | bytes 589832 | tf_op jit(solution)/shard_map/ppermute | solution.py:146
  112.0 28.8 %collective-permute-start.34 = (bf16[2,4,96,256]{3,2,1,0:T(8,128)(2,1)S(1)}, bf16[2,4,96,256]{3,2,1,0:T(8,128)(2,1)S(1)}, u32[]{:S(2)}, u32[]{:S(2)}) collective-permute-start(bf16[2,4,96,256]{3,2,1,0:T(8,128)(2,1)S(1)} %copy-done.42), channel_id=1, source_target_pairs={{0,4},{1,5},{2,6},{3,7},{4,0},{5,1},{6,2},{7,3},{8,12},{9,13},{10,... | collective-permute-start | bytes 1179656 | tf_op jit(solution)/shard_map/ppermute | solution.py:146
  113.1 49.8 %copy-start.9 = (bf16[2,4,96,256]{3,2,1,0:T(8,128)(2,1)}, bf16[2,4,96,256]{3,2,1,0:T(8,128)(2,1)S(1)}, u32[]{:S(2)}) copy-start(bf16[2,4,96,256]{3,2,1,0:T(8,128)(2,1)S(1)} %collective-permute-done.31.refs_1_) | copy-start | bytes 1179652
  113.1 32.9 %collective-permute-start.35 = (bf16[2,4,96,256]{3,2,1,0:T(8,128)(2,1)S(1)}, bf16[2,4,96,256]{3,2,1,0:T(8,128)(2,1)S(1)}, u32[]{:S(2)}, u32[]{:S(2)}) collective-permute-start(bf16[2,4,96,256]{3,2,1,0:T(8,128)(2,1)S(1)} %copy-done.41), channel_id=1, source_target_pairs={{0,5},{1,4},{2,7},{3,6},{4,1},{5,0},{6,3},{7,2},{8,13},{9,12},{10,... | collective-permute-start | bytes 1179656 | tf_op jit(solution)/shard_map/ppermute | solution.py:146
  113.2 27.6 %copy-start.10 = (bf16[2,4,96,256]{3,2,1,0:T(8,128)(2,1)}, bf16[2,4,96,256]{3,2,1,0:T(8,128)(2,1)S(1)}, u32[]{:S(2)}) copy-start(bf16[2,4,96,256]{3,2,1,0:T(8,128)(2,1)S(1)} %collective-permute-done.32.refs_2_) | copy-start | bytes 1179652
  113.2 36.1 %collective-permute-start.36 = (bf16[2,4,96,256]{3,2,1,0:T(8,128)(2,1)S(1)}, bf16[2,4,96,256]{3,2,1,0:T(8,128)(2,1)S(1)}, u32[]{:S(2)}, u32[]{:S(2)}) collective-permute-start(bf16[2,4,96,256]{3,2,1,0:T(8,128)(2,1)S(1)} %copy-done.40), channel_id=1, source_target_pairs={{0,6},{1,7},{2,4},{3,5},{4,2},{5,3},{6,0},{7,1},{8,14},{9,15},{10,... | collective-permute-start | bytes 1179656 | tf_op jit(solution)/shard_map/ppermute | solution.py:146
  115.1 36.0 %collective-permute-start.37 = (bf16[2,4,96,256]{3,2,1,0:T(8,128)(2,1)}, bf16[2,4,96,256]{3,2,1,0:T(8,128)(2,1)S(1)}, u32[]{:S(2)}, u32[]{:S(2)}) collective-permute-start(bf16[2,4,96,256]{3,2,1,0:T(8,128)(2,1)} %get-tuple-element.104), channel_id=1, source_target_pairs={{0,7},{1,6},{2,5},{3,4},{4,3},{5,2},{6,1},{7,0},{8,15},{9,14},{10,... | collective-permute-start | bytes 1179656 | tf_op jit(solution)/shard_map/ppermute | solution.py:146
  140.9 22.1 %collective-permute-start.25 = (bf16[2,8,96,256]{3,2,1,0:T(8,128)(2,1)}, bf16[2,8,96,256]{3,2,1,0:T(8,128)(2,1)S(1)}, u32[]{:S(2)}, u32[]{:S(2)}) collective-permute-start(bf16[2,8,96,256]{3,2,1,0:T(8,128)(2,1)} %get-tuple-element.91), channel_id=1, source_target_pairs={{0,2},{1,3},{2,0},{3,1},{4,6},{5,7},{6,4},{7,5},{8,10},{9,11},{10,... | collective-permute-start | bytes 2359304 | tf_op jit(solution)/shard_map/ppermute | solution.py:146
  146.8 30.6 %collective-permute-start.26 = (bf16[2,8,96,256]{3,2,1,0:T(8,128)(2,1)}, bf16[2,8,96,256]{3,2,1,0:T(8,128)(2,1)S(1)}, u32[]{:S(2)}, u32[]{:S(2)}) collective-permute-start(bf16[2,8,96,256]{3,2,1,0:T(8,128)(2,1)} %get-tuple-element.92), channel_id=1, source_target_pairs={{0,3},{1,2},{2,1},{3,0},{4,7},{5,6},{6,5},{7,4},{8,11},{9,10},{10,... | collective-permute-start | bytes 2359304 | tf_op jit(solution)/shard_map/ppermute | solution.py:146
  150.1 28.6 %collective-permute-start.27 = (bf16[2,8,96,256]{3,2,1,0:T(8,128)(2,1)}, bf16[2,8,96,256]{3,2,1,0:T(8,128)(2,1)S(1)}, u32[]{:S(2)}, u32[]{:S(2)}) collective-permute-start(bf16[2,8,96,256]{3,2,1,0:T(8,128)(2,1)} %get-tuple-element.93), channel_id=1, source_target_pairs={{0,4},{1,5},{2,6},{3,7},{4,0},{5,1},{6,2},{7,3},{8,12},{9,13},{10,... | collective-permute-start | bytes 2359304 | tf_op jit(solution)/shard_map/ppermute | solution.py:146
  151.0 67.0 %collective-permute-start.28 = (bf16[2,8,96,256]{3,2,1,0:T(8,128)(2,1)}, bf16[2,8,96,256]{3,2,1,0:T(8,128)(2,1)}, u32[]{:S(2)}, u32[]{:S(2)}) collective-permute-start(bf16[2,8,96,256]{3,2,1,0:T(8,128)(2,1)} %get-tuple-element.94), channel_id=1, source_target_pairs={{0,5},{1,4},{2,7},{3,6},{4,1},{5,0},{6,3},{7,2},{8,13},{9,12},{10,... | collective-permute-start | bytes 2359304 | tf_op jit(solution)/shard_map/ppermute | solution.py:146
  151.8 68.7 %collective-permute-start.29 = (bf16[2,8,96,256]{3,2,1,0:T(8,128)(2,1)}, bf16[2,8,96,256]{3,2,1,0:T(8,128)(2,1)}, u32[]{:S(2)}, u32[]{:S(2)}) collective-permute-start(bf16[2,8,96,256]{3,2,1,0:T(8,128)(2,1)} %get-tuple-element.95), channel_id=1, source_target_pairs={{0,6},{1,7},{2,4},{3,5},{4,2},{5,3},{6,0},{7,1},{8,14},{9,15},{10,... | collective-permute-start | bytes 2359304 | tf_op jit(solution)/shard_map/ppermute | solution.py:146
  163.0 68.5 %copy-start.1 = (bf16[2,8,96,256]{3,2,1,0:T(8,128)(2,1)}, bf16[2,8,96,256]{3,2,1,0:T(8,128)(2,1)S(1)}, u32[]{:S(2)}) copy-start(bf16[2,8,96,256]{3,2,1,0:T(8,128)(2,1)S(1)} %collective-permute-done.25.refs_2_) | copy-start | bytes 2359300
  163.0 68.5 %collective-permute-start.30 = (bf16[2,8,96,256]{3,2,1,0:T(8,128)(2,1)}, bf16[2,8,96,256]{3,2,1,0:T(8,128)(2,1)}, u32[]{:S(2)}, u32[]{:S(2)}) collective-permute-start(bf16[2,8,96,256]{3,2,1,0:T(8,128)(2,1)} %get-tuple-element.96), channel_id=1, source_target_pairs={{0,7},{1,6},{2,5},{3,4},{4,3},{5,2},{6,1},{7,0},{8,15},{9,14},{10,... | collective-permute-start | bytes 2359304 | tf_op jit(solution)/shard_map/ppermute | solution.py:146
  177.4 54.0 %copy-start.2 = (bf16[2,8,96,256]{3,2,1,0:T(8,128)(2,1)}, bf16[2,8,96,256]{3,2,1,0:T(8,128)(2,1)S(1)}, u32[]{:S(2)}) copy-start(bf16[2,8,96,256]{3,2,1,0:T(8,128)(2,1)S(1)} %collective-permute-done.26.refs_3_) | copy-start | bytes 2359300
  177.4 54.1 %collective-permute-start.17 = (bf16[2,8,96,256]{3,2,1,0:T(8,128)(2,1)}, bf16[2,8,96,256]{3,2,1,0:T(8,128)(2,1)S(1)}, u32[]{:S(2)}, u32[]{:S(2)}) collective-permute-start(bf16[2,8,96,256]{3,2,1,0:T(8,128)(2,1)} %get-tuple-element.82), channel_id=1, source_target_pairs={{0,1},{1,0},{2,3},{3,2},{4,5},{5,4},{6,7},{7,6},{8,9},{9,8},{10,11... | collective-permute-start | bytes 2359304 | tf_op jit(solution)/shard_map/ppermute | solution.py:146
  178.6 52.9 %copy-start.3 = (bf16[2,8,96,256]{3,2,1,0:T(8,128)(2,1)}, bf16[2,8,96,256]{3,2,1,0:T(8,128)(2,1)S(1)}, u32[]{:S(2)}) copy-start(bf16[2,8,96,256]{3,2,1,0:T(8,128)(2,1)S(1)} %collective-permute-done.27.refs_4_) | copy-start | bytes 2359300
  178.6 54.1 %collective-permute-start.18 = (bf16[2,8,96,256]{3,2,1,0:T(8,128)(2,1)}, bf16[2,8,96,256]{3,2,1,0:T(8,128)(2,1)}, u32[]{:S(2)}, u32[]{:S(2)}) collective-permute-start(bf16[2,8,96,256]{3,2,1,0:T(8,128)(2,1)} %get-tuple-element.83), channel_id=1, source_target_pairs={{0,2},{1,3},{2,0},{3,1},{4,6},{5,7},{6,4},{7,5},{8,10},{9,11},{10,... | collective-permute-start | bytes 2359304 | tf_op jit(solution)/shard_map/ppermute | solution.py:146
  218.0 25.3 %collective-permute-start.19 = (bf16[2,8,96,256]{3,2,1,0:T(8,128)(2,1)}, bf16[2,8,96,256]{3,2,1,0:T(8,128)(2,1)}, u32[]{:S(2)}, u32[]{:S(2)}) collective-permute-start(bf16[2,8,96,256]{3,2,1,0:T(8,128)(2,1)} %get-tuple-element.84), channel_id=1, source_target_pairs={{0,3},{1,2},{2,1},{3,0},{4,7},{5,6},{6,5},{7,4},{8,11},{9,10},{10,... | collective-permute-start | bytes 2359304 | tf_op jit(solution)/shard_map/ppermute | solution.py:146
  220.5 23.3 %collective-permute-start.20 = (bf16[2,8,96,256]{3,2,1,0:T(8,128)(2,1)}, bf16[2,8,96,256]{3,2,1,0:T(8,128)(2,1)}, u32[]{:S(2)}, u32[]{:S(2)}) collective-permute-start(bf16[2,8,96,256]{3,2,1,0:T(8,128)(2,1)} %get-tuple-element.85), channel_id=1, source_target_pairs={{0,4},{1,5},{2,6},{3,7},{4,0},{5,1},{6,2},{7,3},{8,12},{9,13},{10,... | collective-permute-start | bytes 2359304 | tf_op jit(solution)/shard_map/ppermute | solution.py:146
  231.5 57.0 %collective-permute-start.21 = (bf16[2,8,96,256]{3,2,1,0:T(8,128)(2,1)}, bf16[2,8,96,256]{3,2,1,0:T(8,128)(2,1)S(1)}, u32[]{:S(2)}, u32[]{:S(2)}) collective-permute-start(bf16[2,8,96,256]{3,2,1,0:T(8,128)(2,1)} %get-tuple-element.86), channel_id=1, source_target_pairs={{0,5},{1,4},{2,7},{3,6},{4,1},{5,0},{6,3},{7,2},{8,13},{9,12},{10,... | collective-permute-start | bytes 2359304 | tf_op jit(solution)/shard_map/ppermute | solution.py:146
  231.6 140.2 %copy-start.4 = (bf16[2,8,96,256]{3,2,1,0:T(8,128)(2,1)}, bf16[2,8,96,256]{3,2,1,0:T(8,128)(2,1)S(1)}, u32[]{:S(2)}) copy-start(bf16[2,8,96,256]{3,2,1,0:T(8,128)(2,1)S(1)} %collective-permute-done.17.refs_1_) | copy-start | bytes 2359300
  231.6 59.4 %collective-permute-start.22 = (bf16[2,8,96,256]{3,2,1,0:T(8,128)(2,1)}, bf16[2,8,96,256]{3,2,1,0:T(8,128)(2,1)S(1)}, u32[]{:S(2)}, u32[]{:S(2)}) collective-permute-start(bf16[2,8,96,256]{3,2,1,0:T(8,128)(2,1)} %get-tuple-element.87), channel_id=1, source_target_pairs={{0,6},{1,7},{2,4},{3,5},{4,2},{5,3},{6,0},{7,1},{8,14},{9,15},{10,... | collective-permute-start | bytes 2359304 | tf_op jit(solution)/shard_map/ppermute | solution.py:146
  232.8 59.2 %collective-permute-start.23 = (bf16[2,8,96,256]{3,2,1,0:T(8,128)(2,1)}, bf16[2,8,96,256]{3,2,1,0:T(8,128)(2,1)S(1)}, u32[]{:S(2)}, u32[]{:S(2)}) collective-permute-start(bf16[2,8,96,256]{3,2,1,0:T(8,128)(2,1)} %get-tuple-element.88), channel_id=1, source_target_pairs={{0,7},{1,6},{2,5},{3,4},{4,3},{5,2},{6,1},{7,0},{8,15},{9,14},{10,... | collective-permute-start | bytes 2359304 | tf_op jit(solution)/shard_map/ppermute | solution.py:146
  243.3 48.6 %collective-permute-start.10 = (bf16[2,8,96,256]{3,2,1,0:T(8,128)(2,1)}, bf16[2,8,96,256]{3,2,1,0:T(8,128)(2,1)S(1)}, u32[]{:S(2)}, u32[]{:S(2)}) collective-permute-start(bf16[2,8,96,256]{3,2,1,0:T(8,128)(2,1)} %get-tuple-element.74), channel_id=1, source_target_pairs={{0,1},{1,0},{2,3},{3,2},{4,5},{5,4},{6,7},{7,6},{8,9},{9,8},{10,11... | collective-permute-start | bytes 2359304 | tf_op jit(solution)/shard_map/ppermute | solution.py:146
  243.8 50.3 %collective-permute-start.11 = (bf16[2,8,96,256]{3,2,1,0:T(8,128)(2,1)}, bf16[2,8,96,256]{3,2,1,0:T(8,128)(2,1)}, u32[]{:S(2)}, u32[]{:S(2)}) collective-permute-start(bf16[2,8,96,256]{3,2,1,0:T(8,128)(2,1)} %get-tuple-element.75), channel_id=1, source_target_pairs={{0,2},{1,3},{2,0},{3,1},{4,6},{5,7},{6,4},{7,5},{8,10},{9,11},{10,... | collective-permute-start | bytes 2359304 | tf_op jit(solution)/shard_map/ppermute | solution.py:146
  288.5 83.3 %copy-start.5 = (bf16[2,8,96,256]{3,2,1,0:T(8,128)(2,1)}, bf16[2,8,96,256]{3,2,1,0:T(8,128)(2,1)S(1)}, u32[]{:S(2)}) copy-start(bf16[2,8,96,256]{3,2,1,0:T(8,128)(2,1)S(1)} %collective-permute-done.21.refs_5_) | copy-start | bytes 2359300
  288.5 20.7 %collective-permute-start.12 = (bf16[2,8,96,256]{3,2,1,0:T(8,128)(2,1)}, bf16[2,8,96,256]{3,2,1,0:T(8,128)(2,1)}, u32[]{:S(2)}, u32[]{:S(2)}) collective-permute-start(bf16[2,8,96,256]{3,2,1,0:T(8,128)(2,1)} %get-tuple-element.76), channel_id=1, source_target_pairs={{0,3},{1,2},{2,1},{3,0},{4,7},{5,6},{6,5},{7,4},{8,11},{9,10},{10,... | collective-permute-start | bytes 2359304 | tf_op jit(solution)/shard_map/ppermute | solution.py:146
  291.0 80.9 %copy-start.6 = (bf16[2,8,96,256]{3,2,1,0:T(8,128)(2,1)}, bf16[2,8,96,256]{3,2,1,0:T(8,128)(2,1)S(1)}, u32[]{:S(2)}) copy-start(bf16[2,8,96,256]{3,2,1,0:T(8,128)(2,1)S(1)} %collective-permute-done.22.refs_6_) | copy-start | bytes 2359300
  291.0 54.4 %collective-permute-start.13 = (bf16[2,8,96,256]{3,2,1,0:T(8,128)(2,1)}, bf16[2,8,96,256]{3,2,1,0:T(8,128)(2,1)}, u32[]{:S(2)}, u32[]{:S(2)}) collective-permute-start(bf16[2,8,96,256]{3,2,1,0:T(8,128)(2,1)} %get-tuple-element.77), channel_id=1, source_target_pairs={{0,4},{1,5},{2,6},{3,7},{4,0},{5,1},{6,2},{7,3},{8,12},{9,13},{10,... | collective-permute-start | bytes 2359304 | tf_op jit(solution)/shard_map/ppermute | solution.py:146
  291.9 68.8 %collective-permute-start.14 = (bf16[2,8,96,256]{3,2,1,0:T(8,128)(2,1)}, bf16[2,8,96,256]{3,2,1,0:T(8,128)(2,1)}, u32[]{:S(2)}, u32[]{:S(2)}) collective-permute-start(bf16[2,8,96,256]{3,2,1,0:T(8,128)(2,1)} %get-tuple-element.78), channel_id=1, source_target_pairs={{0,5},{1,4},{2,7},{3,6},{4,1},{5,0},{6,3},{7,2},{8,13},{9,12},{10,... | collective-permute-start | bytes 2359304 | tf_op jit(solution)/shard_map/ppermute | solution.py:146
  292.8 79.0 %copy-start.7 = (bf16[2,8,96,256]{3,2,1,0:T(8,128)(2,1)}, bf16[2,8,96,256]{3,2,1,0:T(8,128)(2,1)S(1)}, u32[]{:S(2)}) copy-start(bf16[2,8,96,256]{3,2,1,0:T(8,128)(2,1)S(1)} %collective-permute-done.10.refs_1_) | copy-start | bytes 2359300
  292.8 69.8 %collective-permute-start.15 = (bf16[2,8,96,256]{3,2,1,0:T(8,128)(2,1)}, bf16[2,8,96,256]{3,2,1,0:T(8,128)(2,1)}, u32[]{:S(2)}, u32[]{:S(2)}) collective-permute-start(bf16[2,8,96,256]{3,2,1,0:T(8,128)(2,1)} %get-tuple-element.79), channel_id=1, source_target_pairs={{0,6},{1,7},{2,4},{3,5},{4,2},{5,3},{6,0},{7,1},{8,14},{9,15},{10,... | collective-permute-start | bytes 2359304 | tf_op jit(solution)/shard_map/ppermute | solution.py:146
  294.2 69.8 %collective-permute-start.16 = (bf16[2,8,96,256]{3,2,1,0:T(8,128)(2,1)}, bf16[2,8,96,256]{3,2,1,0:T(8,128)(2,1)}, u32[]{:S(2)}, u32[]{:S(2)}) collective-permute-start(bf16[2,8,96,256]{3,2,1,0:T(8,128)(2,1)} %get-tuple-element.80), channel_id=1, source_target_pairs={{0,7},{1,6},{2,5},{3,4},{4,3},{5,2},{6,1},{7,0},{8,15},{9,14},{10,... | collective-permute-start | bytes 2359304 | tf_op jit(solution)/shard_map/ppermute | solution.py:146
  309.2 86.7 %collective-permute-start.5 = (bf16[2,2,96,256]{3,2,1,0:T(8,128)(2,1)}, bf16[2,2,96,256]{3,2,1,0:T(8,128)(2,1)S(1)}, u32[]{:S(2)}, u32[]{:S(2)}) collective-permute-start(bf16[2,2,96,256]{3,2,1,0:T(8,128)(2,1)} %get-tuple-element.68), channel_id=1, source_target_pairs={{0,3},{1,2},{2,1},{3,0},{4,7},{5,6},{6,5},{7,4},{8,11},{9,10},{10,... | collective-permute-start | bytes 589832 | tf_op jit(solution)/shard_map/ppermute | solution.py:146
  345.4 50.5 %collective-permute-start.6 = (bf16[2,2,96,256]{3,2,1,0:T(8,128)(2,1)}, bf16[2,2,96,256]{3,2,1,0:T(8,128)(2,1)S(1)}, u32[]{:S(2)}, u32[]{:S(2)}) collective-permute-start(bf16[2,2,96,256]{3,2,1,0:T(8,128)(2,1)} %get-tuple-element.69), channel_id=1, source_target_pairs={{0,4},{1,5},{2,6},{3,7},{4,0},{5,1},{6,2},{7,3},{8,12},{9,13},{10,... | collective-permute-start | bytes 589832 | tf_op jit(solution)/shard_map/ppermute | solution.py:146
  360.7 35.2 %collective-permute-start.7 = (bf16[2,2,96,256]{3,2,1,0:T(8,128)(2,1)}, bf16[2,2,96,256]{3,2,1,0:T(8,128)(2,1)}, u32[]{:S(2)}, u32[]{:S(2)}) collective-permute-start(bf16[2,2,96,256]{3,2,1,0:T(8,128)(2,1)} %get-tuple-element.70), channel_id=1, source_target_pairs={{0,5},{1,4},{2,7},{3,6},{4,1},{5,0},{6,3},{7,2},{8,13},{9,12},{10,... | collective-permute-start | bytes 589832 | tf_op jit(solution)/shard_map/ppermute | solution.py:146
  362.6 33.3 %collective-permute-start.8 = (bf16[2,2,96,256]{3,2,1,0:T(8,128)(2,1)}, bf16[2,2,96,256]{3,2,1,0:T(8,128)(2,1)}, u32[]{:S(2)}, u32[]{:S(2)}) collective-permute-start(bf16[2,2,96,256]{3,2,1,0:T(8,128)(2,1)} %get-tuple-element.71), channel_id=1, source_target_pairs={{0,6},{1,7},{2,4},{3,5},{4,2},{5,3},{6,0},{7,1},{8,14},{9,15},{10,... | collective-permute-start | bytes 589832 | tf_op jit(solution)/shard_map/ppermute | solution.py:146
  364.0 32.0 %collective-permute-start.9 = (bf16[2,2,96,256]{3,2,1,0:T(8,128)(2,1)}, bf16[2,2,96,256]{3,2,1,0:T(8,128)(2,1)}, u32[]{:S(2)}, u32[]{:S(2)}) collective-permute-start(bf16[2,2,96,256]{3,2,1,0:T(8,128)(2,1)} %get-tuple-element.72), channel_id=1, source_target_pairs={{0,7},{1,6},{2,5},{3,4},{4,3},{5,2},{6,1},{7,0},{8,15},{9,14},{10,... | collective-permute-start | bytes 589832 | tf_op jit(solution)/shard_map/ppermute | solution.py:146
  (34 other events, 227.5 us)

commit v2 on v1

--- a/solution.py
+++ b/solution.py
@@ -10,13 +10,17 @@
     return [(i, i ^ k) for i in range(size)]
 
 
+def granted(mib):
+    return pltpu.CompilerParams(vmem_limit_bytes=mib << 20)
+
+
 def cost(flops, moved):
     return pl.CostEstimate(flops=flops, bytes_accessed=moved, transcendentals=0)
 
 
 def square_sums(w_gate, w_up, first, count):
     _, rows, cols = w_gate.shape
-    per_step = 2 if count % 2 == 0 and first % 2 == 0 else 1
+    per_step = 2
 
     def kernel(gate_ref, up_ref, out_ref):
         step = pl.program_id(0)
@@ -32,21 +36,23 @@
         in_specs=[weights, weights],
         out_specs=pl.BlockSpec((2, count, cols), lambda i: (0, 0, 0)),
         out_shape=jax.ShapeDtypeStruct((2, count, cols), jnp.float32),
+        compiler_params=granted(44),
         cost_estimate=cost(4 * count * rows * cols, 8 * count * rows * cols),
     )(w_gate, w_up)
 
 
-def scaled_pieces(w_gate, w_up, total, first, count, start, size):
+def scaled_pieces(w_gate, w_up, totals, first, count, start, size):
     _, rows, cols = w_gate.shape
     width = cols // size
 
-    def kernel(gate_ref, up_ref, total_ref, *refs):
-        outs, held = refs[:size], refs[size]
+    def kernel(gate_ref, up_ref, *refs):
+        total_refs, outs, held = refs[: len(totals)], refs[len(totals) : -1], refs[-1]
         me = lax.axis_index("zero")
         step = pl.program_id(0)
-        for side, ref in enumerate((gate_ref, up_ref)):
-            inverse = 1.0 / jnp.sqrt(total_ref[side, pl.ds(start + step, 1), :])
-            held[side] = (ref[0] * inverse).astype(jnp.bfloat16).T
+        for side, w_ref in enumerate((gate_ref, up_ref)):
+            total = sum(ref[side, pl.ds(start + step, 1), :] for ref in total_refs)
+            inverse = 1.0 / jnp.sqrt(total)
+            held[side] = (w_ref[0] * inverse).astype(jnp.bfloat16).T
             for k in range(size):
                 offset = pl.multiple_of(lax.bitwise_xor(me, k) * width, width)
                 outs[k][side, 0] = held[side, pl.ds(offset, width), :]
@@ -56,12 +62,13 @@
     return pl.pallas_call(
         kernel,
         grid=(count,),
-        in_specs=[weights, weights, pl.BlockSpec(total.shape, lambda i: (0, 0, 0))],
+        in_specs=[weights, weights] + [pl.BlockSpec(memory_space=pltpu.VMEM)] * len(totals),
         out_specs=[piece] * size,
         out_shape=[jax.ShapeDtypeStruct((2, count, width, rows), jnp.bfloat16)] * size,
         scratch_shapes=[pltpu.VMEM((2, cols, rows), jnp.bfloat16)],
+        compiler_params=granted(44),
         cost_estimate=cost(4 * count * rows * cols, 12 * count * rows * cols),
-    )(w_gate, w_up, total)
+    )(w_gate, w_up, *totals)
 
 
 def assembled(pieces, outputs, first, experts):
@@ -86,6 +93,7 @@
         out_specs=[whole, whole],
         out_shape=[jax.ShapeDtypeStruct((experts, width, size * rows), jnp.bfloat16)] * 2,
         input_output_aliases={size + n: n for n in range(len(kept))},
+        compiler_params=granted(44),
         cost_estimate=cost(count * width * rows * size, 8 * count * width * rows * size),
     )(*pieces, *kept)
 
@@ -128,14 +136,8 @@
 
 
 def chunk_sizes(experts):
-    sizes, left = [], experts
-    for part in (16, 8, 4, 4, 4, 8, 16):
-        take = max(1, experts // part)
-        sizes.append(min(take, left))
-        left -= sizes[-1]
-    if left:
-        sizes[len(sizes) // 2] += left
-    return [n for n in sizes if n]
+    unit = experts // 32
+    return [[unit * n for n in group] for group in ((2,), (2, 4), (4, 8, 8, 3, 1))]
 
 
 def piped(w_gate, w_up, router_weight, router_gain, size, banks):
@@ -145,22 +147,27 @@
     def send(x, k, axis="zero", count=size):
         return lax.ppermute(x, axis, xor_pairs(count, k))
 
-    total = square_sums(w_gate, w_up, 0, experts)
-    k = 1
-    while k < size:
-        total = total + send(total, k)
-        k *= 2
-
-    sizes = chunk_sizes(experts)
+    groups = chunk_sizes(experts)
+    sizes = [n for group in groups for n in group]
     chunks = range(len(sizes))
     firsts = [sum(sizes[:c]) for c in chunks]
-    sent, got = [], [dict() for _ in chunks]
+
+    totals, starts = [], [sum(map(sum, groups[:g])) for g in range(len(groups))]
+    for g, group in enumerate(groups):
+        own = square_sums(w_gate, w_up, starts[g], sum(group))
+        own = own + send(own, 1)
+        totals.append([own] + [send(own, k) for k in range(2, size, 2)])
+
+    sent, got = [], []
     for c in chunks:
-        sent.append(scaled_pieces(w_gate, w_up, total, firsts[c], sizes[c], firsts[c], size))
-        got[c] = [sent[c][0]] + [send(sent[c][k], k) for k in range(1, size)]
+        group = max(g for g in range(len(groups)) if starts[g] <= firsts[c])
+        start = firsts[c] - starts[group]
+        sent.append(scaled_pieces(w_gate, w_up, totals[group], firsts[c], sizes[c], start, size))
+        got.append([sent[c][0]] + [send(sent[c][k], k) for k in range(1, size)])
 
     part = (router_weight * router_gain[:, None]).astype(jnp.bfloat16).T
-    row = joined_rows([part] + [send(part, k) for k in range(1, size)])
+    parts = [part] + [send(part, k) for k in range(1, size)]
+    row = joined_rows(parts)
     columns = [row] + [send(row, k, "bank", banks) for k in range(1, banks)]
     serve_router = joined_columns(columns)
 
@@ -169,8 +176,10 @@
         outputs = assembled(got[c], outputs, firsts[c], experts)
     serve_gate, serve_up = (jnp.swapaxes(x, 1, 2) for x in outputs)
 
-    mine = lax.dynamic_slice_in_dim(total, lax.axis_index("zero") * width, width, axis=2)
-    scale = jnp.sqrt(mine)
+    mine = [
+        lax.dynamic_slice_in_dim(sum(parts), lax.axis_index("zero") * width, width, axis=2) for parts in totals
+    ]
+    scale = jnp.sqrt(jnp.concatenate(mine, axis=1))
     return (serve_gate, serve_up, scale[0], scale[1], serve_router)
 
 
@@ -213,10 +222,10 @@
         )
 
     def whole(w_gate, w_up, router_weight, router_gain):
-        _, rows, cols = w_gate.shape
+        experts, rows, cols = w_gate.shape
         powers = size & (size - 1) == 0 and banks & (banks - 1) == 0
         aligned = rows % (128 * size) == 0 and cols % (16 * size) == 0 and router_weight.shape[1] % (16 * banks) == 0
-        if not (powers and aligned and size >= 8):
+        if not (powers and aligned and size >= 8 and experts % (32 * banks) == 0):
             return placed_over(plain)(w_gate, w_up, router_weight, router_gain)
 
         def shards(*args):

time: 402 us -> 404 us (level)
  local copies, waits for them, and re-layouts: 8.04 us -> 45.1 us
  waiting for transfers between devices: 225 us -> 191 us
  Pallas kernels: 99.1 us -> 83.8 us
  starting transfers between devices: 64.1 us -> 78.8 us
    unnamed x86 -> x252, local copies, waits for them, and re-layouts: 6.51 us -> 44.5 us
    ppermute x55 -> x78, waiting for transfers between devices: 225 us -> 191 us  [send(): return lax.ppermute(x, axis, xor_pairs(count, k))]
    ppermute x55 -> x78, starting transfers between devices: 64.1 us -> 78.8 us  [send(): return lax.ppermute(x, axis, xor_pairs(count, k))]
    pallas_call x6 -> x8, Pallas kernels: 33.4 us -> 23.2 us  [assembled(): pl.pallas_call(kernel, grid=(count,), in_specs=[piece] * size + [pl.Block...]
    pallas_call x6 -> x8, Pallas kernels: 41.7 us -> 35.4 us  [scaled_pieces(): pl.pallas_call(kernel, grid=(count,), in_specs=[weights, weights] + [pl.B...]
    pallas_call x1 -> x3, Pallas kernels: 20.4 us -> 21.6 us  [square_sums(): pl.pallas_call(kernel, grid=(count // per_step,), in_specs=[weights, weig...]
  transfers between devices with their start and end apart: 55 -> 78, of which waited for: 20 -> 24; matrix products, arithmetic and copies ran while one was open for 0% -> 1% of each run, Pallas kernels for 18% -> 20%
where the time goes in v2:
time: 404 us; the launch traced here: 403 us
  waiting for transfers between devices  191 us (47%)
  Pallas kernels  83.8 us (21%)
  starting transfers between devices  78.8 us (20%)
  local copies, waits for them, and re-layouts  45.1 us (11%)
    ppermute x78, waiting for transfers between devices, send(): return lax.ppermute(x, axis, xor_pairs(count, k))  191 us
    ppermute x78, starting transfers between devices, send(): return lax.ppermute(x, axis, xor_pairs(count, k))  78.8 us
    unnamed x252, local copies, waits for them, and re-layouts  44.5 us
    pallas_call x8, Pallas kernels, scaled_pieces(): pl.pallas_call(kernel, grid=(count,), in_specs=[weights, weights] + [pl.B...  35.4 us
    pallas_call x8, Pallas kernels, assembled(): pl.pallas_call(kernel, grid=(count,), in_specs=[piece] * size + [pl.Block...  23.2 us
    pallas_call x3, Pallas kernels, square_sums(): pl.pallas_call(kernel, grid=(count // per_step,), in_specs=[weights, weig...  21.6 us
  transfers between devices with their start and end apart: 78, of which 24 were waited for; matrix products, arithmetic and copies ran while one was open for 1% of the time, Pallas kernels for 20%

profile of v2, /device:TPU:0, one launch (start us, length us, event | category | flops | bytes accessed | tf_op | source)
XLA Modules:
  0.0 402.9 jit_solution(4154227501235202631)
XLA Ops:
  1.9 2.5 collective-permute-start.69
  4.5 1.8 collective-permute-start.71
  6.3 2.6 collective-permute-start.73
  9.4 1.5 collective-permute-done.73.refs_6_
  11.0 2.0 collective-permute-done.74.refs_7_
  13.6 1.5 shard_map.102.refs_0_
  15.1 1.6 collective-permute-start.75
  16.7 2.6 collective-permute-start.76
  19.3 4.5 %shard_map.89 = f32[2,6,768]{2,1,0:T(8,128)S(1)} custom-call(f32[32,256,768]{2,1,0:T(8,128)} %gate_ref.21, f32[32,256,768]{2,1,0:T(8,128)} %up_ref.21), custom_call_target="tpu_custom_call" | custom-call | flops 4718592 | bytes 9437184 | tf_op jit(solution)/shard_map/pallas_call | solution.py:33
  23.9 2.2 shard_map.92
  29.2 1.7 collective-permute-start.60
  32.0 1.8 collective-permute-done.60.refs_3_
  34.6 2.3 shard_map.93
  37.9 1.7 collective-permute-start.42
  39.6 3.3 collective-permute-done.42.refs_3_
  44.5 14.9 %shard_map.83 = f32[2,24,768]{2,1,0:T(8,128)S(1)} custom-call(f32[32,256,768]{2,1,0:T(8,128)} %gate_ref.21, f32[32,256,768]{2,1,0:T(8,128)} %up_ref.21), custom_call_target="tpu_custom_call" | custom-call | flops 18874368 | bytes 37748736 | tf_op jit(solution)/shard_map/pallas_call | solution.py:33
  62.5 1.6 collective-permute-start.66
  65.2 2.3 shard_map.91
  68.7 8.2 %collective-permute-done.64.refs_4_ = bf16[2,2,96,256]{3,2,1,0:T(8,128)(2,1)S(1)} collective-permute-done((bf16[2,2,96,256]{3,2,1,0:T(8,128)(2,1)S(1)}, bf16[2,2,96,256]{3,2,1,0:T(8,128)(2,1)S(1)}, u32[]{:S(2)}, u32[]{:S(2)}) %collective-permute-start.64) | collective-permute-done | bytes 196640 | tf_op jit(solution)/shard_map/ppermute | solution.py:148
  82.0 1.4 collective-permute-start.53
  86.0 1.4 collective-permute-start.1
  88.3 5.6 %collective-permute-done.53.refs_4_ = bf16[2,2,96,256]{3,2,1,0:T(8,128)(2,1)S(1)} collective-permute-done((bf16[2,2,96,256]{3,2,1,0:T(8,128)(2,1)S(1)}, bf16[2,2,96,256]{3,2,1,0:T(8,128)(2,1)S(1)}, u32[]{:S(2)}, u32[]{:S(2)}) %collective-permute-start.53) | collective-permute-done | bytes 196640 | tf_op jit(solution)/shard_map/ppermute | solution.py:148
  94.0 1.4 collective-permute-start.3
  95.3 4.9 %collective-permute-done.54.refs_5_ = bf16[2,2,96,256]{3,2,1,0:T(8,128)(2,1)S(1)} collective-permute-done((bf16[2,2,96,256]{3,2,1,0:T(8,128)(2,1)S(1)}, bf16[2,2,96,256]{3,2,1,0:T(8,128)(2,1)S(1)}, u32[]{:S(2)}, u32[]{:S(2)}) %collective-permute-start.54) | collective-permute-done | bytes 196640 | tf_op jit(solution)/shard_map/ppermute | solution.py:148
  100.9 1.9 collective-permute-start.56
  102.8 4.2 %shard_map.90 = (bf16[2,4,96,256]{3,2,1,0:T(8,128)(2,1)S(1)}, bf16[2,4,96,256]{3,2,1,0:T(8,128)(2,1)S(1)}, bf16[2,4,96,256]{3,2,1,0:T(8,128)(2,1)S(1)}, bf16[2,4...) custom-call(f32[32,256,768]{2,1,0:T(8,128)} %gate_ref.21, ...), custom_call_target="tpu_custom_call" | custom-call | flops 3145728 | bytes 9437184 | tf_op jit(solution)/shard_map/pallas_call | solution.py:62
  107.7 1.5 collective-permute-start.44
  110.8 1.7 shard_map.84
  118.4 11.6 %collective-permute-done.10.refs_7_ = bf16[2,1,96,256]{3,2,1,0:T(8,128)(2,1)S(1)} collective-permute-done((bf16[2,1,96,256]{3,2,1,0:T(8,128)(2,1)S(1)}, bf16[2,1,96,256]{3,2,1,0:T(8,128)(2,1)S(1)}, u32[]{:S(2)}, u32[]{:S(2)}) %collective-permute-start.10) | collective-permute-done | bytes 98336 | tf_op jit(solution)/shard_map/ppermute | solution.py:148
  133.2 1.6 collective-permute-start.48
  135.7 3.6 shard_map.85
  140.0 1.5 collective-permute-start.12
  141.5 18.8 %collective-permute-done.47.refs_5_ = bf16[2,4,96,256]{3,2,1,0:T(8,128)(2,1)S(1)} collective-permute-done((bf16[2,4,96,256]{3,2,1,0:T(8,128)(2,1)S(1)}, bf16[2,4,96,256]{3,2,1,0:T(8,128)(2,1)S(1)}, u32[]{:S(2)}, u32[]{:S(2)}) %collective-permute-start.47) | collective-permute-done | bytes 393248 | tf_op jit(solution)/shard_map/ppermute | solution.py:148
  161.2 1.4 collective-permute-start.14
  163.5 1.4 collective-permute-start.16
  164.8 1.5 collective-permute-start.17
  166.3 4.2 %shard_map.88 = (bf16[2,4,96,256]{3,2,1,0:T(8,128)(2,1)S(1)}, bf16[2,4,96,256]{3,2,1,0:T(8,128)(2,1)S(1)}, bf16[2,4,96,256]{3,2,1,0:T(8,128)(2,1)S(1)}, bf16[2,4...) custom-call(f32[32,256,768]{2,1,0:T(8,128)} %gate_ref.21, ...), custom_call_target="tpu_custom_call" | custom-call | flops 3145728 | bytes 9437184 | tf_op jit(solution)/shard_map/pallas_call | solution.py:62
  172.2 11.4 %collective-permute-done.14.refs_4_ = bf16[2,3,96,256]{3,2,1,0:T(8,128)(2,1)S(1)} collective-permute-done((bf16[2,3,96,256]{3,2,1,0:T(8,128)(2,1)S(1)}, bf16[2,3,96,256]{3,2,1,0:T(8,128)(2,1)S(1)}, u32[]{:S(2)}, u32[]{:S(2)}) %collective-permute-start.14) | collective-permute-done | bytes 294944 | tf_op jit(solution)/shard_map/ppermute | solution.py:148
  185.5 3.0 collective-permute-done.15.refs_5_
  189.2 1.6 collective-permute-start.34
  194.0 1.7 collective-permute-start.37
  195.8 7.9 %shard_map.87 = (bf16[2,8,96,256]{3,2,1,0:T(8,128)(2,1)S(1)}, bf16[2,8,96,256]{3,2,1,0:T(8,128)(2,1)S(1)}, bf16[2,8,96,256]{3,2,1,0:T(8,128)(2,1)S(1)}, bf16[2,8...) custom-call(f32[32,256,768]{2,1,0:T(8,128)} %gate_ref.21, ...), custom_call_target="tpu_custom_call" | custom-call | flops 6291456 | bytes 18874368 | tf_op jit(solution)/shard_map/pallas_call | solution.py:62
  206.7 5.3 %collective-permute-done.35.refs_4_ = bf16[2,4,96,256]{3,2,1,0:T(8,128)(2,1)S(1)} collective-permute-done((bf16[2,4,96,256]{3,2,1,0:T(8,128)(2,1)S(1)}, bf16[2,4,96,256]{3,2,1,0:T(8,128)(2,1)S(1)}, u32[]{:S(2)}, u32[]{:S(2)}) %collective-permute-start.35) | collective-permute-done | bytes 393248 | tf_op jit(solution)/shard_map/ppermute | solution.py:148
  212.7 5.0 %collective-permute-done.36.refs_5_ = bf16[2,4,96,256]{3,2,1,0:T(8,128)(2,1)S(1)} collective-permute-done((bf16[2,4,96,256]{3,2,1,0:T(8,128)(2,1)S(1)}, bf16[2,4,96,256]{3,2,1,0:T(8,128)(2,1)S(1)}, u32[]{:S(2)}, u32[]{:S(2)}) %collective-permute-start.36) | collective-permute-done | bytes 393248 | tf_op jit(solution)/shard_map/ppermute | solution.py:148
  219.0 1.9 collective-permute-start.38
  220.9 9.4 %shard_map.86 = (bf16[2,8,96,256]{3,2,1,0:T(8,128)(2,1)S(1)}, bf16[2,8,96,256]{3,2,1,0:T(8,128)(2,1)S(1)}, bf16[2,8,96,256]{3,2,1,0:T(8,128)(2,1)S(1)}, bf16[2,8...) custom-call(f32[32,256,768]{2,1,0:T(8,128)} %gate_ref.21, ...), custom_call_target="tpu_custom_call" | custom-call | flops 6291456 | bytes 18874368 | tf_op jit(solution)/shard_map/pallas_call | solution.py:62
  231.2 19.9 %collective-permute-done.38.refs_7_ = bf16[2,4,96,256]{3,2,1,0:T(8,128)(2,1)S(1)} collective-permute-done((bf16[2,4,96,256]{3,2,1,0:T(8,128)(2,1)S(1)}, bf16[2,4,96,256]{3,2,1,0:T(8,128)(2,1)S(1)}, u32[]{:S(2)}, u32[]{:S(2)}) %collective-permute-start.38) | collective-permute-done | bytes 393248 | tf_op jit(solution)/shard_map/ppermute | solution.py:148
  252.9 1.6 collective-permute-start.30
  258.9 45.4 %collective-permute-done.29.refs_5_ = bf16[2,8,96,256]{3,2,1,0:T(8,128)(2,1)S(1)} collective-permute-done((bf16[2,8,96,256]{3,2,1,0:T(8,128)(2,1)S(1)}, bf16[2,8,96,256]{3,2,1,0:T(8,128)(2,1)S(1)}, u32[]{:S(2)}, u32[]{:S(2)}) %collective-permute-start.29) | collective-permute-done | bytes 786464 | tf_op jit(solution)/shard_map/ppermute | solution.py:148
  305.2 1.8 collective-permute-start.20
  310.6 1.8 collective-permute-start.23
  313.4 1.6 collective-permute-start.24
  316.5 2.1 shard_map.103
  326.0 1.4 shard_map.94
  335.0 1.4 shard_map.95
  337.6 24.7 %collective-permute-done.21.refs_4_ = bf16[2,8,96,256]{3,2,1,0:T(8,128)(2,1)} collective-permute-done((bf16[2,8,96,256]{3,2,1,0:T(8,128)(2,1)}, bf16[2,8,96,256]{3,2,1,0:T(8,128)(2,1)}, u32[]{:S(2)}, u32[]{:S(2)}) %collective-permute-start.21) | collective-permute-done | bytes 786464 | tf_op jit(solution)/shard_map/ppermute | solution.py:148
  362.3 14.1 %collective-permute-done.22.refs_5_ = bf16[2,8,96,256]{3,2,1,0:T(8,128)(2,1)} collective-permute-done((bf16[2,8,96,256]{3,2,1,0:T(8,128)(2,1)}, bf16[2,8,96,256]{3,2,1,0:T(8,128)(2,1)}, u32[]{:S(2)}, u32[]{:S(2)}) %collective-permute-start.22) | collective-permute-done | bytes 786464 | tf_op jit(solution)/shard_map/ppermute | solution.py:148
  377.5 1.5 collective-permute-start.8
  379.0 1.8 collective-permute-start.9
  381.5 2.5 shard_map.96
  384.1 2.5 shard_map.97
  387.3 4.5 %shard_map.98 = (bf16[32,96,2048]{2,1,0:T(8,128)(2,1)}, bf16[32,96,2048]{2,1,0:T(8,128)(2,1)}) custom-call(bf16[2,8,96,256]{3,2,1,0:T(8,128)(2,1)S(1)} %get-tuple-element.109.refs_0_, bf16[2,8,96,256]{3,2,1,0:T(8,128)(2,1)S(1)} %collective-permute-done.25.refs_1_, ...), custom_call_target="tpu_custom_call", output_to_operand_aliasing={{0}: (8, {}), {1}: (9, {})} | custom-call | flops 1572864 | bytes 12582912 | tf_op jit(solution)/shard_map/pallas_call | solution.py:89
  391.9 7.7 %shard_map.99 = (bf16[32,96,2048]{2,1,0:T(8,128)(2,1)}, bf16[32,96,2048]{2,1,0:T(8,128)(2,1)}) custom-call(bf16[2,8,96,256]{3,2,1,0:T(8,128)(2,1)S(1)} %copy-done.5, bf16[2,8,96,256]{3,2,1,0:T(8,128)(2,1)S(1)} %copy-done.11, bf16[2,8,96,256]{3,2,1,0:T(8,128)(2,1)S(1)} %copy-done.15, ...), custom_call_target="tpu_custom_call", output_to_operand_aliasing={{0}: (8, {}), {1}: (9, {})} | custom-call | flops 1572864 | bytes 12582912 | tf_op jit(solution)/shard_map/pallas_call | solution.py:89
  399.7 2.1 shard_map.100
  (374 shorter events, 85.6 us)
Async XLA Ops:
  1.9 7.0 %collective-permute-start.69 = (bf16[32,256]{1,0:T(8,128)(2,1)S(1)}, bf16[32,256]{1,0:T(8,128)(2,1)S(1)}, u32[]{:S(2)}, u32[]{:S(2)}) collective-permute-start(bf16[32,256]{1,0:T(8,128)(2,1)S(1)} %fusion.refs_0_), channel_id=1, source_target_pairs={{0,2},{1,3},{2,0},{3,1},{4,6},{5,7},{6,4},{7,5},{8,10},{9,11},{10,... | collective-permute-start | bytes 49160 | tf_op jit(solution)/shard_map/ppermute | solution.py:148
  15.1 28.7 %collective-permute-start.75 = (bf16[32,2048]{1,0:T(8,128)(2,1)}, bf16[32,2048]{1,0:T(8,128)(2,1)S(1)}, u32[]{:S(2)}, u32[]{:S(2)}) collective-permute-start(bf16[32,2048]{1,0:T(8,128)(2,1)} %shard_map.102.refs_0_), channel_id=1, source_target_pairs={{0,8},{8,0},{16,24},{24,16},{1,9},{9,1},{17,25},{25,17},{2,10},{10... | collective-permute-start | bytes 393224 | tf_op jit(solution)/shard_map/ppermute | solution.py:148
  16.7 42.7 %collective-permute-start.76 = (bf16[32,2048]{1,0:T(8,128)(2,1)}, bf16[32,2048]{1,0:T(8,128)(2,1)S(1)}, u32[]{:S(2)}, u32[]{:S(2)}) collective-permute-start(bf16[32,2048]{1,0:T(8,128)(2,1)} %shard_map.102.refs_0_), channel_id=1, source_target_pairs={{0,16},{8,24},{16,0},{24,8},{1,17},{9,25},{17,1},{25,9},{2,18},{10... | collective-permute-start | bytes 393224 | tf_op jit(solution)/shard_map/ppermute | solution.py:148
  23.8 5.5 %collective-permute-start.39 = (f32[2,6,768]{2,1,0:T(8,128)S(1)}, f32[2,6,768]{2,1,0:T(8,128)S(1)}, u32[]{:S(2)}, u32[]{:S(2)}) collective-permute-start(f32[2,6,768]{2,1,0:T(8,128)S(1)} %shard_map.89), channel_id=1, source_target_pairs={{0,1},{1,0},{2,3},{3,2},{4,5},{5,4},{6,7},{7,6},{8,9},{9,8},{10,11... | collective-permute-start | bytes 110600 | tf_op jit(solution)/shard_map/ppermute | solution.py:148
  31.2 5.8 %collective-permute-start.40 = (f32[2,6,768]{2,1,0:T(8,128)S(1)}, f32[2,6,768]{2,1,0:T(8,128)S(1)}, u32[]{:S(2)}, u32[]{:S(2)}) collective-permute-start(f32[2,6,768]{2,1,0:T(8,128)S(1)} %add.42.refs_0_), channel_id=1, source_target_pairs={{0,2},{1,3},{2,0},{3,1},{4,6},{5,7},{6,4},{7,5},{8,10},{9,11},{10,... | collective-permute-start | bytes 110600 | tf_op jit(solution)/shard_map/ppermute | solution.py:148
  31.7 29.0 %collective-permute-start.77 = (bf16[32,2048]{1,0:T(8,128)(2,1)S(1)}, bf16[32,2048]{1,0:T(8,128)(2,1)S(1)}, u32[]{:S(2)}, u32[]{:S(2)}) collective-permute-start(bf16[32,2048]{1,0:T(8,128)(2,1)S(1)} %copy-done.113), channel_id=1, source_target_pairs={{0,24},{8,16},{16,8},{24,0},{1,25},{9,17},{17,9},{25,1},{2,26},{10... | collective-permute-start | bytes 393224 | tf_op jit(solution)/shard_map/ppermute | solution.py:148
  37.0 25.6 %collective-permute-start.61 = (bf16[2,2,96,256]{3,2,1,0:T(8,128)(2,1)S(1)}, bf16[2,2,96,256]{3,2,1,0:T(8,128)(2,1)S(1)}, u32[]{:S(2)}, u32[]{:S(2)}) collective-permute-start(bf16[2,2,96,256]{3,2,1,0:T(8,128)(2,1)S(1)} %get-tuple-element.142), channel_id=1, source_target_pairs={{0,1},{1,0},{2,3},{3,2},{4,5},{5,4},{6,7},{7,6},{8,9},{9,8},{10,11... | collective-permute-start | bytes 589832 | tf_op jit(solution)/shard_map/ppermute | solution.py:148
  42.9 21.2 %collective-permute-start.62 = (bf16[2,2,96,256]{3,2,1,0:T(8,128)(2,1)S(1)}, bf16[2,2,96,256]{3,2,1,0:T(8,128)(2,1)S(1)}, u32[]{:S(2)}, u32[]{:S(2)}) collective-permute-start(bf16[2,2,96,256]{3,2,1,0:T(8,128)(2,1)S(1)} %get-tuple-element.143), channel_id=1, source_target_pairs={{0,2},{1,3},{2,0},{3,1},{4,6},{5,7},{6,4},{7,5},{8,10},{9,11},{10,... | collective-permute-start | bytes 589832 | tf_op jit(solution)/shard_map/ppermute | solution.py:148
  44.5 23.1 %collective-permute-start.63 = (bf16[2,2,96,256]{3,2,1,0:T(8,128)(2,1)S(1)}, bf16[2,2,96,256]{3,2,1,0:T(8,128)(2,1)S(1)}, u32[]{:S(2)}, u32[]{:S(2)}) collective-permute-start(bf16[2,2,96,256]{3,2,1,0:T(8,128)(2,1)S(1)} %get-tuple-element.144), channel_id=1, source_target_pairs={{0,3},{1,2},{2,1},{3,0},{4,7},{5,6},{6,5},{7,4},{8,11},{9,10},{10,... | collective-permute-start | bytes 589832 | tf_op jit(solution)/shard_map/ppermute | solution.py:148
  60.8 16.2 %collective-permute-start.64 = (bf16[2,2,96,256]{3,2,1,0:T(8,128)(2,1)S(1)}, bf16[2,2,96,256]{3,2,1,0:T(8,128)(2,1)S(1)}, u32[]{:S(2)}, u32[]{:S(2)}) collective-permute-start(bf16[2,2,96,256]{3,2,1,0:T(8,128)(2,1)S(1)} %get-tuple-element.145), channel_id=1, source_target_pairs={{0,4},{1,5},{2,6},{3,7},{4,0},{5,1},{6,2},{7,3},{8,12},{9,13},{10,... | collective-permute-start | bytes 589832 | tf_op jit(solution)/shard_map/ppermute | solution.py:148
  61.8 17.7 %collective-permute-start.65 = (bf16[2,2,96,256]{3,2,1,0:T(8,128)(2,1)S(1)}, bf16[2,2,96,256]{3,2,1,0:T(8,128)(2,1)S(1)}, u32[]{:S(2)}, u32[]{:S(2)}) collective-permute-start(bf16[2,2,96,256]{3,2,1,0:T(8,128)(2,1)S(1)} %get-tuple-element.146), channel_id=1, source_target_pairs={{0,5},{1,4},{2,7},{3,6},{4,1},{5,0},{6,3},{7,2},{8,13},{9,12},{10,... | collective-permute-start | bytes 589832 | tf_op jit(solution)/shard_map/ppermute | solution.py:148
  62.5 18.8 %collective-permute-start.66 = (bf16[2,2,96,256]{3,2,1,0:T(8,128)(2,1)S(1)}, bf16[2,2,96,256]{3,2,1,0:T(8,128)(2,1)S(1)}, u32[]{:S(2)}, u32[]{:S(2)}) collective-permute-start(bf16[2,2,96,256]{3,2,1,0:T(8,128)(2,1)S(1)} %get-tuple-element.147), channel_id=1, source_target_pairs={{0,6},{1,7},{2,4},{3,5},{4,2},{5,3},{6,0},{7,1},{8,14},{9,15},{10,... | collective-permute-start | bytes 589832 | tf_op jit(solution)/shard_map/ppermute | solution.py:148
  64.1 19.3 %collective-permute-start.67 = (bf16[2,2,96,256]{3,2,1,0:T(8,128)(2,1)S(1)}, bf16[2,2,96,256]{3,2,1,0:T(8,128)(2,1)S(1)}, u32[]{:S(2)}, u32[]{:S(2)}) collective-permute-start(bf16[2,2,96,256]{3,2,1,0:T(8,128)(2,1)S(1)} %get-tuple-element.148), channel_id=1, source_target_pairs={{0,7},{1,6},{2,5},{3,4},{4,3},{5,2},{6,1},{7,0},{8,15},{9,14},{10,... | collective-permute-start | bytes 589832 | tf_op jit(solution)/shard_map/ppermute | solution.py:148
  68.3 15.8 %collective-permute-start.50 = (bf16[2,2,96,256]{3,2,1,0:T(8,128)(2,1)S(1)}, bf16[2,2,96,256]{3,2,1,0:T(8,128)(2,1)S(1)}, u32[]{:S(2)}, u32[]{:S(2)}) collective-permute-start(bf16[2,2,96,256]{3,2,1,0:T(8,128)(2,1)S(1)} %get-tuple-element.134), channel_id=1, source_target_pairs={{0,1},{1,0},{2,3},{3,2},{4,5},{5,4},{6,7},{7,6},{8,9},{9,8},{10,11... | collective-permute-start | bytes 589832 | tf_op jit(solution)/shard_map/ppermute | solution.py:148
  77.6 7.7 %collective-permute-start.51 = (bf16[2,2,96,256]{3,2,1,0:T(8,128)(2,1)S(1)}, bf16[2,2,96,256]{3,2,1,0:T(8,128)(2,1)S(1)}, u32[]{:S(2)}, u32[]{:S(2)}) collective-permute-start(bf16[2,2,96,256]{3,2,1,0:T(8,128)(2,1)S(1)} %get-tuple-element.135), channel_id=1, source_target_pairs={{0,2},{1,3},{2,0},{3,1},{4,6},{5,7},{6,4},{7,5},{8,10},{9,11},{10,... | collective-permute-start | bytes 589832 | tf_op jit(solution)/shard_map/ppermute | solution.py:148
  80.1 7.3 %collective-permute-start.52 = (bf16[2,2,96,256]{3,2,1,0:T(8,128)(2,1)S(1)}, bf16[2,2,96,256]{3,2,1,0:T(8,128)(2,1)S(1)}, u32[]{:S(2)}, u32[]{:S(2)}) collective-permute-start(bf16[2,2,96,256]{3,2,1,0:T(8,128)(2,1)S(1)} %get-tuple-element.136), channel_id=1, source_target_pairs={{0,3},{1,2},{2,1},{3,0},{4,7},{5,6},{6,5},{7,4},{8,11},{9,10},{10,... | collective-permute-start | bytes 589832 | tf_op jit(solution)/shard_map/ppermute | solution.py:148
  82.0 12.0 %collective-permute-start.53 = (bf16[2,2,96,256]{3,2,1,0:T(8,128)(2,1)S(1)}, bf16[2,2,96,256]{3,2,1,0:T(8,128)(2,1)S(1)}, u32[]{:S(2)}, u32[]{:S(2)}) collective-permute-start(bf16[2,2,96,256]{3,2,1,0:T(8,128)(2,1)S(1)} %get-tuple-element.137), channel_id=1, source_target_pairs={{0,4},{1,5},{2,6},{3,7},{4,0},{5,1},{6,2},{7,3},{8,12},{9,13},{10,... | collective-permute-start | bytes 589832 | tf_op jit(solution)/shard_map/ppermute | solution.py:148
  84.1 16.2 %collective-permute-start.54 = (bf16[2,2,96,256]{3,2,1,0:T(8,128)(2,1)S(1)}, bf16[2,2,96,256]{3,2,1,0:T(8,128)(2,1)S(1)}, u32[]{:S(2)}, u32[]{:S(2)}) collective-permute-start(bf16[2,2,96,256]{3,2,1,0:T(8,128)(2,1)S(1)} %get-tuple-element.138), channel_id=1, source_target_pairs={{0,5},{1,4},{2,7},{3,6},{4,1},{5,0},{6,3},{7,2},{8,13},{9,12},{10,... | collective-permute-start | bytes 589832 | tf_op jit(solution)/shard_map/ppermute | solution.py:148
  84.1 22.9 %collective-permute-start.55 = (bf16[2,2,96,256]{3,2,1,0:T(8,128)(2,1)S(1)}, bf16[2,2,96,256]{3,2,1,0:T(8,128)(2,1)S(1)}, u32[]{:S(2)}, u32[]{:S(2)}) collective-permute-start(bf16[2,2,96,256]{3,2,1,0:T(8,128)(2,1)S(1)} %get-tuple-element.139), channel_id=1, source_target_pairs={{0,6},{1,7},{2,4},{3,5},{4,2},{5,3},{6,0},{7,1},{8,14},{9,15},{10,... | collective-permute-start | bytes 589832 | tf_op jit(solution)/shard_map/ppermute | solution.py:148
  86.0 21.7 %collective-permute-start.1 = (f32[2,24,768]{2,1,0:T(8,128)S(1)}, f32[2,24,768]{2,1,0:T(8,128)S(1)}, u32[]{:S(2)}, u32[]{:S(2)}) collective-permute-start(f32[2,24,768]{2,1,0:T(8,128)S(1)} %add.41.refs_0_), channel_id=1, source_target_pairs={{0,2},{1,3},{2,0},{3,1},{4,6},{5,7},{6,4},{7,5},{8,10},{9,11},{10,... | collective-permute-start | bytes 442376 | tf_op jit(solution)/shard_map/ppermute | solution.py:148
  87.4 21.8 %collective-permute-start.2 = (f32[2,24,768]{2,1,0:T(8,128)S(1)}, f32[2,24,768]{2,1,0:T(8,128)S(1)}, u32[]{:S(2)}, u32[]{:S(2)}) collective-permute-start(f32[2,24,768]{2,1,0:T(8,128)S(1)} %add.41.refs_0_), channel_id=1, source_target_pairs={{0,4},{1,5},{2,6},{3,7},{4,0},{5,1},{6,2},{7,3},{8,12},{9,13},{10,... | collective-permute-start | bytes 442376 | tf_op jit(solution)/shard_map/ppermute | solution.py:148
  94.0 15.6 %collective-permute-start.3 = (f32[2,24,768]{2,1,0:T(8,128)S(1)}, f32[2,24,768]{2,1,0:T(8,128)S(1)}, u32[]{:S(2)}, u32[]{:S(2)}) collective-permute-start(f32[2,24,768]{2,1,0:T(8,128)S(1)} %add.41.refs_0_), channel_id=1, source_target_pairs={{0,6},{1,7},{2,4},{3,5},{4,2},{5,3},{6,0},{7,1},{8,14},{9,15},{10,... | collective-permute-start | bytes 442376 | tf_op jit(solution)/shard_map/ppermute | solution.py:148
  100.9 15.4 %collective-permute-start.56 = (bf16[2,2,96,256]{3,2,1,0:T(8,128)(2,1)S(1)}, bf16[2,2,96,256]{3,2,1,0:T(8,128)(2,1)S(1)}, u32[]{:S(2)}, u32[]{:S(2)}) collective-permute-start(bf16[2,2,96,256]{3,2,1,0:T(8,128)(2,1)S(1)} %get-tuple-element.140), channel_id=1, source_target_pairs={{0,7},{1,6},{2,5},{3,4},{4,3},{5,2},{6,1},{7,0},{8,15},{9,14},{10,... | collective-permute-start | bytes 589832 | tf_op jit(solution)/shard_map/ppermute | solution.py:148
  107.7 25.5 %collective-permute-start.43 = (bf16[2,4,96,256]{3,2,1,0:T(8,128)(2,1)S(1)}, bf16[2,4,96,256]{3,2,1,0:T(8,128)(2,1)S(1)}, u32[]{:S(2)}, u32[]{:S(2)}) collective-permute-start(bf16[2,4,96,256]{3,2,1,0:T(8,128)(2,1)S(1)} %get-tuple-element.126), channel_id=1, source_target_pairs={{0,1},{1,0},{2,3},{3,2},{4,5},{5,4},{6,7},{7,6},{8,9},{9,8},{10,11... | collective-permute-start | bytes 1179656 | tf_op jit(solution)/shard_map/ppermute | solution.py:148
  107.7 27.1 %collective-permute-start.44 = (bf16[2,4,96,256]{3,2,1,0:T(8,128)(2,1)S(1)}, bf16[2,4,96,256]{3,2,1,0:T(8,128)(2,1)S(1)}, u32[]{:S(2)}, u32[]{:S(2)}) collective-permute-start(bf16[2,4,96,256]{3,2,1,0:T(8,128)(2,1)S(1)} %get-tuple-element.127), channel_id=1, source_target_pairs={{0,2},{1,3},{2,0},{3,1},{4,6},{5,7},{6,4},{7,5},{8,10},{9,11},{10,... | collective-permute-start | bytes 1179656 | tf_op jit(solution)/shard_map/ppermute | solution.py:148
  109.2 30.2 %collective-permute-start.45 = (bf16[2,4,96,256]{3,2,1,0:T(8,128)(2,1)S(1)}, bf16[2,4,96,256]{3,2,1,0:T(8,128)(2,1)S(1)}, u32[]{:S(2)}, u32[]{:S(2)}) collective-permute-start(bf16[2,4,96,256]{3,2,1,0:T(8,128)(2,1)S(1)} %get-tuple-element.128), channel_id=1, source_target_pairs={{0,3},{1,2},{2,1},{3,0},{4,7},{5,6},{6,5},{7,4},{8,11},{9,10},{10,... | collective-permute-start | bytes 1179656 | tf_op jit(solution)/shard_map/ppermute | solution.py:148
  109.6 30.4 %collective-permute-start.46 = (bf16[2,4,96,256]{3,2,1,0:T(8,128)(2,1)S(1)}, bf16[2,4,96,256]{3,2,1,0:T(8,128)(2,1)S(1)}, u32[]{:S(2)}, u32[]{:S(2)}) collective-permute-start(bf16[2,4,96,256]{3,2,1,0:T(8,128)(2,1)S(1)} %get-tuple-element.129), channel_id=1, source_target_pairs={{0,4},{1,5},{2,6},{3,7},{4,0},{5,1},{6,2},{7,3},{8,12},{9,13},{10,... | collective-permute-start | bytes 1179656 | tf_op jit(solution)/shard_map/ppermute | solution.py:148
  117.0 12.9 %collective-permute-start.10 = (bf16[2,1,96,256]{3,2,1,0:T(8,128)(2,1)S(1)}, bf16[2,1,96,256]{3,2,1,0:T(8,128)(2,1)S(1)}, u32[]{:S(2)}, u32[]{:S(2)}) collective-permute-start(bf16[2,1,96,256]{3,2,1,0:T(8,128)(2,1)S(1)} %get-tuple-element.92), channel_id=1, source_target_pairs={{0,7},{1,6},{2,5},{3,4},{4,3},{5,2},{6,1},{7,0},{8,15},{9,14},{10,... | collective-permute-start | bytes 294920 | tf_op jit(solution)/shard_map/ppermute | solution.py:148
  132.5 27.8 %collective-permute-start.47 = (bf16[2,4,96,256]{3,2,1,0:T(8,128)(2,1)S(1)}, bf16[2,4,96,256]{3,2,1,0:T(8,128)(2,1)S(1)}, u32[]{:S(2)}, u32[]{:S(2)}) collective-permute-start(bf16[2,4,96,256]{3,2,1,0:T(8,128)(2,1)S(1)} %get-tuple-element.130), channel_id=1, source_target_pairs={{0,5},{1,4},{2,7},{3,6},{4,1},{5,0},{6,3},{7,2},{8,13},{9,12},{10,... | collective-permute-start | bytes 1179656 | tf_op jit(solution)/shard_map/ppermute | solution.py:148
  133.2 27.9 %collective-permute-start.48 = (bf16[2,4,96,256]{3,2,1,0:T(8,128)(2,1)S(1)}, bf16[2,4,96,256]{3,2,1,0:T(8,128)(2,1)S(1)}, u32[]{:S(2)}, u32[]{:S(2)}) collective-permute-start(bf16[2,4,96,256]{3,2,1,0:T(8,128)(2,1)S(1)} %get-tuple-element.131), channel_id=1, source_target_pairs={{0,6},{1,7},{2,4},{3,5},{4,2},{5,3},{6,0},{7,1},{8,14},{9,15},{10,... | collective-permute-start | bytes 1179656 | tf_op jit(solution)/shard_map/ppermute | solution.py:148
  134.8 27.7 %collective-permute-start.49 = (bf16[2,4,96,256]{3,2,1,0:T(8,128)(2,1)S(1)}, bf16[2,4,96,256]{3,2,1,0:T(8,128)(2,1)S(1)}, u32[]{:S(2)}, u32[]{:S(2)}) collective-permute-start(bf16[2,4,96,256]{3,2,1,0:T(8,128)(2,1)S(1)} %get-tuple-element.132), channel_id=1, source_target_pairs={{0,7},{1,6},{2,5},{3,4},{4,3},{5,2},{6,1},{7,0},{8,15},{9,14},{10,... | collective-permute-start | bytes 1179656 | tf_op jit(solution)/shard_map/ppermute | solution.py:148
  139.4 23.4 %collective-permute-start.11 = (bf16[2,3,96,256]{3,2,1,0:T(8,128)(2,1)S(1)}, bf16[2,3,96,256]{3,2,1,0:T(8,128)(2,1)S(1)}, u32[]{:S(2)}, u32[]{:S(2)}) collective-permute-start(bf16[2,3,96,256]{3,2,1,0:T(8,128)(2,1)S(1)} %get-tuple-element.94), channel_id=1, source_target_pairs={{0,1},{1,0},{2,3},{3,2},{4,5},{5,4},{6,7},{7,6},{8,9},{9,8},{10,11... | collective-permute-start | bytes 884744 | tf_op jit(solution)/shard_map/ppermute | solution.py:148
  140.0 24.8 %collective-permute-start.12 = (bf16[2,3,96,256]{3,2,1,0:T(8,128)(2,1)S(1)}, bf16[2,3,96,256]{3,2,1,0:T(8,128)(2,1)S(1)}, u32[]{:S(2)}, u32[]{:S(2)}) collective-permute-start(bf16[2,3,96,256]{3,2,1,0:T(8,128)(2,1)S(1)} %get-tuple-element.95), channel_id=1, source_target_pairs={{0,2},{1,3},{2,0},{3,1},{4,6},{5,7},{6,4},{7,5},{8,10},{9,11},{10,... | collective-permute-start | bytes 884744 | tf_op jit(solution)/shard_map/ppermute | solution.py:148
  160.3 11.0 %collective-permute-start.13 = (bf16[2,3,96,256]{3,2,1,0:T(8,128)(2,1)S(1)}, bf16[2,3,96,256]{3,2,1,0:T(8,128)(2,1)S(1)}, u32[]{:S(2)}, u32[]{:S(2)}) collective-permute-start(bf16[2,3,96,256]{3,2,1,0:T(8,128)(2,1)S(1)} %get-tuple-element.96), channel_id=1, source_target_pairs={{0,3},{1,2},{2,1},{3,0},{4,7},{5,6},{6,5},{7,4},{8,11},{9,10},{10,... | collective-permute-start | bytes 884744 | tf_op jit(solution)/shard_map/ppermute | solution.py:148
  161.2 22.5 %collective-permute-start.14 = (bf16[2,3,96,256]{3,2,1,0:T(8,128)(2,1)S(1)}, bf16[2,3,96,256]{3,2,1,0:T(8,128)(2,1)S(1)}, u32[]{:S(2)}, u32[]{:S(2)}) collective-permute-start(bf16[2,3,96,256]{3,2,1,0:T(8,128)(2,1)S(1)} %get-tuple-element.97), channel_id=1, source_target_pairs={{0,4},{1,5},{2,6},{3,7},{4,0},{5,1},{6,2},{7,3},{8,12},{9,13},{10,... | collective-permute-start | bytes 884744 | tf_op jit(solution)/shard_map/ppermute | solution.py:148
  162.5 25.9 %collective-permute-start.15 = (bf16[2,3,96,256]{3,2,1,0:T(8,128)(2,1)S(1)}, bf16[2,3,96,256]{3,2,1,0:T(8,128)(2,1)S(1)}, u32[]{:S(2)}, u32[]{:S(2)}) collective-permute-start(bf16[2,3,96,256]{3,2,1,0:T(8,128)(2,1)S(1)} %get-tuple-element.98), channel_id=1, source_target_pairs={{0,5},{1,4},{2,7},{3,6},{4,1},{5,0},{6,3},{7,2},{8,13},{9,12},{10,... | collective-permute-start | bytes 884744 | tf_op jit(solution)/shard_map/ppermute | solution.py:148
  163.5 27.4 %collective-permute-start.16 = (bf16[2,3,96,256]{3,2,1,0:T(8,128)(2,1)S(1)}, bf16[2,3,96,256]{3,2,1,0:T(8,128)(2,1)S(1)}, u32[]{:S(2)}, u32[]{:S(2)}) collective-permute-start(bf16[2,3,96,256]{3,2,1,0:T(8,128)(2,1)S(1)} %get-tuple-element.99), channel_id=1, source_target_pairs={{0,6},{1,7},{2,4},{3,5},{4,2},{5,3},{6,0},{7,1},{8,14},{9,15},{10,... | collective-permute-start | bytes 884744 | tf_op jit(solution)/shard_map/ppermute | solution.py:148
  164.8 27.5 %collective-permute-start.17 = (bf16[2,3,96,256]{3,2,1,0:T(8,128)(2,1)S(1)}, bf16[2,3,96,256]{3,2,1,0:T(8,128)(2,1)S(1)}, u32[]{:S(2)}, u32[]{:S(2)}) collective-permute-start(bf16[2,3,96,256]{3,2,1,0:T(8,128)(2,1)S(1)} %get-tuple-element.100), channel_id=1, source_target_pairs={{0,7},{1,6},{2,5},{3,4},{4,3},{5,2},{6,1},{7,0},{8,15},{9,14},{10,... | collective-permute-start | bytes 884744 | tf_op jit(solution)/shard_map/ppermute | solution.py:148
  172.0 21.3 %collective-permute-start.32 = (bf16[2,4,96,256]{3,2,1,0:T(8,128)(2,1)S(1)}, bf16[2,4,96,256]{3,2,1,0:T(8,128)(2,1)S(1)}, u32[]{:S(2)}, u32[]{:S(2)}) collective-permute-start(bf16[2,4,96,256]{3,2,1,0:T(8,128)(2,1)S(1)} %get-tuple-element.118), channel_id=1, source_target_pairs={{0,1},{1,0},{2,3},{3,2},{4,5},{5,4},{6,7},{7,6},{8,9},{9,8},{10,11... | collective-permute-start | bytes 1179656 | tf_op jit(solution)/shard_map/ppermute | solution.py:148
  184.4 19.3 %collective-permute-start.33 = (bf16[2,4,96,256]{3,2,1,0:T(8,128)(2,1)S(1)}, bf16[2,4,96,256]{3,2,1,0:T(8,128)(2,1)S(1)}, u32[]{:S(2)}, u32[]{:S(2)}) collective-permute-start(bf16[2,4,96,256]{3,2,1,0:T(8,128)(2,1)S(1)} %get-tuple-element.119), channel_id=1, source_target_pairs={{0,2},{1,3},{2,0},{3,1},{4,6},{5,7},{6,4},{7,5},{8,10},{9,11},{10,... | collective-permute-start | bytes 1179656 | tf_op jit(solution)/shard_map/ppermute | solution.py:148
  189.2 16.1 %collective-permute-start.34 = (bf16[2,4,96,256]{3,2,1,0:T(8,128)(2,1)S(1)}, bf16[2,4,96,256]{3,2,1,0:T(8,128)(2,1)S(1)}, u32[]{:S(2)}, u32[]{:S(2)}) collective-permute-start(bf16[2,4,96,256]{3,2,1,0:T(8,128)(2,1)S(1)} %get-tuple-element.120), channel_id=1, source_target_pairs={{0,3},{1,2},{2,1},{3,0},{4,7},{5,6},{6,5},{7,4},{8,11},{9,10},{10,... | collective-permute-start | bytes 1179656 | tf_op jit(solution)/shard_map/ppermute | solution.py:148
  191.6 20.4 %collective-permute-start.35 = (bf16[2,4,96,256]{3,2,1,0:T(8,128)(2,1)S(1)}, bf16[2,4,96,256]{3,2,1,0:T(8,128)(2,1)S(1)}, u32[]{:S(2)}, u32[]{:S(2)}) collective-permute-start(bf16[2,4,96,256]{3,2,1,0:T(8,128)(2,1)S(1)} %get-tuple-element.121), channel_id=1, source_target_pairs={{0,4},{1,5},{2,6},{3,7},{4,0},{5,1},{6,2},{7,3},{8,12},{9,13},{10,... | collective-permute-start | bytes 1179656 | tf_op jit(solution)/shard_map/ppermute | solution.py:148
  193.1 24.6 %collective-permute-start.36 = (bf16[2,4,96,256]{3,2,1,0:T(8,128)(2,1)S(1)}, bf16[2,4,96,256]{3,2,1,0:T(8,128)(2,1)S(1)}, u32[]{:S(2)}, u32[]{:S(2)}) collective-permute-start(bf16[2,4,96,256]{3,2,1,0:T(8,128)(2,1)S(1)} %get-tuple-element.122), channel_id=1, source_target_pairs={{0,5},{1,4},{2,7},{3,6},{4,1},{5,0},{6,3},{7,2},{8,13},{9,12},{10,... | collective-permute-start | bytes 1179656 | tf_op jit(solution)/shard_map/ppermute | solution.py:148
  194.0 24.9 %collective-permute-start.37 = (bf16[2,4,96,256]{3,2,1,0:T(8,128)(2,1)S(1)}, bf16[2,4,96,256]{3,2,1,0:T(8,128)(2,1)S(1)}, u32[]{:S(2)}, u32[]{:S(2)}) collective-permute-start(bf16[2,4,96,256]{3,2,1,0:T(8,128)(2,1)S(1)} %get-tuple-element.123), channel_id=1, source_target_pairs={{0,6},{1,7},{2,4},{3,5},{4,2},{5,3},{6,0},{7,1},{8,14},{9,15},{10,... | collective-permute-start | bytes 1179656 | tf_op jit(solution)/shard_map/ppermute | solution.py:148
  204.5 48.4 %collective-permute-start.25 = (bf16[2,8,96,256]{3,2,1,0:T(8,128)(2,1)S(1)}, bf16[2,8,96,256]{3,2,1,0:T(8,128)(2,1)S(1)}, u32[]{:S(2)}, u32[]{:S(2)}) collective-permute-start(bf16[2,8,96,256]{3,2,1,0:T(8,128)(2,1)S(1)} %get-tuple-element.110), channel_id=1, source_target_pairs={{0,1},{1,0},{2,3},{3,2},{4,5},{5,4},{6,7},{7,6},{8,9},{9,8},{10,11... | collective-permute-start | bytes 2359304 | tf_op jit(solution)/shard_map/ppermute | solution.py:148
  206.1 48.4 %collective-permute-start.26 = (bf16[2,8,96,256]{3,2,1,0:T(8,128)(2,1)S(1)}, bf16[2,8,96,256]{3,2,1,0:T(8,128)(2,1)S(1)}, u32[]{:S(2)}, u32[]{:S(2)}) collective-permute-start(bf16[2,8,96,256]{3,2,1,0:T(8,128)(2,1)S(1)} %get-tuple-element.111), channel_id=1, source_target_pairs={{0,2},{1,3},{2,0},{3,1},{4,6},{5,7},{6,4},{7,5},{8,10},{9,11},{10,... | collective-permute-start | bytes 2359304 | tf_op jit(solution)/shard_map/ppermute | solution.py:148
  212.7 42.6 %collective-permute-start.27 = (bf16[2,8,96,256]{3,2,1,0:T(8,128)(2,1)S(1)}, bf16[2,8,96,256]{3,2,1,0:T(8,128)(2,1)S(1)}, u32[]{:S(2)}, u32[]{:S(2)}) collective-permute-start(bf16[2,8,96,256]{3,2,1,0:T(8,128)(2,1)S(1)} %get-tuple-element.112), channel_id=1, source_target_pairs={{0,3},{1,2},{2,1},{3,0},{4,7},{5,6},{6,5},{7,4},{8,11},{9,10},{10,... | collective-permute-start | bytes 2359304 | tf_op jit(solution)/shard_map/ppermute | solution.py:148
  217.7 39.2 %collective-permute-start.28 = (bf16[2,8,96,256]{3,2,1,0:T(8,128)(2,1)S(1)}, bf16[2,8,96,256]{3,2,1,0:T(8,128)(2,1)S(1)}, u32[]{:S(2)}, u32[]{:S(2)}) collective-permute-start(bf16[2,8,96,256]{3,2,1,0:T(8,128)(2,1)S(1)} %get-tuple-element.113), channel_id=1, source_target_pairs={{0,4},{1,5},{2,6},{3,7},{4,0},{5,1},{6,2},{7,3},{8,12},{9,13},{10,... | collective-permute-start | bytes 2359304 | tf_op jit(solution)/shard_map/ppermute | solution.py:148
  219.0 32.0 %collective-permute-start.38 = (bf16[2,4,96,256]{3,2,1,0:T(8,128)(2,1)S(1)}, bf16[2,4,96,256]{3,2,1,0:T(8,128)(2,1)S(1)}, u32[]{:S(2)}, u32[]{:S(2)}) collective-permute-start(bf16[2,4,96,256]{3,2,1,0:T(8,128)(2,1)S(1)} %get-tuple-element.124), channel_id=1, source_target_pairs={{0,7},{1,6},{2,5},{3,4},{4,3},{5,2},{6,1},{7,0},{8,15},{9,14},{10,... | collective-permute-start | bytes 1179656 | tf_op jit(solution)/shard_map/ppermute | solution.py:148
  251.8 52.5 %collective-permute-start.29 = (bf16[2,8,96,256]{3,2,1,0:T(8,128)(2,1)S(1)}, bf16[2,8,96,256]{3,2,1,0:T(8,128)(2,1)S(1)}, u32[]{:S(2)}, u32[]{:S(2)}) collective-permute-start(bf16[2,8,96,256]{3,2,1,0:T(8,128)(2,1)S(1)} %get-tuple-element.114), channel_id=1, source_target_pairs={{0,5},{1,4},{2,7},{3,6},{4,1},{5,0},{6,3},{7,2},{8,13},{9,12},{10,... | collective-permute-start | bytes 2359304 | tf_op jit(solution)/shard_map/ppermute | solution.py:148
  252.9 54.1 %collective-permute-start.30 = (bf16[2,8,96,256]{3,2,1,0:T(8,128)(2,1)S(1)}, bf16[2,8,96,256]{3,2,1,0:T(8,128)(2,1)S(1)}, u32[]{:S(2)}, u32[]{:S(2)}) collective-permute-start(bf16[2,8,96,256]{3,2,1,0:T(8,128)(2,1)S(1)} %get-tuple-element.115), channel_id=1, source_target_pairs={{0,6},{1,7},{2,4},{3,5},{4,2},{5,3},{6,0},{7,1},{8,14},{9,15},{10,... | collective-permute-start | bytes 2359304 | tf_op jit(solution)/shard_map/ppermute | solution.py:148
  254.5 54.2 %collective-permute-start.31 = (bf16[2,8,96,256]{3,2,1,0:T(8,128)(2,1)S(1)}, bf16[2,8,96,256]{3,2,1,0:T(8,128)(2,1)S(1)}, u32[]{:S(2)}, u32[]{:S(2)}) collective-permute-start(bf16[2,8,96,256]{3,2,1,0:T(8,128)(2,1)S(1)} %get-tuple-element.116), channel_id=1, source_target_pairs={{0,7},{1,6},{2,5},{3,4},{4,3},{5,2},{6,1},{7,0},{8,15},{9,14},{10,... | collective-permute-start | bytes 2359304 | tf_op jit(solution)/shard_map/ppermute | solution.py:148
  256.2 53.5 %collective-permute-start.18 = (bf16[2,8,96,256]{3,2,1,0:T(8,128)(2,1)S(1)}, bf16[2,8,96,256]{3,2,1,0:T(8,128)(2,1)S(1)}, u32[]{:S(2)}, u32[]{:S(2)}) collective-permute-start(bf16[2,8,96,256]{3,2,1,0:T(8,128)(2,1)S(1)} %get-tuple-element.102), channel_id=1, source_target_pairs={{0,1},{1,0},{2,3},{3,2},{4,5},{5,4},{6,7},{7,6},{8,9},{9,8},{10,11... | collective-permute-start | bytes 2359304 | tf_op jit(solution)/shard_map/ppermute | solution.py:148
  257.8 54.6 %collective-permute-start.19 = (bf16[2,8,96,256]{3,2,1,0:T(8,128)(2,1)S(1)}, bf16[2,8,96,256]{3,2,1,0:T(8,128)(2,1)S(1)}, u32[]{:S(2)}, u32[]{:S(2)}) collective-permute-start(bf16[2,8,96,256]{3,2,1,0:T(8,128)(2,1)S(1)} %get-tuple-element.103), channel_id=1, source_target_pairs={{0,2},{1,3},{2,0},{3,1},{4,6},{5,7},{6,4},{7,5},{8,10},{9,11},{10,... | collective-permute-start | bytes 2359304 | tf_op jit(solution)/shard_map/ppermute | solution.py:148
  305.2 31.4 %collective-permute-start.20 = (bf16[2,8,96,256]{3,2,1,0:T(8,128)(2,1)}, bf16[2,8,96,256]{3,2,1,0:T(8,128)(2,1)}, u32[]{:S(2)}, u32[]{:S(2)}) collective-permute-start(bf16[2,8,96,256]{3,2,1,0:T(8,128)(2,1)} %get-tuple-element.104), channel_id=1, source_target_pairs={{0,3},{1,2},{2,1},{3,0},{4,7},{5,6},{6,5},{7,4},{8,11},{9,10},{10,... | collective-permute-start | bytes 2359304 | tf_op jit(solution)/shard_map/ppermute | solution.py:148
  307.9 54.4 %collective-permute-start.21 = (bf16[2,8,96,256]{3,2,1,0:T(8,128)(2,1)}, bf16[2,8,96,256]{3,2,1,0:T(8,128)(2,1)}, u32[]{:S(2)}, u32[]{:S(2)}) collective-permute-start(bf16[2,8,96,256]{3,2,1,0:T(8,128)(2,1)} %get-tuple-element.105), channel_id=1, source_target_pairs={{0,4},{1,5},{2,6},{3,7},{4,0},{5,1},{6,2},{7,3},{8,12},{9,13},{10,... | collective-permute-start | bytes 2359304 | tf_op jit(solution)/shard_map/ppermute | solution.py:148
  309.6 66.9 %collective-permute-start.22 = (bf16[2,8,96,256]{3,2,1,0:T(8,128)(2,1)}, bf16[2,8,96,256]{3,2,1,0:T(8,128)(2,1)}, u32[]{:S(2)}, u32[]{:S(2)}) collective-permute-start(bf16[2,8,96,256]{3,2,1,0:T(8,128)(2,1)} %get-tuple-element.106), channel_id=1, source_target_pairs={{0,5},{1,4},{2,7},{3,6},{4,1},{5,0},{6,3},{7,2},{8,13},{9,12},{10,... | collective-permute-start | bytes 2359304 | tf_op jit(solution)/shard_map/ppermute | solution.py:148
  310.6 66.8 %collective-permute-start.23 = (bf16[2,8,96,256]{3,2,1,0:T(8,128)(2,1)}, bf16[2,8,96,256]{3,2,1,0:T(8,128)(2,1)}, u32[]{:S(2)}, u32[]{:S(2)}) collective-permute-start(bf16[2,8,96,256]{3,2,1,0:T(8,128)(2,1)} %get-tuple-element.107), channel_id=1, source_target_pairs={{0,6},{1,7},{2,4},{3,5},{4,2},{5,3},{6,0},{7,1},{8,14},{9,15},{10,... | collective-permute-start | bytes 2359304 | tf_op jit(solution)/shard_map/ppermute | solution.py:148
  313.4 65.6 %collective-permute-start.24 = (bf16[2,8,96,256]{3,2,1,0:T(8,128)(2,1)}, bf16[2,8,96,256]{3,2,1,0:T(8,128)(2,1)}, u32[]{:S(2)}, u32[]{:S(2)}) collective-permute-start(bf16[2,8,96,256]{3,2,1,0:T(8,128)(2,1)} %get-tuple-element.108), channel_id=1, source_target_pairs={{0,7},{1,6},{2,5},{3,4},{4,3},{5,2},{6,1},{7,0},{8,15},{9,14},{10,... | collective-permute-start | bytes 2359304 | tf_op jit(solution)/shard_map/ppermute | solution.py:148
  336.6 65.3 %collective-permute-start.5 = (bf16[2,1,96,256]{3,2,1,0:T(8,128)(2,1)S(1)}, bf16[2,1,96,256]{3,2,1,0:T(8,128)(2,1)S(1)}, u32[]{:S(2)}, u32[]{:S(2)}) collective-permute-start(bf16[2,1,96,256]{3,2,1,0:T(8,128)(2,1)S(1)} %copy-done.112), channel_id=1, source_target_pairs={{0,2},{1,3},{2,0},{3,1},{4,6},{5,7},{6,4},{7,5},{8,10},{9,11},{10,... | collective-permute-start | bytes 294920 | tf_op jit(solution)/shard_map/ppermute | solution.py:148
  362.3 39.6 %collective-permute-start.6 = (bf16[2,1,96,256]{3,2,1,0:T(8,128)(2,1)S(1)}, bf16[2,1,96,256]{3,2,1,0:T(8,128)(2,1)S(1)}, u32[]{:S(2)}, u32[]{:S(2)}) collective-permute-start(bf16[2,1,96,256]{3,2,1,0:T(8,128)(2,1)S(1)} %copy-done.110), channel_id=1, source_target_pairs={{0,3},{1,2},{2,1},{3,0},{4,7},{5,6},{6,5},{7,4},{8,11},{9,10},{10,... | collective-permute-start | bytes 294920 | tf_op jit(solution)/shard_map/ppermute | solution.py:148
  376.5 25.4 %collective-permute-start.7 = (bf16[2,1,96,256]{3,2,1,0:T(8,128)(2,1)S(1)}, bf16[2,1,96,256]{3,2,1,0:T(8,128)(2,1)S(1)}, u32[]{:S(2)}, u32[]{:S(2)}) collective-permute-start(bf16[2,1,96,256]{3,2,1,0:T(8,128)(2,1)S(1)} %copy-done.108), channel_id=1, source_target_pairs={{0,4},{1,5},{2,6},{3,7},{4,0},{5,1},{6,2},{7,3},{8,12},{9,13},{10,... | collective-permute-start | bytes 294920 | tf_op jit(solution)/shard_map/ppermute | solution.py:148
  377.5 24.4 %collective-permute-start.8 = (bf16[2,1,96,256]{3,2,1,0:T(8,128)(2,1)S(1)}, bf16[2,1,96,256]{3,2,1,0:T(8,128)(2,1)S(1)}, u32[]{:S(2)}, u32[]{:S(2)}) collective-permute-start(bf16[2,1,96,256]{3,2,1,0:T(8,128)(2,1)S(1)} %copy-done.106), channel_id=1, source_target_pairs={{0,5},{1,4},{2,7},{3,6},{4,1},{5,0},{6,3},{7,2},{8,13},{9,12},{10,... | collective-permute-start | bytes 294920 | tf_op jit(solution)/shard_map/ppermute | solution.py:148
  379.0 22.9 %collective-permute-start.9 = (bf16[2,1,96,256]{3,2,1,0:T(8,128)(2,1)S(1)}, bf16[2,1,96,256]{3,2,1,0:T(8,128)(2,1)S(1)}, u32[]{:S(2)}, u32[]{:S(2)}) collective-permute-start(bf16[2,1,96,256]{3,2,1,0:T(8,128)(2,1)S(1)} %copy-done.104), channel_id=1, source_target_pairs={{0,6},{1,7},{2,4},{3,5},{4,2},{5,3},{6,0},{7,1},{8,14},{9,15},{10,... | collective-permute-start | bytes 294920 | tf_op jit(solution)/shard_map/ppermute | solution.py:148
  (140 other events, 1042.6 us)

commit v3 on v2

--- a/solution.py
+++ b/solution.py
@@ -18,30 +18,58 @@
     return pl.CostEstimate(flops=flops, bytes_accessed=moved, transcendentals=0)
 
 
-def square_sums(w_gate, w_up, first, count):
+def fetches(sources, first, held, arrived, n):
+    return [
+        pltpu.make_async_copy(source.at[first + n], held.at[n, side], arrived.at[n, side])
+        for side, source in enumerate(sources)
+    ]
+
+
+def square_sums(w_gate, w_up, first, count, halved=False):
     _, rows, cols = w_gate.shape
-    per_step = 2
-
-    def kernel(gate_ref, up_ref, out_ref):
-        step = pl.program_id(0)
-        for n in range(per_step):
-            for side, ref in enumerate((gate_ref, up_ref)):
-                w = ref[n]
-                out_ref[side, pl.ds(step * per_step + n, 1), :] = jnp.sum(w * w, axis=0, keepdims=True)
-
-    weights = pl.BlockSpec((per_step, rows, cols), lambda i: (first // per_step + i, 0, 0))
-    return pl.pallas_call(
-        kernel,
-        grid=(count // per_step,),
-        in_specs=[weights, weights],
-        out_specs=pl.BlockSpec((2, count, cols), lambda i: (0, 0, 0)),
-        out_shape=jax.ShapeDtypeStruct((2, count, cols), jnp.float32),
+    results = 2 if halved else 1
+    height = count // results
+
+    def kernel(*refs):
+        sources, out_refs, (held, arrived) = refs[:2], refs[2:-2], refs[-2:]
+        for n in range(count):
+            for copy in fetches(sources, first, held, arrived, n):
+                copy.start()
+        mine = lax.axis_index("zero") % 2
+        for half in range(results):
+
+            @pl.loop(0, height)
+            def _(n):
+                row = half * height + n
+                for side, copy in enumerate(fetches(sources, first, held, arrived, row)):
+                    copy.wait()
+                    w = held[row, side]
+                    found = jnp.sum(w * w, axis=0, keepdims=True)
+                    if halved:
+
+                        @pl.when(mine == half)
+                        def _():
+                            out_refs[0][side, pl.ds(n, 1), :] = found
+
+                        @pl.when(mine != half)
+                        def _():
+                            out_refs[1][side, pl.ds(n, 1), :] = found
+
+                    else:
+                        out_refs[0][side, pl.ds(n, 1), :] = found
+
+    return pl.pallas_call(
+        kernel,
+        in_specs=[pl.BlockSpec(memory_space=pl.ANY)] * 2,
+        out_specs=[pl.BlockSpec(memory_space=pltpu.VMEM)] * results,
+        out_shape=[jax.ShapeDtypeStruct((2, height, cols), jnp.float32)] * results,
+        scratch_shapes=[pltpu.VMEM((count, 2, rows, cols), jnp.float32), pltpu.SemaphoreType.DMA((count, 2))],
         compiler_params=granted(44),
         cost_estimate=cost(4 * count * rows * cols, 8 * count * rows * cols),
     )(w_gate, w_up)
 
 
-def scaled_pieces(w_gate, w_up, totals, first, count, start, size):
+def scaled_pieces(w_gate, w_up, totals, halved, first, count, start, size):
     _, rows, cols = w_gate.shape
     width = cols // size
 
@@ -50,7 +78,15 @@
         me = lax.axis_index("zero")
         step = pl.program_id(0)
         for side, w_ref in enumerate((gate_ref, up_ref)):
-            total = sum(ref[side, pl.ds(start + step, 1), :] for ref in total_refs)
+            if halved:
+                height = totals[0].shape[1]
+                half = jnp.where(start + step >= height, 1, 0)
+                row = pl.ds(start + step - half * height, 1)
+                total = jnp.where(
+                    half == me % 2, total_refs[0][side, row, :], total_refs[1][side, row, :]
+                )
+            else:
+                total = sum(ref[side, pl.ds(start + step, 1), :] for ref in total_refs)
             inverse = 1.0 / jnp.sqrt(total)
             held[side] = (w_ref[0] * inverse).astype(jnp.bfloat16).T
             for k in range(size):
@@ -153,20 +189,31 @@
     firsts = [sum(sizes[:c]) for c in chunks]
 
     totals, starts = [], [sum(map(sum, groups[:g])) for g in range(len(groups))]
-    for g, group in enumerate(groups):
-        own = square_sums(w_gate, w_up, starts[g], sum(group))
+    last = len(groups) - 1
+    for g, group in enumerate(groups[:last]):
+        (own,) = square_sums(w_gate, w_up, starts[g], sum(group))
         own = own + send(own, 1)
         totals.append([own] + [send(own, k) for k in range(2, size, 2)])
+    own, other = square_sums(w_gate, w_up, starts[last], sum(groups[last]), halved=True)
+    own = own + send(other, 1)
+    k = 2
+    while k < size:
+        own = own + send(own, k)
+        k *= 2
+    totals.append([own, send(own, 1)])
 
     sent, got = [], []
     for c in chunks:
         group = max(g for g in range(len(groups)) if starts[g] <= firsts[c])
         start = firsts[c] - starts[group]
-        sent.append(scaled_pieces(w_gate, w_up, totals[group], firsts[c], sizes[c], start, size))
+        sent.append(scaled_pieces(w_gate, w_up, totals[group], group == last, firsts[c], sizes[c], start, size))
         got.append([sent[c][0]] + [send(sent[c][k], k) for k in range(1, size)])
 
     part = (router_weight * router_gain[:, None]).astype(jnp.bfloat16).T
-    parts = [part] + [send(part, k) for k in range(1, size)]
+    parts = [part, send(part, 1)]
+    for k in range(2, size, 2):
+        parts.append(send(part, k))
+        parts.append(send(parts[k], 1))
     row = joined_rows(parts)
     columns = [row] + [send(row, k, "bank", banks) for k in range(1, banks)]
     serve_router = joined_columns(columns)
@@ -176,8 +223,11 @@
         outputs = assembled(got[c], outputs, firsts[c], experts)
     serve_gate, serve_up = (jnp.swapaxes(x, 1, 2) for x in outputs)
 
+    even = lax.axis_index("zero") % 2 == 0
+    low, high = (jnp.where(even, x, y) for x, y in (totals[last], totals[last][::-1]))
     mine = [
-        lax.dynamic_slice_in_dim(sum(parts), lax.axis_index("zero") * width, width, axis=2) for parts in totals
+        lax.dynamic_slice_in_dim(x, lax.axis_index("zero") * width, width, axis=2)
+        for x in [sum(parts) for parts in totals[:last]] + [low, high]
     ]
     scale = jnp.sqrt(jnp.concatenate(mine, axis=1))
     return (serve_gate, serve_up, scale[0], scale[1], serve_router)

time: 404 us -> 392 us (0.970)
  waiting for transfers between devices: 191 us -> 185 us
    ppermute x78, waiting for transfers between devices: 191 us -> 185 us  [send(): return lax.ppermute(x, axis, xor_pairs(count, k))]
    unnamed x252 -> x256, local copies, waits for them, and re-layouts: 44.5 us -> 46.6 us
  transfers between devices with their start and end apart: 78 -> 78, of which waited for: 24 -> 18; matrix products, arithmetic and copies ran while one was open for 1% -> 1% of each run, Pallas kernels for 20% -> 17%
where the time goes in v3:
time: 392 us; the launch traced here: 391 us
  waiting for transfers between devices  185 us (47%)
  Pallas kernels  80.3 us (20%)
  starting transfers between devices  75.1 us (19%)
  local copies, waits for them, and re-layouts  47.3 us (12%)
    ppermute x78, waiting for transfers between devices, send(): return lax.ppermute(x, axis, xor_pairs(count, k))  185 us
    ppermute x78, starting transfers between devices, send(): return lax.ppermute(x, axis, xor_pairs(count, k))  75.1 us
    unnamed x256, local copies, waits for them, and re-layouts  46.6 us
    pallas_call x8, Pallas kernels, scaled_pieces(): pl.pallas_call(kernel, grid=(count,), in_specs=[weights, weights] + [pl.B...  35.4 us
    pallas_call x8, Pallas kernels, assembled(): pl.pallas_call(kernel, grid=(count,), in_specs=[piece] * size + [pl.Block...  23.2 us
    pallas_call x3, Pallas kernels, square_sums(): pl.pallas_call(kernel, in_specs=[pl.BlockSpec(memory_space=pl.ANY)] * 2,...  18.1 us
  transfers between devices with their start and end apart: 78, of which 18 were waited for; matrix products, arithmetic and copies ran while one was open for 1% of the time, Pallas kernels for 17%

profile of v3, /device:TPU:0, one launch (start us, length us, event | category | flops | bytes accessed | tf_op | source)
XLA Modules:
  0.0 390.8 jit_solution(2399840511942352070)
XLA Ops:
  0.7 12.3 %shard_map.83 = (f32[2,12,768]{2,1,0:T(8,128)S(1)}, f32[2,12,768]{2,1,0:T(8,128)S(1)}) custom-call(f32[32,256,768]{2,1,0:T(8,128)} %gate_ref.15, f32[32,256,768]{2,1,0:T(8,128)} %up_ref.15), custom_call_target="tpu_custom_call" | custom-call | flops 18874368 | bytes 37748736 | tf_op jit(solution)/shard_map/pallas_call | solution.py:61
  13.6 2.6 collective-permute-start.69
  16.1 1.9 shard_map.92
  18.4 3.9 shard_map.89
  22.6 1.5 collective-permute-start.71
  24.2 2.1 collective-permute-done.71.refs_4_
  26.3 2.4 collective-permute-done.73.refs_6_
  29.9 1.6 collective-permute-start.40
  32.0 1.5 collective-permute-start.59
  33.6 1.5 shard_map.102.refs_0_
  35.1 1.6 collective-permute-start.75
  37.2 2.4 collective-permute-start.42
  39.7 1.6 collective-permute-done.60.refs_3_
  41.9 2.3 shard_map.93
  44.8 1.6 collective-permute-start.62
  46.4 2.6 collective-permute-start.76
  49.4 9.2 %collective-permute-done.76.refs_2_ = bf16[32,2048]{1,0:T(8,128)(2,1)S(1)} collective-permute-done((bf16[32,2048]{1,0:T(8,128)(2,1)S(1)}, bf16[32,2048]{1,0:T(8,128)(2,1)S(1)}, u32[]{:S(2)}, u32[]{:S(2)}) %collective-permute-start.76) | collective-permute-done | bytes 131104 | tf_op jit(solution)/shard_map/ppermute | solution.py:184
  58.6 1.3 collective-permute-start.64
  62.0 2.4 collective-permute-start.67
  64.4 2.3 shard_map.91
  67.5 7.3 %collective-permute-done.64.refs_4_ = bf16[2,2,96,256]{3,2,1,0:T(8,128)(2,1)S(1)} collective-permute-done((bf16[2,2,96,256]{3,2,1,0:T(8,128)(2,1)S(1)}, bf16[2,2,96,256]{3,2,1,0:T(8,128)(2,1)S(1)}, u32[]{:S(2)}, u32[]{:S(2)}) %collective-permute-start.64) | collective-permute-done | bytes 196640 | tf_op jit(solution)/shard_map/ppermute | solution.py:184
  78.8 2.8 collective-permute-start.52
  83.2 1.7 collective-permute-start.55
  85.6 2.4 collective-permute-start.56
  88.0 4.2 %shard_map.90 = (bf16[2,4,96,256]{3,2,1,0:T(8,128)(2,1)S(1)}, bf16[2,4,96,256]{3,2,1,0:T(8,128)(2,1)S(1)}, bf16[2,4,96,256]{3,2,1,0:T(8,128)(2,1)S(1)}, bf16[2,4...) custom-call(f32[32,256,768]{2,1,0:T(8,128)} %gate_ref.15, ...), custom_call_target="tpu_custom_call" | custom-call | flops 3145728 | bytes 9437184 | tf_op jit(solution)/shard_map/pallas_call | solution.py:98
  93.7 1.2 collective-permute-start.44
  94.9 4.8 %collective-permute-done.54.refs_5_ = bf16[2,2,96,256]{3,2,1,0:T(8,128)(2,1)S(1)} collective-permute-done((bf16[2,2,96,256]{3,2,1,0:T(8,128)(2,1)S(1)}, bf16[2,2,96,256]{3,2,1,0:T(8,128)(2,1)S(1)}, u32[]{:S(2)}, u32[]{:S(2)}) %collective-permute-start.54) | collective-permute-done | bytes 196640 | tf_op jit(solution)/shard_map/ppermute | solution.py:184
  103.9 1.7 shard_map.84
  111.2 6.0 %collective-permute-done.10.refs_7_ = bf16[2,1,96,256]{3,2,1,0:T(8,128)(2,1)S(1)} collective-permute-done((bf16[2,1,96,256]{3,2,1,0:T(8,128)(2,1)S(1)}, bf16[2,1,96,256]{3,2,1,0:T(8,128)(2,1)S(1)}, u32[]{:S(2)}, u32[]{:S(2)}) %collective-permute-start.10) | collective-permute-done | bytes 98336 | tf_op jit(solution)/shard_map/ppermute | solution.py:184
  121.8 1.6 collective-permute-start.49
  123.4 3.6 shard_map.85
  128.7 19.0 %collective-permute-done.47.refs_5_ = bf16[2,4,96,256]{3,2,1,0:T(8,128)(2,1)S(1)} collective-permute-done((bf16[2,4,96,256]{3,2,1,0:T(8,128)(2,1)S(1)}, bf16[2,4,96,256]{3,2,1,0:T(8,128)(2,1)S(1)}, u32[]{:S(2)}, u32[]{:S(2)}) %collective-permute-start.47) | collective-permute-done | bytes 393248 | tf_op jit(solution)/shard_map/ppermute | solution.py:184
  150.6 2.0 collective-permute-start.16
  153.3 4.1 %shard_map.88 = (bf16[2,4,96,256]{3,2,1,0:T(8,128)(2,1)S(1)}, bf16[2,4,96,256]{3,2,1,0:T(8,128)(2,1)S(1)}, bf16[2,4,96,256]{3,2,1,0:T(8,128)(2,1)S(1)}, bf16[2,4...) custom-call(f32[32,256,768]{2,1,0:T(8,128)} %gate_ref.15, ...), custom_call_target="tpu_custom_call" | custom-call | flops 3145728 | bytes 9437184 | tf_op jit(solution)/shard_map/pallas_call | solution.py:98
  158.6 12.1 %collective-permute-done.14.refs_4_ = bf16[2,3,96,256]{3,2,1,0:T(8,128)(2,1)S(1)} collective-permute-done((bf16[2,3,96,256]{3,2,1,0:T(8,128)(2,1)S(1)}, bf16[2,3,96,256]{3,2,1,0:T(8,128)(2,1)S(1)}, u32[]{:S(2)}, u32[]{:S(2)}) %collective-permute-start.14) | collective-permute-done | bytes 294944 | tf_op jit(solution)/shard_map/ppermute | solution.py:184
  171.4 1.4 collective-permute-start.33
  172.8 2.9 collective-permute-done.15.refs_5_
  176.5 1.7 collective-permute-start.34
  178.9 1.3 collective-permute-start.35
  182.8 7.9 %shard_map.87 = (bf16[2,8,96,256]{3,2,1,0:T(8,128)(2,1)S(1)}, bf16[2,8,96,256]{3,2,1,0:T(8,128)(2,1)S(1)}, bf16[2,8,96,256]{3,2,1,0:T(8,128)(2,1)S(1)}, bf16[2,8...) custom-call(f32[32,256,768]{2,1,0:T(8,128)} %gate_ref.15, ...), custom_call_target="tpu_custom_call" | custom-call | flops 6291456 | bytes 18874368 | tf_op jit(solution)/shard_map/pallas_call | solution.py:98
  192.9 1.5 collective-permute-start.26
  194.4 4.6 %collective-permute-done.35.refs_4_ = bf16[2,4,96,256]{3,2,1,0:T(8,128)(2,1)S(1)} collective-permute-done((bf16[2,4,96,256]{3,2,1,0:T(8,128)(2,1)S(1)}, bf16[2,4,96,256]{3,2,1,0:T(8,128)(2,1)S(1)}, u32[]{:S(2)}, u32[]{:S(2)}) %collective-permute-start.35) | collective-permute-done | bytes 393248 | tf_op jit(solution)/shard_map/ppermute | solution.py:184
  199.8 5.6 %collective-permute-done.36.refs_5_ = bf16[2,4,96,256]{3,2,1,0:T(8,128)(2,1)S(1)} collective-permute-done((bf16[2,4,96,256]{3,2,1,0:T(8,128)(2,1)S(1)}, bf16[2,4,96,256]{3,2,1,0:T(8,128)(2,1)S(1)}, u32[]{:S(2)}, u32[]{:S(2)}) %collective-permute-start.36) | collective-permute-done | bytes 393248 | tf_op jit(solution)/shard_map/ppermute | solution.py:184
  206.1 1.3 collective-permute-start.28
  207.4 1.5 collective-permute-start.38
  208.9 9.4 %shard_map.86 = (bf16[2,8,96,256]{3,2,1,0:T(8,128)(2,1)S(1)}, bf16[2,8,96,256]{3,2,1,0:T(8,128)(2,1)S(1)}, bf16[2,8,96,256]{3,2,1,0:T(8,128)(2,1)S(1)}, bf16[2,8...) custom-call(f32[32,256,768]{2,1,0:T(8,128)} %gate_ref.15, ...), custom_call_target="tpu_custom_call" | custom-call | flops 6291456 | bytes 18874368 | tf_op jit(solution)/shard_map/pallas_call | solution.py:98
  219.1 20.0 %collective-permute-done.38.refs_7_ = bf16[2,4,96,256]{3,2,1,0:T(8,128)(2,1)S(1)} collective-permute-done((bf16[2,4,96,256]{3,2,1,0:T(8,128)(2,1)S(1)}, bf16[2,4,96,256]{3,2,1,0:T(8,128)(2,1)S(1)}, u32[]{:S(2)}, u32[]{:S(2)}) %collective-permute-start.38) | collective-permute-done | bytes 393248 | tf_op jit(solution)/shard_map/ppermute | solution.py:184
  240.1 3.7 collective-permute-start.30
  245.9 46.2 %collective-permute-done.29.refs_5_ = bf16[2,8,96,256]{3,2,1,0:T(8,128)(2,1)S(1)} collective-permute-done((bf16[2,8,96,256]{3,2,1,0:T(8,128)(2,1)S(1)}, bf16[2,8,96,256]{3,2,1,0:T(8,128)(2,1)S(1)}, u32[]{:S(2)}, u32[]{:S(2)}) %collective-permute-start.29) | collective-permute-done | bytes 786464 | tf_op jit(solution)/shard_map/ppermute | solution.py:184
  293.0 2.4 collective-permute-start.20
  298.8 2.0 collective-permute-start.23
  301.7 1.8 collective-permute-start.24
  304.9 2.1 shard_map.103
  314.5 1.4 shard_map.94
  323.4 1.4 shard_map.95
  325.7 25.1 %collective-permute-done.21.refs_4_ = bf16[2,8,96,256]{3,2,1,0:T(8,128)(2,1)} collective-permute-done((bf16[2,8,96,256]{3,2,1,0:T(8,128)(2,1)}, bf16[2,8,96,256]{3,2,1,0:T(8,128)(2,1)}, u32[]{:S(2)}, u32[]{:S(2)}) %collective-permute-start.21) | collective-permute-done | bytes 786464 | tf_op jit(solution)/shard_map/ppermute | solution.py:184
  350.8 14.3 %collective-permute-done.22.refs_5_ = bf16[2,8,96,256]{3,2,1,0:T(8,128)(2,1)} collective-permute-done((bf16[2,8,96,256]{3,2,1,0:T(8,128)(2,1)}, bf16[2,8,96,256]{3,2,1,0:T(8,128)(2,1)}, u32[]{:S(2)}, u32[]{:S(2)}) %collective-permute-start.22) | collective-permute-done | bytes 786464 | tf_op jit(solution)/shard_map/ppermute | solution.py:184
  365.1 2.5 collective-permute-start.7
  367.7 1.5 collective-permute-start.9
  369.9 2.5 shard_map.96
  372.5 2.5 shard_map.97
  375.1 4.5 %shard_map.98 = (bf16[32,96,2048]{2,1,0:T(8,128)(2,1)}, bf16[32,96,2048]{2,1,0:T(8,128)(2,1)}) custom-call(bf16[2,8,96,256]{3,2,1,0:T(8,128)(2,1)S(1)} %get-tuple-element.113.refs_0_, bf16[2,8,96,256]{3,2,1,0:T(8,128)(2,1)S(1)} %collective-permute-done.25.refs_1_, ...), custom_call_target="tpu_custom_call", output_to_operand_aliasing={{0}: (8, {}), {1}: (9, {})} | custom-call | flops 1572864 | bytes 12582912 | tf_op jit(solution)/shard_map/pallas_call | solution.py:125
  379.7 7.7 %shard_map.99 = (bf16[32,96,2048]{2,1,0:T(8,128)(2,1)}, bf16[32,96,2048]{2,1,0:T(8,128)(2,1)}) custom-call(bf16[2,8,96,256]{3,2,1,0:T(8,128)(2,1)S(1)} %copy-done.3, bf16[2,8,96,256]{3,2,1,0:T(8,128)(2,1)S(1)} %copy-done.9, bf16[2,8,96,256]{3,2,1,0:T(8,128)(2,1)S(1)} %copy-done.13, ...), custom_call_target="tpu_custom_call", output_to_operand_aliasing={{0}: (8, {}), {1}: (9, {})} | custom-call | flops 1572864 | bytes 12582912 | tf_op jit(solution)/shard_map/pallas_call | solution.py:125
  387.6 2.1 shard_map.100
  (380 shorter events, 73.2 us)
Async XLA Ops:
  13.0 24.3 %collective-permute-start = (f32[2,12,768]{2,1,0:T(8,128)S(1)}, f32[2,12,768]{2,1,0:T(8,128)S(1)}, u32[]{:S(2)}, u32[]{:S(2)}) collective-permute-start(f32[2,12,768]{2,1,0:T(8,128)S(1)} %get-tuple-element.88), channel_id=1, source_target_pairs={{0,1},{1,0},{2,3},{3,2},{4,5},{5,4},{6,7},{7,6},{8,9},{9,8},{10,11... | collective-permute-start | bytes 221192 | tf_op jit(solution)/shard_map/ppermute | solution.py:184
  13.6 10.6 %collective-permute-start.69 = (bf16[32,256]{1,0:T(8,128)(2,1)S(1)}, bf16[32,256]{1,0:T(8,128)(2,1)S(1)}, u32[]{:S(2)}, u32[]{:S(2)}) collective-permute-start(bf16[32,256]{1,0:T(8,128)(2,1)S(1)} %fusion.refs_0_), channel_id=1, source_target_pairs={{0,2},{1,3},{2,0},{3,1},{4,6},{5,7},{6,4},{7,5},{8,10},{9,11},{10,... | collective-permute-start | bytes 49160 | tf_op jit(solution)/shard_map/ppermute | solution.py:184
  29.9 14.9 %collective-permute-start.40 = (f32[2,6,768]{2,1,0:T(8,128)S(1)}, f32[2,6,768]{2,1,0:T(8,128)S(1)}, u32[]{:S(2)}, u32[]{:S(2)}) collective-permute-start(f32[2,6,768]{2,1,0:T(8,128)S(1)} %add.46.refs_0_), channel_id=1, source_target_pairs={{0,2},{1,3},{2,0},{3,1},{4,6},{5,7},{6,4},{7,5},{8,10},{9,11},{10,... | collective-permute-start | bytes 110600 | tf_op jit(solution)/shard_map/ppermute | solution.py:184
  31.5 13.3 %collective-permute-start.41 = (f32[2,6,768]{2,1,0:T(8,128)S(1)}, f32[2,6,768]{2,1,0:T(8,128)S(1)}, u32[]{:S(2)}, u32[]{:S(2)}) collective-permute-start(f32[2,6,768]{2,1,0:T(8,128)S(1)} %add.46.refs_0_), channel_id=1, source_target_pairs={{0,4},{1,5},{2,6},{3,7},{4,0},{5,1},{6,2},{7,3},{8,12},{9,13},{10,... | collective-permute-start | bytes 110600 | tf_op jit(solution)/shard_map/ppermute | solution.py:184
  35.1 14.3 %collective-permute-start.75 = (bf16[32,2048]{1,0:T(8,128)(2,1)}, bf16[32,2048]{1,0:T(8,128)(2,1)S(1)}, u32[]{:S(2)}, u32[]{:S(2)}) collective-permute-start(bf16[32,2048]{1,0:T(8,128)(2,1)} %shard_map.102.refs_0_), channel_id=1, source_target_pairs={{0,8},{8,0},{16,24},{24,16},{1,9},{9,1},{17,25},{25,17},{2,10},{10... | collective-permute-start | bytes 393224 | tf_op jit(solution)/shard_map/ppermute | solution.py:184
  37.2 9.2 %collective-permute-start.42 = (f32[2,6,768]{2,1,0:T(8,128)S(1)}, f32[2,6,768]{2,1,0:T(8,128)S(1)}, u32[]{:S(2)}, u32[]{:S(2)}) collective-permute-start(f32[2,6,768]{2,1,0:T(8,128)S(1)} %add.46.refs_0_), channel_id=1, source_target_pairs={{0,6},{1,7},{2,4},{3,5},{4,2},{5,3},{6,0},{7,1},{8,14},{9,15},{10,... | collective-permute-start | bytes 110600 | tf_op jit(solution)/shard_map/ppermute | solution.py:184
  41.3 7.7 %collective-permute-start.1 = (f32[2,12,768]{2,1,0:T(8,128)S(1)}, f32[2,12,768]{2,1,0:T(8,128)S(1)}, u32[]{:S(2)}, u32[]{:S(2)}) collective-permute-start(f32[2,12,768]{2,1,0:T(8,128)S(1)} %add.43), channel_id=1, source_target_pairs={{0,2},{1,3},{2,0},{3,1},{4,6},{5,7},{6,4},{7,5},{8,10},{9,11},{10,... | collective-permute-start | bytes 221192 | tf_op jit(solution)/shard_map/ppermute | solution.py:184
  44.8 15.0 %collective-permute-start.61 = (bf16[2,2,96,256]{3,2,1,0:T(8,128)(2,1)S(1)}, bf16[2,2,96,256]{3,2,1,0:T(8,128)(2,1)S(1)}, u32[]{:S(2)}, u32[]{:S(2)}) collective-permute-start(bf16[2,2,96,256]{3,2,1,0:T(8,128)(2,1)S(1)} %get-tuple-element.146), channel_id=1, source_target_pairs={{0,1},{1,0},{2,3},{3,2},{4,5},{5,4},{6,7},{7,6},{8,9},{9,8},{10,11... | collective-permute-start | bytes 589832 | tf_op jit(solution)/shard_map/ppermute | solution.py:184
  44.8 16.5 %collective-permute-start.62 = (bf16[2,2,96,256]{3,2,1,0:T(8,128)(2,1)S(1)}, bf16[2,2,96,256]{3,2,1,0:T(8,128)(2,1)S(1)}, u32[]{:S(2)}, u32[]{:S(2)}) collective-permute-start(bf16[2,2,96,256]{3,2,1,0:T(8,128)(2,1)S(1)} %get-tuple-element.147), channel_id=1, source_target_pairs={{0,2},{1,3},{2,0},{3,1},{4,6},{5,7},{6,4},{7,5},{8,10},{9,11},{10,... | collective-permute-start | bytes 589832 | tf_op jit(solution)/shard_map/ppermute | solution.py:184
  46.4 12.2 %collective-permute-start.76 = (bf16[32,2048]{1,0:T(8,128)(2,1)S(1)}, bf16[32,2048]{1,0:T(8,128)(2,1)S(1)}, u32[]{:S(2)}, u32[]{:S(2)}) collective-permute-start(bf16[32,2048]{1,0:T(8,128)(2,1)S(1)} %copy-done.113), channel_id=1, source_target_pairs={{0,16},{8,24},{16,0},{24,8},{1,17},{9,25},{17,1},{25,9},{2,18},{10... | collective-permute-start | bytes 393224 | tf_op jit(solution)/shard_map/ppermute | solution.py:184
  49.0 10.9 %collective-permute-start.77 = (bf16[32,2048]{1,0:T(8,128)(2,1)S(1)}, bf16[32,2048]{1,0:T(8,128)(2,1)S(1)}, u32[]{:S(2)}, u32[]{:S(2)}) collective-permute-start(bf16[32,2048]{1,0:T(8,128)(2,1)S(1)} %copy-done.113), channel_id=1, source_target_pairs={{0,24},{8,16},{16,8},{24,0},{1,25},{9,17},{17,9},{25,1},{2,26},{10... | collective-permute-start | bytes 393224 | tf_op jit(solution)/shard_map/ppermute | solution.py:184
  49.4 17.4 %collective-permute-start.63 = (bf16[2,2,96,256]{3,2,1,0:T(8,128)(2,1)S(1)}, bf16[2,2,96,256]{3,2,1,0:T(8,128)(2,1)S(1)}, u32[]{:S(2)}, u32[]{:S(2)}) collective-permute-start(bf16[2,2,96,256]{3,2,1,0:T(8,128)(2,1)S(1)} %get-tuple-element.148), channel_id=1, source_target_pairs={{0,3},{1,2},{2,1},{3,0},{4,7},{5,6},{6,5},{7,4},{8,11},{9,10},{10,... | collective-permute-start | bytes 589832 | tf_op jit(solution)/shard_map/ppermute | solution.py:184
  58.6 16.2 %collective-permute-start.64 = (bf16[2,2,96,256]{3,2,1,0:T(8,128)(2,1)S(1)}, bf16[2,2,96,256]{3,2,1,0:T(8,128)(2,1)S(1)}, u32[]{:S(2)}, u32[]{:S(2)}) collective-permute-start(bf16[2,2,96,256]{3,2,1,0:T(8,128)(2,1)S(1)} %get-tuple-element.149), channel_id=1, source_target_pairs={{0,4},{1,5},{2,6},{3,7},{4,0},{5,1},{6,2},{7,3},{8,12},{9,13},{10,... | collective-permute-start | bytes 589832 | tf_op jit(solution)/shard_map/ppermute | solution.py:184
  59.9 17.0 %collective-permute-start.65 = (bf16[2,2,96,256]{3,2,1,0:T(8,128)(2,1)S(1)}, bf16[2,2,96,256]{3,2,1,0:T(8,128)(2,1)S(1)}, u32[]{:S(2)}, u32[]{:S(2)}) collective-permute-start(bf16[2,2,96,256]{3,2,1,0:T(8,128)(2,1)S(1)} %get-tuple-element.150), channel_id=1, source_target_pairs={{0,5},{1,4},{2,7},{3,6},{4,1},{5,0},{6,3},{7,2},{8,13},{9,12},{10,... | collective-permute-start | bytes 589832 | tf_op jit(solution)/shard_map/ppermute | solution.py:184
  60.6 17.5 %collective-permute-start.66 = (bf16[2,2,96,256]{3,2,1,0:T(8,128)(2,1)S(1)}, bf16[2,2,96,256]{3,2,1,0:T(8,128)(2,1)S(1)}, u32[]{:S(2)}, u32[]{:S(2)}) collective-permute-start(bf16[2,2,96,256]{3,2,1,0:T(8,128)(2,1)S(1)} %get-tuple-element.151), channel_id=1, source_target_pairs={{0,6},{1,7},{2,4},{3,5},{4,2},{5,3},{6,0},{7,1},{8,14},{9,15},{10,... | collective-permute-start | bytes 589832 | tf_op jit(solution)/shard_map/ppermute | solution.py:184
  62.0 19.5 %collective-permute-start.67 = (bf16[2,2,96,256]{3,2,1,0:T(8,128)(2,1)S(1)}, bf16[2,2,96,256]{3,2,1,0:T(8,128)(2,1)S(1)}, u32[]{:S(2)}, u32[]{:S(2)}) collective-permute-start(bf16[2,2,96,256]{3,2,1,0:T(8,128)(2,1)S(1)} %get-tuple-element.152), channel_id=1, source_target_pairs={{0,7},{1,6},{2,5},{3,4},{4,3},{5,2},{6,1},{7,0},{8,15},{9,14},{10,... | collective-permute-start | bytes 589832 | tf_op jit(solution)/shard_map/ppermute | solution.py:184
  67.5 15.0 %collective-permute-start.50 = (bf16[2,2,96,256]{3,2,1,0:T(8,128)(2,1)S(1)}, bf16[2,2,96,256]{3,2,1,0:T(8,128)(2,1)S(1)}, u32[]{:S(2)}, u32[]{:S(2)}) collective-permute-start(bf16[2,2,96,256]{3,2,1,0:T(8,128)(2,1)S(1)} %get-tuple-element.138), channel_id=1, source_target_pairs={{0,1},{1,0},{2,3},{3,2},{4,5},{5,4},{6,7},{7,6},{8,9},{9,8},{10,11... | collective-permute-start | bytes 589832 | tf_op jit(solution)/shard_map/ppermute | solution.py:184
  77.5 7.4 %collective-permute-start.51 = (bf16[2,2,96,256]{3,2,1,0:T(8,128)(2,1)S(1)}, bf16[2,2,96,256]{3,2,1,0:T(8,128)(2,1)S(1)}, u32[]{:S(2)}, u32[]{:S(2)}) collective-permute-start(bf16[2,2,96,256]{3,2,1,0:T(8,128)(2,1)S(1)} %get-tuple-element.139), channel_id=1, source_target_pairs={{0,2},{1,3},{2,0},{3,1},{4,6},{5,7},{6,4},{7,5},{8,10},{9,11},{10,... | collective-permute-start | bytes 589832 | tf_op jit(solution)/shard_map/ppermute | solution.py:184
  78.8 14.2 %collective-permute-start.52 = (bf16[2,2,96,256]{3,2,1,0:T(8,128)(2,1)S(1)}, bf16[2,2,96,256]{3,2,1,0:T(8,128)(2,1)S(1)}, u32[]{:S(2)}, u32[]{:S(2)}) collective-permute-start(bf16[2,2,96,256]{3,2,1,0:T(8,128)(2,1)S(1)} %get-tuple-element.140), channel_id=1, source_target_pairs={{0,3},{1,2},{2,1},{3,0},{4,7},{5,6},{6,5},{7,4},{8,11},{9,10},{10,... | collective-permute-start | bytes 589832 | tf_op jit(solution)/shard_map/ppermute | solution.py:184
  82.2 10.7 %collective-permute-start.53 = (bf16[2,2,96,256]{3,2,1,0:T(8,128)(2,1)S(1)}, bf16[2,2,96,256]{3,2,1,0:T(8,128)(2,1)S(1)}, u32[]{:S(2)}, u32[]{:S(2)}) collective-permute-start(bf16[2,2,96,256]{3,2,1,0:T(8,128)(2,1)S(1)} %get-tuple-element.141), channel_id=1, source_target_pairs={{0,4},{1,5},{2,6},{3,7},{4,0},{5,1},{6,2},{7,3},{8,12},{9,13},{10,... | collective-permute-start | bytes 589832 | tf_op jit(solution)/shard_map/ppermute | solution.py:184
  82.5 17.2 %collective-permute-start.54 = (bf16[2,2,96,256]{3,2,1,0:T(8,128)(2,1)S(1)}, bf16[2,2,96,256]{3,2,1,0:T(8,128)(2,1)S(1)}, u32[]{:S(2)}, u32[]{:S(2)}) collective-permute-start(bf16[2,2,96,256]{3,2,1,0:T(8,128)(2,1)S(1)} %get-tuple-element.142), channel_id=1, source_target_pairs={{0,5},{1,4},{2,7},{3,6},{4,1},{5,0},{6,3},{7,2},{8,13},{9,12},{10,... | collective-permute-start | bytes 589832 | tf_op jit(solution)/shard_map/ppermute | solution.py:184
  83.2 18.2 %collective-permute-start.55 = (bf16[2,2,96,256]{3,2,1,0:T(8,128)(2,1)S(1)}, bf16[2,2,96,256]{3,2,1,0:T(8,128)(2,1)S(1)}, u32[]{:S(2)}, u32[]{:S(2)}) collective-permute-start(bf16[2,2,96,256]{3,2,1,0:T(8,128)(2,1)S(1)} %get-tuple-element.143), channel_id=1, source_target_pairs={{0,6},{1,7},{2,4},{3,5},{4,2},{5,3},{6,0},{7,1},{8,14},{9,15},{10,... | collective-permute-start | bytes 589832 | tf_op jit(solution)/shard_map/ppermute | solution.py:184
  85.6 23.9 %collective-permute-start.56 = (bf16[2,2,96,256]{3,2,1,0:T(8,128)(2,1)S(1)}, bf16[2,2,96,256]{3,2,1,0:T(8,128)(2,1)S(1)}, u32[]{:S(2)}, u32[]{:S(2)}) collective-permute-start(bf16[2,2,96,256]{3,2,1,0:T(8,128)(2,1)S(1)} %get-tuple-element.144), channel_id=1, source_target_pairs={{0,7},{1,6},{2,5},{3,4},{4,3},{5,2},{6,1},{7,0},{8,15},{9,14},{10,... | collective-permute-start | bytes 589832 | tf_op jit(solution)/shard_map/ppermute | solution.py:184
  92.9 27.8 %collective-permute-start.43 = (bf16[2,4,96,256]{3,2,1,0:T(8,128)(2,1)S(1)}, bf16[2,4,96,256]{3,2,1,0:T(8,128)(2,1)S(1)}, u32[]{:S(2)}, u32[]{:S(2)}) collective-permute-start(bf16[2,4,96,256]{3,2,1,0:T(8,128)(2,1)S(1)} %get-tuple-element.130), channel_id=1, source_target_pairs={{0,1},{1,0},{2,3},{3,2},{4,5},{5,4},{6,7},{7,6},{8,9},{9,8},{10,11... | collective-permute-start | bytes 1179656 | tf_op jit(solution)/shard_map/ppermute | solution.py:184
  93.7 28.1 %collective-permute-start.44 = (bf16[2,4,96,256]{3,2,1,0:T(8,128)(2,1)S(1)}, bf16[2,4,96,256]{3,2,1,0:T(8,128)(2,1)S(1)}, u32[]{:S(2)}, u32[]{:S(2)}) collective-permute-start(bf16[2,4,96,256]{3,2,1,0:T(8,128)(2,1)S(1)} %get-tuple-element.131), channel_id=1, source_target_pairs={{0,2},{1,3},{2,0},{3,1},{4,6},{5,7},{6,4},{7,5},{8,10},{9,11},{10,... | collective-permute-start | bytes 1179656 | tf_op jit(solution)/shard_map/ppermute | solution.py:184
  102.0 25.7 %collective-permute-start.45 = (bf16[2,4,96,256]{3,2,1,0:T(8,128)(2,1)S(1)}, bf16[2,4,96,256]{3,2,1,0:T(8,128)(2,1)S(1)}, u32[]{:S(2)}, u32[]{:S(2)}) collective-permute-start(bf16[2,4,96,256]{3,2,1,0:T(8,128)(2,1)S(1)} %get-tuple-element.132), channel_id=1, source_target_pairs={{0,3},{1,2},{2,1},{3,0},{4,7},{5,6},{6,5},{7,4},{8,11},{9,10},{10,... | collective-permute-start | bytes 1179656 | tf_op jit(solution)/shard_map/ppermute | solution.py:184
  103.1 25.0 %collective-permute-start.46 = (bf16[2,4,96,256]{3,2,1,0:T(8,128)(2,1)S(1)}, bf16[2,4,96,256]{3,2,1,0:T(8,128)(2,1)S(1)}, u32[]{:S(2)}, u32[]{:S(2)}) collective-permute-start(bf16[2,4,96,256]{3,2,1,0:T(8,128)(2,1)S(1)} %get-tuple-element.133), channel_id=1, source_target_pairs={{0,4},{1,5},{2,6},{3,7},{4,0},{5,1},{6,2},{7,3},{8,12},{9,13},{10,... | collective-permute-start | bytes 1179656 | tf_op jit(solution)/shard_map/ppermute | solution.py:184
  110.1 7.1 %collective-permute-start.10 = (bf16[2,1,96,256]{3,2,1,0:T(8,128)(2,1)S(1)}, bf16[2,1,96,256]{3,2,1,0:T(8,128)(2,1)S(1)}, u32[]{:S(2)}, u32[]{:S(2)}) collective-permute-start(bf16[2,1,96,256]{3,2,1,0:T(8,128)(2,1)S(1)} %get-tuple-element.96), channel_id=1, source_target_pairs={{0,7},{1,6},{2,5},{3,4},{4,3},{5,2},{6,1},{7,0},{8,15},{9,14},{10,... | collective-permute-start | bytes 294920 | tf_op jit(solution)/shard_map/ppermute | solution.py:184
  119.8 27.8 %collective-permute-start.47 = (bf16[2,4,96,256]{3,2,1,0:T(8,128)(2,1)S(1)}, bf16[2,4,96,256]{3,2,1,0:T(8,128)(2,1)S(1)}, u32[]{:S(2)}, u32[]{:S(2)}) collective-permute-start(bf16[2,4,96,256]{3,2,1,0:T(8,128)(2,1)S(1)} %get-tuple-element.134), channel_id=1, source_target_pairs={{0,5},{1,4},{2,7},{3,6},{4,1},{5,0},{6,3},{7,2},{8,13},{9,12},{10,... | collective-permute-start | bytes 1179656 | tf_op jit(solution)/shard_map/ppermute | solution.py:184
  120.8 27.4 %collective-permute-start.48 = (bf16[2,4,96,256]{3,2,1,0:T(8,128)(2,1)S(1)}, bf16[2,4,96,256]{3,2,1,0:T(8,128)(2,1)S(1)}, u32[]{:S(2)}, u32[]{:S(2)}) collective-permute-start(bf16[2,4,96,256]{3,2,1,0:T(8,128)(2,1)S(1)} %get-tuple-element.135), channel_id=1, source_target_pairs={{0,6},{1,7},{2,4},{3,5},{4,2},{5,3},{6,0},{7,1},{8,14},{9,15},{10,... | collective-permute-start | bytes 1179656 | tf_op jit(solution)/shard_map/ppermute | solution.py:184
  121.8 27.5 %collective-permute-start.49 = (bf16[2,4,96,256]{3,2,1,0:T(8,128)(2,1)S(1)}, bf16[2,4,96,256]{3,2,1,0:T(8,128)(2,1)S(1)}, u32[]{:S(2)}, u32[]{:S(2)}) collective-permute-start(bf16[2,4,96,256]{3,2,1,0:T(8,128)(2,1)S(1)} %get-tuple-element.136), channel_id=1, source_target_pairs={{0,7},{1,6},{2,5},{3,4},{4,3},{5,2},{6,1},{7,0},{8,15},{9,14},{10,... | collective-permute-start | bytes 1179656 | tf_op jit(solution)/shard_map/ppermute | solution.py:184
  127.7 22.1 %collective-permute-start.11 = (bf16[2,3,96,256]{3,2,1,0:T(8,128)(2,1)S(1)}, bf16[2,3,96,256]{3,2,1,0:T(8,128)(2,1)S(1)}, u32[]{:S(2)}, u32[]{:S(2)}) collective-permute-start(bf16[2,3,96,256]{3,2,1,0:T(8,128)(2,1)S(1)} %get-tuple-element.98), channel_id=1, source_target_pairs={{0,1},{1,0},{2,3},{3,2},{4,5},{5,4},{6,7},{7,6},{8,9},{9,8},{10,11... | collective-permute-start | bytes 884744 | tf_op jit(solution)/shard_map/ppermute | solution.py:184
  128.2 24.5 %collective-permute-start.12 = (bf16[2,3,96,256]{3,2,1,0:T(8,128)(2,1)S(1)}, bf16[2,3,96,256]{3,2,1,0:T(8,128)(2,1)S(1)}, u32[]{:S(2)}, u32[]{:S(2)}) collective-permute-start(bf16[2,3,96,256]{3,2,1,0:T(8,128)(2,1)S(1)} %get-tuple-element.99), channel_id=1, source_target_pairs={{0,2},{1,3},{2,0},{3,1},{4,6},{5,7},{6,4},{7,5},{8,10},{9,11},{10,... | collective-permute-start | bytes 884744 | tf_op jit(solution)/shard_map/ppermute | solution.py:184
  147.7 9.9 %collective-permute-start.13 = (bf16[2,3,96,256]{3,2,1,0:T(8,128)(2,1)S(1)}, bf16[2,3,96,256]{3,2,1,0:T(8,128)(2,1)S(1)}, u32[]{:S(2)}, u32[]{:S(2)}) collective-permute-start(bf16[2,3,96,256]{3,2,1,0:T(8,128)(2,1)S(1)} %get-tuple-element.100), channel_id=1, source_target_pairs={{0,3},{1,2},{2,1},{3,0},{4,7},{5,6},{6,5},{7,4},{8,11},{9,10},{10,... | collective-permute-start | bytes 884744 | tf_op jit(solution)/shard_map/ppermute | solution.py:184
  148.2 22.5 %collective-permute-start.14 = (bf16[2,3,96,256]{3,2,1,0:T(8,128)(2,1)S(1)}, bf16[2,3,96,256]{3,2,1,0:T(8,128)(2,1)S(1)}, u32[]{:S(2)}, u32[]{:S(2)}) collective-permute-start(bf16[2,3,96,256]{3,2,1,0:T(8,128)(2,1)S(1)} %get-tuple-element.101), channel_id=1, source_target_pairs={{0,4},{1,5},{2,6},{3,7},{4,0},{5,1},{6,2},{7,3},{8,12},{9,13},{10,... | collective-permute-start | bytes 884744 | tf_op jit(solution)/shard_map/ppermute | solution.py:184
  149.3 26.5 %collective-permute-start.15 = (bf16[2,3,96,256]{3,2,1,0:T(8,128)(2,1)S(1)}, bf16[2,3,96,256]{3,2,1,0:T(8,128)(2,1)S(1)}, u32[]{:S(2)}, u32[]{:S(2)}) collective-permute-start(bf16[2,3,96,256]{3,2,1,0:T(8,128)(2,1)S(1)} %get-tuple-element.102), channel_id=1, source_target_pairs={{0,5},{1,4},{2,7},{3,6},{4,1},{5,0},{6,3},{7,2},{8,13},{9,12},{10,... | collective-permute-start | bytes 884744 | tf_op jit(solution)/shard_map/ppermute | solution.py:184
  150.6 27.5 %collective-permute-start.16 = (bf16[2,3,96,256]{3,2,1,0:T(8,128)(2,1)S(1)}, bf16[2,3,96,256]{3,2,1,0:T(8,128)(2,1)S(1)}, u32[]{:S(2)}, u32[]{:S(2)}) collective-permute-start(bf16[2,3,96,256]{3,2,1,0:T(8,128)(2,1)S(1)} %get-tuple-element.103), channel_id=1, source_target_pairs={{0,6},{1,7},{2,4},{3,5},{4,2},{5,3},{6,0},{7,1},{8,14},{9,15},{10,... | collective-permute-start | bytes 884744 | tf_op jit(solution)/shard_map/ppermute | solution.py:184
  152.6 27.5 %collective-permute-start.17 = (bf16[2,3,96,256]{3,2,1,0:T(8,128)(2,1)S(1)}, bf16[2,3,96,256]{3,2,1,0:T(8,128)(2,1)S(1)}, u32[]{:S(2)}, u32[]{:S(2)}) collective-permute-start(bf16[2,3,96,256]{3,2,1,0:T(8,128)(2,1)S(1)} %get-tuple-element.104), channel_id=1, source_target_pairs={{0,7},{1,6},{2,5},{3,4},{4,3},{5,2},{6,1},{7,0},{8,15},{9,14},{10,... | collective-permute-start | bytes 884744 | tf_op jit(solution)/shard_map/ppermute | solution.py:184
  158.3 22.6 %collective-permute-start.32 = (bf16[2,4,96,256]{3,2,1,0:T(8,128)(2,1)S(1)}, bf16[2,4,96,256]{3,2,1,0:T(8,128)(2,1)S(1)}, u32[]{:S(2)}, u32[]{:S(2)}) collective-permute-start(bf16[2,4,96,256]{3,2,1,0:T(8,128)(2,1)S(1)} %get-tuple-element.122), channel_id=1, source_target_pairs={{0,1},{1,0},{2,3},{3,2},{4,5},{5,4},{6,7},{7,6},{8,9},{9,8},{10,11... | collective-permute-start | bytes 1179656 | tf_op jit(solution)/shard_map/ppermute | solution.py:184
  171.4 19.3 %collective-permute-start.33 = (bf16[2,4,96,256]{3,2,1,0:T(8,128)(2,1)S(1)}, bf16[2,4,96,256]{3,2,1,0:T(8,128)(2,1)S(1)}, u32[]{:S(2)}, u32[]{:S(2)}) collective-permute-start(bf16[2,4,96,256]{3,2,1,0:T(8,128)(2,1)S(1)} %get-tuple-element.123), channel_id=1, source_target_pairs={{0,2},{1,3},{2,0},{3,1},{4,6},{5,7},{6,4},{7,5},{8,10},{9,11},{10,... | collective-permute-start | bytes 1179656 | tf_op jit(solution)/shard_map/ppermute | solution.py:184
  176.5 15.7 %collective-permute-start.34 = (bf16[2,4,96,256]{3,2,1,0:T(8,128)(2,1)S(1)}, bf16[2,4,96,256]{3,2,1,0:T(8,128)(2,1)S(1)}, u32[]{:S(2)}, u32[]{:S(2)}) collective-permute-start(bf16[2,4,96,256]{3,2,1,0:T(8,128)(2,1)S(1)} %get-tuple-element.124), channel_id=1, source_target_pairs={{0,3},{1,2},{2,1},{3,0},{4,7},{5,6},{6,5},{7,4},{8,11},{9,10},{10,... | collective-permute-start | bytes 1179656 | tf_op jit(solution)/shard_map/ppermute | solution.py:184
  178.9 20.1 %collective-permute-start.35 = (bf16[2,4,96,256]{3,2,1,0:T(8,128)(2,1)S(1)}, bf16[2,4,96,256]{3,2,1,0:T(8,128)(2,1)S(1)}, u32[]{:S(2)}, u32[]{:S(2)}) collective-permute-start(bf16[2,4,96,256]{3,2,1,0:T(8,128)(2,1)S(1)} %get-tuple-element.125), channel_id=1, source_target_pairs={{0,4},{1,5},{2,6},{3,7},{4,0},{5,1},{6,2},{7,3},{8,12},{9,13},{10,... | collective-permute-start | bytes 1179656 | tf_op jit(solution)/shard_map/ppermute | solution.py:184
  180.9 24.4 %collective-permute-start.36 = (bf16[2,4,96,256]{3,2,1,0:T(8,128)(2,1)S(1)}, bf16[2,4,96,256]{3,2,1,0:T(8,128)(2,1)S(1)}, u32[]{:S(2)}, u32[]{:S(2)}) collective-permute-start(bf16[2,4,96,256]{3,2,1,0:T(8,128)(2,1)S(1)} %get-tuple-element.126), channel_id=1, source_target_pairs={{0,5},{1,4},{2,7},{3,6},{4,1},{5,0},{6,3},{7,2},{8,13},{9,12},{10,... | collective-permute-start | bytes 1179656 | tf_op jit(solution)/shard_map/ppermute | solution.py:184
  181.6 25.7 %collective-permute-start.37 = (bf16[2,4,96,256]{3,2,1,0:T(8,128)(2,1)S(1)}, bf16[2,4,96,256]{3,2,1,0:T(8,128)(2,1)S(1)}, u32[]{:S(2)}, u32[]{:S(2)}) collective-permute-start(bf16[2,4,96,256]{3,2,1,0:T(8,128)(2,1)S(1)} %get-tuple-element.127), channel_id=1, source_target_pairs={{0,6},{1,7},{2,4},{3,5},{4,2},{5,3},{6,0},{7,1},{8,14},{9,15},{10,... | collective-permute-start | bytes 1179656 | tf_op jit(solution)/shard_map/ppermute | solution.py:184
  191.5 48.6 %collective-permute-start.25 = (bf16[2,8,96,256]{3,2,1,0:T(8,128)(2,1)S(1)}, bf16[2,8,96,256]{3,2,1,0:T(8,128)(2,1)S(1)}, u32[]{:S(2)}, u32[]{:S(2)}) collective-permute-start(bf16[2,8,96,256]{3,2,1,0:T(8,128)(2,1)S(1)} %get-tuple-element.114), channel_id=1, source_target_pairs={{0,1},{1,0},{2,3},{3,2},{4,5},{5,4},{6,7},{7,6},{8,9},{9,8},{10,11... | collective-permute-start | bytes 2359304 | tf_op jit(solution)/shard_map/ppermute | solution.py:184
  192.9 50.9 %collective-permute-start.26 = (bf16[2,8,96,256]{3,2,1,0:T(8,128)(2,1)S(1)}, bf16[2,8,96,256]{3,2,1,0:T(8,128)(2,1)S(1)}, u32[]{:S(2)}, u32[]{:S(2)}) collective-permute-start(bf16[2,8,96,256]{3,2,1,0:T(8,128)(2,1)S(1)} %get-tuple-element.115), channel_id=1, source_target_pairs={{0,2},{1,3},{2,0},{3,1},{4,6},{5,7},{6,4},{7,5},{8,10},{9,11},{10,... | collective-permute-start | bytes 2359304 | tf_op jit(solution)/shard_map/ppermute | solution.py:184
  199.8 44.1 %collective-permute-start.27 = (bf16[2,8,96,256]{3,2,1,0:T(8,128)(2,1)S(1)}, bf16[2,8,96,256]{3,2,1,0:T(8,128)(2,1)S(1)}, u32[]{:S(2)}, u32[]{:S(2)}) collective-permute-start(bf16[2,8,96,256]{3,2,1,0:T(8,128)(2,1)S(1)} %get-tuple-element.116), channel_id=1, source_target_pairs={{0,3},{1,2},{2,1},{3,0},{4,7},{5,6},{6,5},{7,4},{8,11},{9,10},{10,... | collective-permute-start | bytes 2359304 | tf_op jit(solution)/shard_map/ppermute | solution.py:184
  206.1 37.9 %collective-permute-start.28 = (bf16[2,8,96,256]{3,2,1,0:T(8,128)(2,1)S(1)}, bf16[2,8,96,256]{3,2,1,0:T(8,128)(2,1)S(1)}, u32[]{:S(2)}, u32[]{:S(2)}) collective-permute-start(bf16[2,8,96,256]{3,2,1,0:T(8,128)(2,1)S(1)} %get-tuple-element.117), channel_id=1, source_target_pairs={{0,4},{1,5},{2,6},{3,7},{4,0},{5,1},{6,2},{7,3},{8,12},{9,13},{10,... | collective-permute-start | bytes 2359304 | tf_op jit(solution)/shard_map/ppermute | solution.py:184
  207.4 31.7 %collective-permute-start.38 = (bf16[2,4,96,256]{3,2,1,0:T(8,128)(2,1)S(1)}, bf16[2,4,96,256]{3,2,1,0:T(8,128)(2,1)S(1)}, u32[]{:S(2)}, u32[]{:S(2)}) collective-permute-start(bf16[2,4,96,256]{3,2,1,0:T(8,128)(2,1)S(1)} %get-tuple-element.128), channel_id=1, source_target_pairs={{0,7},{1,6},{2,5},{3,4},{4,3},{5,2},{6,1},{7,0},{8,15},{9,14},{10,... | collective-permute-start | bytes 1179656 | tf_op jit(solution)/shard_map/ppermute | solution.py:184
  239.9 52.3 %collective-permute-start.29 = (bf16[2,8,96,256]{3,2,1,0:T(8,128)(2,1)S(1)}, bf16[2,8,96,256]{3,2,1,0:T(8,128)(2,1)S(1)}, u32[]{:S(2)}, u32[]{:S(2)}) collective-permute-start(bf16[2,8,96,256]{3,2,1,0:T(8,128)(2,1)S(1)} %get-tuple-element.118), channel_id=1, source_target_pairs={{0,5},{1,4},{2,7},{3,6},{4,1},{5,0},{6,3},{7,2},{8,13},{9,12},{10,... | collective-permute-start | bytes 2359304 | tf_op jit(solution)/shard_map/ppermute | solution.py:184
  240.1 55.3 %collective-permute-start.30 = (bf16[2,8,96,256]{3,2,1,0:T(8,128)(2,1)S(1)}, bf16[2,8,96,256]{3,2,1,0:T(8,128)(2,1)S(1)}, u32[]{:S(2)}, u32[]{:S(2)}) collective-permute-start(bf16[2,8,96,256]{3,2,1,0:T(8,128)(2,1)S(1)} %get-tuple-element.119), channel_id=1, source_target_pairs={{0,6},{1,7},{2,4},{3,5},{4,2},{5,3},{6,0},{7,1},{8,14},{9,15},{10,... | collective-permute-start | bytes 2359304 | tf_op jit(solution)/shard_map/ppermute | solution.py:184
  243.8 52.6 %collective-permute-start.31 = (bf16[2,8,96,256]{3,2,1,0:T(8,128)(2,1)S(1)}, bf16[2,8,96,256]{3,2,1,0:T(8,128)(2,1)S(1)}, u32[]{:S(2)}, u32[]{:S(2)}) collective-permute-start(bf16[2,8,96,256]{3,2,1,0:T(8,128)(2,1)S(1)} %get-tuple-element.120), channel_id=1, source_target_pairs={{0,7},{1,6},{2,5},{3,4},{4,3},{5,2},{6,1},{7,0},{8,15},{9,14},{10,... | collective-permute-start | bytes 2359304 | tf_op jit(solution)/shard_map/ppermute | solution.py:184
  243.8 54.1 %collective-permute-start.18 = (bf16[2,8,96,256]{3,2,1,0:T(8,128)(2,1)S(1)}, bf16[2,8,96,256]{3,2,1,0:T(8,128)(2,1)S(1)}, u32[]{:S(2)}, u32[]{:S(2)}) collective-permute-start(bf16[2,8,96,256]{3,2,1,0:T(8,128)(2,1)S(1)} %get-tuple-element.106), channel_id=1, source_target_pairs={{0,1},{1,0},{2,3},{3,2},{4,5},{5,4},{6,7},{7,6},{8,9},{9,8},{10,11... | collective-permute-start | bytes 2359304 | tf_op jit(solution)/shard_map/ppermute | solution.py:184
  244.9 55.8 %collective-permute-start.19 = (bf16[2,8,96,256]{3,2,1,0:T(8,128)(2,1)S(1)}, bf16[2,8,96,256]{3,2,1,0:T(8,128)(2,1)S(1)}, u32[]{:S(2)}, u32[]{:S(2)}) collective-permute-start(bf16[2,8,96,256]{3,2,1,0:T(8,128)(2,1)S(1)} %get-tuple-element.107), channel_id=1, source_target_pairs={{0,2},{1,3},{2,0},{3,1},{4,6},{5,7},{6,4},{7,5},{8,10},{9,11},{10,... | collective-permute-start | bytes 2359304 | tf_op jit(solution)/shard_map/ppermute | solution.py:184
  293.0 31.9 %collective-permute-start.20 = (bf16[2,8,96,256]{3,2,1,0:T(8,128)(2,1)}, bf16[2,8,96,256]{3,2,1,0:T(8,128)(2,1)}, u32[]{:S(2)}, u32[]{:S(2)}) collective-permute-start(bf16[2,8,96,256]{3,2,1,0:T(8,128)(2,1)} %get-tuple-element.108), channel_id=1, source_target_pairs={{0,3},{1,2},{2,1},{3,0},{4,7},{5,6},{6,5},{7,4},{8,11},{9,10},{10,... | collective-permute-start | bytes 2359304 | tf_op jit(solution)/shard_map/ppermute | solution.py:184
  296.4 54.4 %collective-permute-start.21 = (bf16[2,8,96,256]{3,2,1,0:T(8,128)(2,1)}, bf16[2,8,96,256]{3,2,1,0:T(8,128)(2,1)}, u32[]{:S(2)}, u32[]{:S(2)}) collective-permute-start(bf16[2,8,96,256]{3,2,1,0:T(8,128)(2,1)} %get-tuple-element.109), channel_id=1, source_target_pairs={{0,4},{1,5},{2,6},{3,7},{4,0},{5,1},{6,2},{7,3},{8,12},{9,13},{10,... | collective-permute-start | bytes 2359304 | tf_op jit(solution)/shard_map/ppermute | solution.py:184
  297.3 67.8 %collective-permute-start.22 = (bf16[2,8,96,256]{3,2,1,0:T(8,128)(2,1)}, bf16[2,8,96,256]{3,2,1,0:T(8,128)(2,1)}, u32[]{:S(2)}, u32[]{:S(2)}) collective-permute-start(bf16[2,8,96,256]{3,2,1,0:T(8,128)(2,1)} %get-tuple-element.110), channel_id=1, source_target_pairs={{0,5},{1,4},{2,7},{3,6},{4,1},{5,0},{6,3},{7,2},{8,13},{9,12},{10,... | collective-permute-start | bytes 2359304 | tf_op jit(solution)/shard_map/ppermute | solution.py:184
  298.8 68.9 %collective-permute-start.23 = (bf16[2,8,96,256]{3,2,1,0:T(8,128)(2,1)}, bf16[2,8,96,256]{3,2,1,0:T(8,128)(2,1)}, u32[]{:S(2)}, u32[]{:S(2)}) collective-permute-start(bf16[2,8,96,256]{3,2,1,0:T(8,128)(2,1)} %get-tuple-element.111), channel_id=1, source_target_pairs={{0,6},{1,7},{2,4},{3,5},{4,2},{5,3},{6,0},{7,1},{8,14},{9,15},{10,... | collective-permute-start | bytes 2359304 | tf_op jit(solution)/shard_map/ppermute | solution.py:184
  301.7 66.0 %collective-permute-start.24 = (bf16[2,8,96,256]{3,2,1,0:T(8,128)(2,1)}, bf16[2,8,96,256]{3,2,1,0:T(8,128)(2,1)}, u32[]{:S(2)}, u32[]{:S(2)}) collective-permute-start(bf16[2,8,96,256]{3,2,1,0:T(8,128)(2,1)} %get-tuple-element.112), channel_id=1, source_target_pairs={{0,7},{1,6},{2,5},{3,4},{4,3},{5,2},{6,1},{7,0},{8,15},{9,14},{10,... | collective-permute-start | bytes 2359304 | tf_op jit(solution)/shard_map/ppermute | solution.py:184
  325.0 64.7 %collective-permute-start.5 = (bf16[2,1,96,256]{3,2,1,0:T(8,128)(2,1)S(1)}, bf16[2,1,96,256]{3,2,1,0:T(8,128)(2,1)S(1)}, u32[]{:S(2)}, u32[]{:S(2)}) collective-permute-start(bf16[2,1,96,256]{3,2,1,0:T(8,128)(2,1)S(1)} %copy-done.112), channel_id=1, source_target_pairs={{0,2},{1,3},{2,0},{3,1},{4,6},{5,7},{6,4},{7,5},{8,10},{9,11},{10,... | collective-permute-start | bytes 294920 | tf_op jit(solution)/shard_map/ppermute | solution.py:184
  350.8 38.9 %collective-permute-start.6 = (bf16[2,1,96,256]{3,2,1,0:T(8,128)(2,1)S(1)}, bf16[2,1,96,256]{3,2,1,0:T(8,128)(2,1)S(1)}, u32[]{:S(2)}, u32[]{:S(2)}) collective-permute-start(bf16[2,1,96,256]{3,2,1,0:T(8,128)(2,1)S(1)} %copy-done.110), channel_id=1, source_target_pairs={{0,3},{1,2},{2,1},{3,0},{4,7},{5,6},{6,5},{7,4},{8,11},{9,10},{10,... | collective-permute-start | bytes 294920 | tf_op jit(solution)/shard_map/ppermute | solution.py:184
  365.1 24.6 %collective-permute-start.7 = (bf16[2,1,96,256]{3,2,1,0:T(8,128)(2,1)S(1)}, bf16[2,1,96,256]{3,2,1,0:T(8,128)(2,1)S(1)}, u32[]{:S(2)}, u32[]{:S(2)}) collective-permute-start(bf16[2,1,96,256]{3,2,1,0:T(8,128)(2,1)S(1)} %copy-done.108), channel_id=1, source_target_pairs={{0,4},{1,5},{2,6},{3,7},{4,0},{5,1},{6,2},{7,3},{8,12},{9,13},{10,... | collective-permute-start | bytes 294920 | tf_op jit(solution)/shard_map/ppermute | solution.py:184
  367.7 22.1 %collective-permute-start.8 = (bf16[2,1,96,256]{3,2,1,0:T(8,128)(2,1)S(1)}, bf16[2,1,96,256]{3,2,1,0:T(8,128)(2,1)S(1)}, u32[]{:S(2)}, u32[]{:S(2)}) collective-permute-start(bf16[2,1,96,256]{3,2,1,0:T(8,128)(2,1)S(1)} %copy-done.106), channel_id=1, source_target_pairs={{0,5},{1,4},{2,7},{3,6},{4,1},{5,0},{6,3},{7,2},{8,13},{9,12},{10,... | collective-permute-start | bytes 294920 | tf_op jit(solution)/shard_map/ppermute | solution.py:184
  367.7 22.0 %collective-permute-start.9 = (bf16[2,1,96,256]{3,2,1,0:T(8,128)(2,1)S(1)}, bf16[2,1,96,256]{3,2,1,0:T(8,128)(2,1)S(1)}, u32[]{:S(2)}, u32[]{:S(2)}) collective-permute-start(bf16[2,1,96,256]{3,2,1,0:T(8,128)(2,1)S(1)} %copy-done.104), channel_id=1, source_target_pairs={{0,6},{1,7},{2,4},{3,5},{4,2},{5,3},{6,0},{7,1},{8,14},{9,15},{10,... | collective-permute-start | bytes 294920 | tf_op jit(solution)/shard_map/ppermute | solution.py:184
  (142 other events, 1052.9 us)

commit v4 on v3

--- a/solution.py
+++ b/solution.py
@@ -25,13 +25,18 @@
     ]
 
 
-def square_sums(w_gate, w_up, first, count, halved=False):
+def square_sums(w_gate, w_up, first, count, halved=False, kept=False):
     _, rows, cols = w_gate.shape
     results = 2 if halved else 1
     height = count // results
-
-    def kernel(*refs):
-        sources, out_refs, (held, arrived) = refs[:2], refs[2:-2], refs[-2:]
+    shapes = [jax.ShapeDtypeStruct((2, height, cols), jnp.float32)] * results
+    weights = (count, 2, rows, cols)
+    if kept:
+        shapes.append(jax.ShapeDtypeStruct(weights, jnp.float32))
+
+    def kernel(*refs):
+        sources, out_refs = refs[:2], refs[2 : 2 + results]
+        held, arrived = refs[2 + results :]
         for n in range(count):
             for copy in fetches(sources, first, held, arrived, n):
                 copy.start()
@@ -61,15 +66,15 @@
     return pl.pallas_call(
         kernel,
         in_specs=[pl.BlockSpec(memory_space=pl.ANY)] * 2,
-        out_specs=[pl.BlockSpec(memory_space=pltpu.VMEM)] * results,
-        out_shape=[jax.ShapeDtypeStruct((2, height, cols), jnp.float32)] * results,
-        scratch_shapes=[pltpu.VMEM((count, 2, rows, cols), jnp.float32), pltpu.SemaphoreType.DMA((count, 2))],
+        out_specs=[pl.BlockSpec(memory_space=pltpu.VMEM)] * len(shapes),
+        out_shape=shapes,
+        scratch_shapes=([] if kept else [pltpu.VMEM(weights, jnp.float32)]) + [pltpu.SemaphoreType.DMA((count, 2))],
         compiler_params=granted(44),
         cost_estimate=cost(4 * count * rows * cols, 8 * count * rows * cols),
     )(w_gate, w_up)
 
 
-def scaled_pieces(w_gate, w_up, totals, halved, first, count, start, size):
+def scaled_pieces(w_gate, w_up, totals, first, count, start, size):
     _, rows, cols = w_gate.shape
     width = cols // size
 
@@ -78,15 +83,10 @@
         me = lax.axis_index("zero")
         step = pl.program_id(0)
         for side, w_ref in enumerate((gate_ref, up_ref)):
-            if halved:
-                height = totals[0].shape[1]
-                half = jnp.where(start + step >= height, 1, 0)
-                row = pl.ds(start + step - half * height, 1)
-                total = jnp.where(
-                    half == me % 2, total_refs[0][side, row, :], total_refs[1][side, row, :]
-                )
-            else:
-                total = sum(ref[side, pl.ds(start + step, 1), :] for ref in total_refs)
+            height = totals[0].shape[1]
+            half = jnp.where(start + step >= height, 1, 0)
+            row = pl.ds(start + step - half * height, 1)
+            total = jnp.where(half == me % 2, total_refs[0][side, row, :], total_refs[1][side, row, :])
             inverse = 1.0 / jnp.sqrt(total)
             held[side] = (w_ref[0] * inverse).astype(jnp.bfloat16).T
             for k in range(size):
@@ -105,6 +105,63 @@
         compiler_params=granted(44),
         cost_estimate=cost(4 * count * rows * cols, 12 * count * rows * cols),
     )(w_gate, w_up, *totals)
+
+
+def scaled_held(weights, totals, start, count, size):
+    _, _, rows, cols = weights.shape
+    width = cols // size
+
+    def kernel(w_ref, *refs):
+        total_refs, outs, held = refs[: len(totals)], refs[len(totals) : -1], refs[-1]
+        me = lax.axis_index("zero")
+        for n in range(count):
+            for side in range(2):
+                total = sum(ref[side, pl.ds(start + n, 1), :] for ref in total_refs)
+                inverse = 1.0 / jnp.sqrt(total)
+                held[n, side] = (w_ref[start + n, side] * inverse).astype(jnp.bfloat16).T
+                for k in range(size):
+                    offset = pl.multiple_of(lax.bitwise_xor(me, k) * width, width)
+                    outs[k][side, n] = held[n, side, pl.ds(offset, width), :]
+
+    return pl.pallas_call(
+        kernel,
+        in_specs=[pl.BlockSpec(memory_space=pltpu.VMEM)] * (1 + len(totals)),
+        out_specs=[pl.BlockSpec(memory_space=pltpu.VMEM)] * size,
+        out_shape=[jax.ShapeDtypeStruct((2, count, width, rows), jnp.bfloat16)] * size,
+        scratch_shapes=[pltpu.VMEM((count, 2, cols, rows), jnp.bfloat16)],
+        compiler_params=granted(44),
+        cost_estimate=cost(4 * count * rows * cols, 12 * count * rows * cols),
+    )(weights, *totals)
+
+
+def placed(pieces, outputs, first):
+    size = len(pieces)
+    _, count, width, rows = pieces[0].shape
+
+    def kernel(*refs):
+        ins, outs, left = refs[:size], refs[-3:-1], refs[-1]
+        me = lax.axis_index("zero")
+        copies = []
+        for k in range(size):
+            offset = pl.multiple_of(lax.bitwise_xor(me, k) * rows, rows)
+            for side in range(2):
+                place = outs[side].at[pl.ds(first, count), :, pl.ds(offset, rows)]
+                copies.append(pltpu.make_async_copy(ins[k].at[side], place, left.at[k, side]))
+        for copy in copies:
+            copy.start()
+        for copy in copies:
+            copy.wait()
+
+    return pl.pallas_call(
+        kernel,
+        in_specs=[pl.BlockSpec(memory_space=pltpu.VMEM)] * size + [pl.BlockSpec(memory_space=pl.ANY)] * 2,
+        out_specs=[pl.BlockSpec(memory_space=pl.ANY)] * 2,
+        out_shape=[jax.ShapeDtypeStruct(x.shape, x.dtype) for x in outputs],
+        input_output_aliases={size + n: n for n in range(2)},
+        scratch_shapes=[pltpu.SemaphoreType.DMA((size, 2))],
+        compiler_params=granted(44),
+        cost_estimate=cost(count * width * rows * size, 8 * count * width * rows * size),
+    )(*pieces, *outputs)
 
 
 def assembled(pieces, outputs, first, experts):
@@ -173,7 +230,7 @@
 
 def chunk_sizes(experts):
     unit = experts // 32
-    return [[unit * n for n in group] for group in ((2,), (2, 4), (4, 8, 8, 3, 1))]
+    return [[unit * n for n in group] for group in ((2,), (2, 2), (2, 4, 8, 8, 3, 1))]
 
 
 def piped(w_gate, w_up, router_weight, router_gain, size, banks):
@@ -190,8 +247,10 @@
 
     totals, starts = [], [sum(map(sum, groups[:g])) for g in range(len(groups))]
     last = len(groups) - 1
+    kept = []
     for g, group in enumerate(groups[:last]):
-        (own,) = square_sums(w_gate, w_up, starts[g], sum(group))
+        own, weights = square_sums(w_gate, w_up, starts[g], sum(group), kept=True)
+        kept.append(weights)
         own = own + send(own, 1)
         totals.append([own] + [send(own, k) for k in range(2, size, 2)])
     own, other = square_sums(w_gate, w_up, starts[last], sum(groups[last]), halved=True)
@@ -206,7 +265,10 @@
     for c in chunks:
         group = max(g for g in range(len(groups)) if starts[g] <= firsts[c])
         start = firsts[c] - starts[group]
-        sent.append(scaled_pieces(w_gate, w_up, totals[group], group == last, firsts[c], sizes[c], start, size))
+        if group < last:
+            sent.append(scaled_held(kept[group], totals[group], start, sizes[c], size))
+        else:
+            sent.append(scaled_pieces(w_gate, w_up, totals[group], firsts[c], sizes[c], start, size))
         got.append([sent[c][0]] + [send(sent[c][k], k) for k in range(1, size)])
 
     part = (router_weight * router_gain[:, None]).astype(jnp.bfloat16).T
@@ -220,7 +282,10 @@
 
     outputs = None
     for c in chunks:
-        outputs = assembled(got[c], outputs, firsts[c], experts)
+        if c < len(sizes) - 1:
+            outputs = assembled(got[c], outputs, firsts[c], experts)
+        else:
+            outputs = placed(got[c], outputs, firsts[c])
     serve_gate, serve_up = (jnp.swapaxes(x, 1, 2) for x in outputs)
 
     even = lax.axis_index("zero") % 2 == 0

time: 392 us -> 391 us (level)
  waiting for transfers between devices: 185 us -> 167 us
  local copies, waits for them, and re-layouts: 47.3 us -> 58.8 us
  starting transfers between devices: 75.1 us -> 81.5 us
  Pallas kernels: 80.3 us -> 75.9 us
    ppermute x78 -> x85, waiting for transfers between devices: 185 us -> 167 us  [send(): return lax.ppermute(x, axis, xor_pairs(count, k))]
    unnamed x256 -> x284, local copies, waits for them, and re-layouts: 46.6 us -> 58.2 us
    pallas_call x8 -> x6, Pallas kernels: 35.4 us -> 28.9 us  [scaled_pieces(): pl.pallas_call(kernel, grid=(count,), in_specs=[weights, weights] + [pl.B...]
    ppermute x78 -> x85, starting transfers between devices: 75.1 us -> 81.5 us  [send(): return lax.ppermute(x, axis, xor_pairs(count, k))]
  transfers between devices with their start and end apart: 78 -> 85, of which waited for: 18 -> 20; matrix products, arithmetic and copies ran while one was open for 1% -> 1% of each run, Pallas kernels for 17% -> 19%
where the time goes in v4:
time: 391 us; the launch traced here: 388 us
  waiting for transfers between devices  167 us (43%)
  starting transfers between devices  81.5 us (21%)
  Pallas kernels  75.9 us (19%)
  local copies, waits for them, and re-layouts  58.8 us (15%)
    ppermute x85, waiting for transfers between devices, send(): return lax.ppermute(x, axis, xor_pairs(count, k))  167 us
    ppermute x85, starting transfers between devices, send(): return lax.ppermute(x, axis, xor_pairs(count, k))  81.5 us
    unnamed x284, local copies, waits for them, and re-layouts  58.2 us
    pallas_call x6, Pallas kernels, scaled_pieces(): pl.pallas_call(kernel, grid=(count,), in_specs=[weights, weights] + [pl.B...  28.9 us
    pallas_call x8, Pallas kernels, assembled(): pl.pallas_call(kernel, grid=(count,), in_specs=[piece] * size + [pl.Block...  22.6 us
    pallas_call x3, Pallas kernels, square_sums(): pl.pallas_call(kernel, in_specs=[pl.BlockSpec(memory_space=pl.ANY)] * 2,...  18.1 us
  transfers between devices with their start and end apart: 85, of which 20 were waited for; matrix products, arithmetic and copies ran while one was open for 1% of the time, Pallas kernels for 19%

profile of v4, /device:TPU:0, one launch (start us, length us, event | category | flops | bytes accessed | tf_op | source)
XLA Modules:
  0.0 387.5 jit_solution(17852630161944725860)
XLA Ops:
  0.6 2.0 shard_map.93
  3.2 13.2 %shard_map.83 = (f32[2,13,768]{2,1,0:T(8,128)S(1)}, f32[2,13,768]{2,1,0:T(8,128)S(1)}) custom-call(f32[32,256,768]{2,1,0:T(8,128)} %refs_0_.5, f32[32,256,768]{2,1,0:T(8,128)} %refs_1_.5), custom_call_target="tpu_custom_call" | custom-call | flops 20447232 | bytes 40894464 | tf_op jit(solution)/shard_map/pallas_call | solution.py:66
  16.5 3.0 collective-permute-start.76
  19.5 1.5 collective-permute-start.78
  21.1 2.9 shard_map.90
  24.1 2.7 copy-done
  28.5 1.9 collective-permute-start.65
  31.6 1.5 shard_map.104.refs_0_
  33.1 1.6 collective-permute-start.82
  35.3 1.5 collective-permute-start.66
  36.9 1.4 collective-permute-start.67
  38.3 1.5 collective-permute-start.48
  41.5 2.6 collective-permute-start.83
  44.1 1.4 collective-permute-start.49
  46.7 2.1 collective-permute-done.49.refs_3_
  48.8 1.6 collective-permute-start.69
  51.7 5.7 %collective-permute-done.84.refs_3_ = bf16[32,2048]{1,0:T(8,128)(2,1)S(1)} collective-permute-done((bf16[32,2048]{1,0:T(8,128)(2,1)}, bf16[32,2048]{1,0:T(8,128)(2,1)S(1)}, u32[]{:S(2)}, u32[]{:S(2)}) %collective-permute-start.84) | collective-permute-done | bytes 131104 | tf_op jit(solution)/shard_map/ppermute | solution.py:241
  60.0 2.2 collective-permute-start.74
  62.3 2.8 copy-done.1
  68.3 4.4 %collective-permute-done.72.refs_5_ = bf16[2,2,96,256]{3,2,1,0:T(8,128)(2,1)S(1)} collective-permute-done((bf16[2,2,96,256]{3,2,1,0:T(8,128)(2,1)S(1)}, bf16[2,2,96,256]{3,2,1,0:T(8,128)(2,1)S(1)}, u32[]{:S(2)}, u32[]{:S(2)}) %collective-permute-start.72) | collective-permute-done | bytes 196640 | tf_op jit(solution)/shard_map/ppermute | solution.py:241
  73.4 1.5 collective-permute-start.60
  76.1 6.9 %collective-permute-done.2 = f32[2,13,768]{2,1,0:T(8,128)S(1)} collective-permute-done((f32[2,13,768]{2,1,0:T(8,128)S(1)}, f32[2,13,768]{2,1,0:T(8,128)S(1)}, u32[]{:S(2)}, u32[]{:S(2)}) %collective-permute-start.2) | collective-permute-done | bytes 79904 | tf_op jit(solution)/shard_map/ppermute | solution.py:241
  84.4 1.9 collective-permute-start.62
  89.4 1.4 collective-permute-start.51
  90.8 7.8 %collective-permute-done.61.refs_5_ = bf16[2,2,96,256]{3,2,1,0:T(8,128)(2,1)S(1)} collective-permute-done((bf16[2,2,96,256]{3,2,1,0:T(8,128)(2,1)S(1)}, bf16[2,2,96,256]{3,2,1,0:T(8,128)(2,1)S(1)}, u32[]{:S(2)}, u32[]{:S(2)}) %collective-permute-start.61) | collective-permute-done | bytes 196640 | tf_op jit(solution)/shard_map/ppermute | solution.py:241
  104.9 1.7 shard_map.84
  110.6 1.5 collective-permute-start.10
  112.0 2.3 shard_map.89
  115.0 3.1 collective-permute-done.53.refs_4_
  118.1 2.5 collective-permute-done.54.refs_5_
  125.6 3.6 shard_map.85
  133.7 2.2 collective-permute-start.44
  137.4 2.9 collective-permute-done.43.refs_5_
  140.9 1.6 collective-permute-start.13
  142.5 3.1 collective-permute-done.44.refs_6_
  148.7 2.5 collective-permute-start.15
  154.6 4.1 %shard_map.88 = (bf16[2,4,96,256]{3,2,1,0:T(8,128)(2,1)S(1)}, bf16[2,4,96,256]{3,2,1,0:T(8,128)(2,1)S(1)}, bf16[2,4,96,256]{3,2,1,0:T(8,128)(2,1)S(1)}, bf16[2,4...) custom-call(f32[32,256,768]{2,1,0:T(8,128)} %refs_0_.5, ...), custom_call_target="tpu_custom_call" | custom-call | flops 3145728 | bytes 9437184 | tf_op jit(solution)/shard_map/pallas_call | solution.py:98
  160.6 7.9 %collective-permute-done.14.refs_4_ = bf16[2,3,96,256]{3,2,1,0:T(8,128)(2,1)S(1)} collective-permute-done((bf16[2,3,96,256]{3,2,1,0:T(8,128)(2,1)S(1)}, bf16[2,3,96,256]{3,2,1,0:T(8,128)(2,1)S(1)}, u32[]{:S(2)}, u32[]{:S(2)}) %collective-permute-start.14) | collective-permute-done | bytes 294944 | tf_op jit(solution)/shard_map/ppermute | solution.py:241
  170.2 3.2 collective-permute-done.15.refs_5_
  176.2 1.5 collective-permute-start.35
  178.4 1.9 collective-permute-start.37
  180.3 7.9 %shard_map.87 = (bf16[2,8,96,256]{3,2,1,0:T(8,128)(2,1)S(1)}, bf16[2,8,96,256]{3,2,1,0:T(8,128)(2,1)S(1)}, bf16[2,8,96,256]{3,2,1,0:T(8,128)(2,1)S(1)}, bf16[2,8...) custom-call(f32[32,256,768]{2,1,0:T(8,128)} %refs_0_.5, ...), custom_call_target="tpu_custom_call" | custom-call | flops 6291456 | bytes 18874368 | tf_op jit(solution)/shard_map/pallas_call | solution.py:98
  191.2 5.5 %collective-permute-done.35.refs_4_ = bf16[2,4,96,256]{3,2,1,0:T(8,128)(2,1)S(1)} collective-permute-done((bf16[2,4,96,256]{3,2,1,0:T(8,128)(2,1)S(1)}, bf16[2,4,96,256]{3,2,1,0:T(8,128)(2,1)S(1)}, u32[]{:S(2)}, u32[]{:S(2)}) %collective-permute-start.35) | collective-permute-done | bytes 393248 | tf_op jit(solution)/shard_map/ppermute | solution.py:241
  196.7 6.2 %collective-permute-done.36.refs_5_ = bf16[2,4,96,256]{3,2,1,0:T(8,128)(2,1)S(1)} collective-permute-done((bf16[2,4,96,256]{3,2,1,0:T(8,128)(2,1)S(1)}, bf16[2,4,96,256]{3,2,1,0:T(8,128)(2,1)S(1)}, u32[]{:S(2)}, u32[]{:S(2)}) %collective-permute-start.36) | collective-permute-done | bytes 393248 | tf_op jit(solution)/shard_map/ppermute | solution.py:241
  204.0 1.9 collective-permute-start.38
  206.0 9.4 %shard_map.86 = (bf16[2,8,96,256]{3,2,1,0:T(8,128)(2,1)S(1)}, bf16[2,8,96,256]{3,2,1,0:T(8,128)(2,1)S(1)}, bf16[2,8,96,256]{3,2,1,0:T(8,128)(2,1)S(1)}, bf16[2,8...) custom-call(f32[32,256,768]{2,1,0:T(8,128)} %refs_0_.5, ...), custom_call_target="tpu_custom_call" | custom-call | flops 6291456 | bytes 18874368 | tf_op jit(solution)/shard_map/pallas_call | solution.py:98
  216.2 20.3 %collective-permute-done.38.refs_7_ = bf16[2,4,96,256]{3,2,1,0:T(8,128)(2,1)S(1)} collective-permute-done((bf16[2,4,96,256]{3,2,1,0:T(8,128)(2,1)S(1)}, bf16[2,4,96,256]{3,2,1,0:T(8,128)(2,1)S(1)}, u32[]{:S(2)}, u32[]{:S(2)}) %collective-permute-start.38) | collective-permute-done | bytes 393248 | tf_op jit(solution)/shard_map/ppermute | solution.py:241
  237.8 1.9 collective-permute-start.30
  242.7 47.3 %collective-permute-done.29.refs_5_ = bf16[2,8,96,256]{3,2,1,0:T(8,128)(2,1)S(1)} collective-permute-done((bf16[2,8,96,256]{3,2,1,0:T(8,128)(2,1)S(1)}, bf16[2,8,96,256]{3,2,1,0:T(8,128)(2,1)S(1)}, u32[]{:S(2)}, u32[]{:S(2)}) %collective-permute-start.29) | collective-permute-done | bytes 786464 | tf_op jit(solution)/shard_map/ppermute | solution.py:241
  295.9 1.7 collective-permute-start.23
  298.6 1.4 collective-permute-start.24
  300.9 2.1 shard_map.105
  319.4 1.4 shard_map.96
  321.4 1.4 shard_map.97
  322.9 1.6 collective-permute-start.5
  324.5 22.8 %collective-permute-done.21.refs_4_ = bf16[2,8,96,256]{3,2,1,0:T(8,128)(2,1)} collective-permute-done((bf16[2,8,96,256]{3,2,1,0:T(8,128)(2,1)}, bf16[2,8,96,256]{3,2,1,0:T(8,128)(2,1)}, u32[]{:S(2)}, u32[]{:S(2)}) %collective-permute-start.21) | collective-permute-done | bytes 786464 | tf_op jit(solution)/shard_map/ppermute | solution.py:241
  347.3 14.7 %collective-permute-done.22.refs_5_ = bf16[2,8,96,256]{3,2,1,0:T(8,128)(2,1)} collective-permute-done((bf16[2,8,96,256]{3,2,1,0:T(8,128)(2,1)}, bf16[2,8,96,256]{3,2,1,0:T(8,128)(2,1)}, u32[]{:S(2)}, u32[]{:S(2)}) %collective-permute-start.22) | collective-permute-done | bytes 786464 | tf_op jit(solution)/shard_map/ppermute | solution.py:241
  362.7 1.6 collective-permute-start.8
  364.3 1.6 collective-permute-start.9
  366.7 1.4 shard_map.98
  369.0 2.5 shard_map.99
  371.7 4.5 %shard_map.100 = (bf16[32,96,2048]{2,1,0:T(8,128)(2,1)}, bf16[32,96,2048]{2,1,0:T(8,128)(2,1)}) custom-call(bf16[2,8,96,256]{3,2,1,0:T(8,128)(2,1)S(1)} %get-tuple-element.127.refs_0_, bf16[2,8,96,256]{3,2,1,0:T(8,128)(2,1)S(1)} %collective-permute-done.25.refs_1_, ...), custom_call_target="tpu_custom_call", output_to_operand_aliasing={{0}: (8, {}), {1}: (9, {})} | custom-call | flops 1572864 | bytes 12582912 | tf_op jit(solution)/shard_map/pallas_call | solution.py:182
  376.3 7.7 %shard_map.101 = (bf16[32,96,2048]{2,1,0:T(8,128)(2,1)}, bf16[32,96,2048]{2,1,0:T(8,128)(2,1)}) custom-call(bf16[2,8,96,256]{3,2,1,0:T(8,128)(2,1)S(1)} %copy-done.5, bf16[2,8,96,256]{3,2,1,0:T(8,128)(2,1)S(1)} %copy-done.11, bf16[2,8,96,256]{3,2,1,0:T(8,128)(2,1)S(1)} %copy-done.15, ...), custom_call_target="tpu_custom_call", output_to_operand_aliasing={{0}: (8, {}), {1}: (9, {})} | custom-call | flops 1572864 | bytes 12582912 | tf_op jit(solution)/shard_map/pallas_call | solution.py:182
  384.2 2.1 shard_map.102
  (424 shorter events, 93.7 us)
Async XLA Ops:
  2.6 18.5 %collective-permute-start.64 = (f32[2,2,768]{2,1,0:T(2,128)S(1)}, f32[2,2,768]{2,1,0:T(2,128)S(1)}, u32[]{:S(2)}, u32[]{:S(2)}) collective-permute-start(f32[2,2,768]{2,1,0:T(2,128)S(1)} %get-tuple-element.170), channel_id=1, source_target_pairs={{0,1},{1,0},{2,3},{3,2},{4,5},{5,4},{6,7},{7,6},{8,9},{9,8},{10,11... | collective-permute-start | bytes 36872 | tf_op jit(solution)/shard_map/ppermute | solution.py:241
  16.4 21.9 %collective-permute-start = (f32[2,13,768]{2,1,0:T(8,128)S(1)}, f32[2,13,768]{2,1,0:T(8,128)}, u32[]{:S(2)}, u32[]{:S(2)}) collective-permute-start(f32[2,13,768]{2,1,0:T(8,128)S(1)} %get-tuple-element.102), channel_id=1, source_target_pairs={{0,1},{1,0},{2,3},{3,2},{4,5},{5,4},{6,7},{7,6},{8,9},{9,8},{10,11... | collective-permute-start | bytes 239624 | tf_op jit(solution)/shard_map/ppermute | solution.py:241
  33.1 17.5 %collective-permute-start.82 = (bf16[32,2048]{1,0:T(8,128)(2,1)}, bf16[32,2048]{1,0:T(8,128)(2,1)S(1)}, u32[]{:S(2)}, u32[]{:S(2)}) collective-permute-start(bf16[32,2048]{1,0:T(8,128)(2,1)} %shard_map.104.refs_0_), channel_id=1, source_target_pairs={{0,8},{8,0},{16,24},{24,16},{1,9},{9,1},{17,25},{25,17},{2,10},{10... | collective-permute-start | bytes 393224 | tf_op jit(solution)/shard_map/ppermute | solution.py:241
  46.7 11.3 %collective-permute-start.68 = (bf16[2,2,96,256]{3,2,1,0:T(8,128)(2,1)S(1)}, bf16[2,2,96,256]{3,2,1,0:T(8,128)(2,1)S(1)}, u32[]{:S(2)}, u32[]{:S(2)}) collective-permute-start(bf16[2,2,96,256]{3,2,1,0:T(8,128)(2,1)S(1)} %get-tuple-element.172), channel_id=1, source_target_pairs={{0,1},{1,0},{2,3},{3,2},{4,5},{5,4},{6,7},{7,6},{8,9},{9,8},{10,11... | collective-permute-start | bytes 589832 | tf_op jit(solution)/shard_map/ppermute | solution.py:241
  48.8 10.5 %collective-permute-start.69 = (bf16[2,2,96,256]{3,2,1,0:T(8,128)(2,1)S(1)}, bf16[2,2,96,256]{3,2,1,0:T(8,128)(2,1)S(1)}, u32[]{:S(2)}, u32[]{:S(2)}) collective-permute-start(bf16[2,2,96,256]{3,2,1,0:T(8,128)(2,1)S(1)} %get-tuple-element.173), channel_id=1, source_target_pairs={{0,2},{1,3},{2,0},{3,1},{4,6},{5,7},{6,4},{7,5},{8,10},{9,11},{10,... | collective-permute-start | bytes 589832 | tf_op jit(solution)/shard_map/ppermute | solution.py:241
  50.6 15.6 %collective-permute-start.70 = (bf16[2,2,96,256]{3,2,1,0:T(8,128)(2,1)S(1)}, bf16[2,2,96,256]{3,2,1,0:T(8,128)(2,1)S(1)}, u32[]{:S(2)}, u32[]{:S(2)}) collective-permute-start(bf16[2,2,96,256]{3,2,1,0:T(8,128)(2,1)S(1)} %get-tuple-element.174), channel_id=1, source_target_pairs={{0,3},{1,2},{2,1},{3,0},{4,7},{5,6},{6,5},{7,4},{8,11},{9,10},{10,... | collective-permute-start | bytes 589832 | tf_op jit(solution)/shard_map/ppermute | solution.py:241
  51.3 15.8 %collective-permute-start.71 = (bf16[2,2,96,256]{3,2,1,0:T(8,128)(2,1)S(1)}, bf16[2,2,96,256]{3,2,1,0:T(8,128)(2,1)S(1)}, u32[]{:S(2)}, u32[]{:S(2)}) collective-permute-start(bf16[2,2,96,256]{3,2,1,0:T(8,128)(2,1)S(1)} %get-tuple-element.175), channel_id=1, source_target_pairs={{0,4},{1,5},{2,6},{3,7},{4,0},{5,1},{6,2},{7,3},{8,12},{9,13},{10,... | collective-permute-start | bytes 589832 | tf_op jit(solution)/shard_map/ppermute | solution.py:241
  58.0 14.6 %collective-permute-start.72 = (bf16[2,2,96,256]{3,2,1,0:T(8,128)(2,1)S(1)}, bf16[2,2,96,256]{3,2,1,0:T(8,128)(2,1)S(1)}, u32[]{:S(2)}, u32[]{:S(2)}) collective-permute-start(bf16[2,2,96,256]{3,2,1,0:T(8,128)(2,1)S(1)} %get-tuple-element.176), channel_id=1, source_target_pairs={{0,5},{1,4},{2,7},{3,6},{4,1},{5,0},{6,3},{7,2},{8,13},{9,12},{10,... | collective-permute-start | bytes 589832 | tf_op jit(solution)/shard_map/ppermute | solution.py:241
  58.7 13.9 %collective-permute-start.73 = (bf16[2,2,96,256]{3,2,1,0:T(8,128)(2,1)S(1)}, bf16[2,2,96,256]{3,2,1,0:T(8,128)(2,1)S(1)}, u32[]{:S(2)}, u32[]{:S(2)}) collective-permute-start(bf16[2,2,96,256]{3,2,1,0:T(8,128)(2,1)S(1)} %get-tuple-element.177), channel_id=1, source_target_pairs={{0,6},{1,7},{2,4},{3,5},{4,2},{5,3},{6,0},{7,1},{8,14},{9,15},{10,... | collective-permute-start | bytes 589832 | tf_op jit(solution)/shard_map/ppermute | solution.py:241
  60.0 15.0 %collective-permute-start.74 = (bf16[2,2,96,256]{3,2,1,0:T(8,128)(2,1)S(1)}, bf16[2,2,96,256]{3,2,1,0:T(8,128)(2,1)S(1)}, u32[]{:S(2)}, u32[]{:S(2)}) collective-permute-start(bf16[2,2,96,256]{3,2,1,0:T(8,128)(2,1)S(1)} %get-tuple-element.178), channel_id=1, source_target_pairs={{0,7},{1,6},{2,5},{3,4},{4,3},{5,2},{6,1},{7,0},{8,15},{9,14},{10,... | collective-permute-start | bytes 589832 | tf_op jit(solution)/shard_map/ppermute | solution.py:241
  66.9 16.7 %collective-permute-start.57 = (bf16[2,2,96,256]{3,2,1,0:T(8,128)(2,1)S(1)}, bf16[2,2,96,256]{3,2,1,0:T(8,128)(2,1)S(1)}, u32[]{:S(2)}, u32[]{:S(2)}) collective-permute-start(bf16[2,2,96,256]{3,2,1,0:T(8,128)(2,1)S(1)} %get-tuple-element.162), channel_id=1, source_target_pairs={{0,1},{1,0},{2,3},{3,2},{4,5},{5,4},{6,7},{7,6},{8,9},{9,8},{10,11... | collective-permute-start | bytes 589832 | tf_op jit(solution)/shard_map/ppermute | solution.py:241
  67.8 18.4 %collective-permute-start.58 = (bf16[2,2,96,256]{3,2,1,0:T(8,128)(2,1)S(1)}, bf16[2,2,96,256]{3,2,1,0:T(8,128)(2,1)S(1)}, u32[]{:S(2)}, u32[]{:S(2)}) collective-permute-start(bf16[2,2,96,256]{3,2,1,0:T(8,128)(2,1)S(1)} %get-tuple-element.163), channel_id=1, source_target_pairs={{0,2},{1,3},{2,0},{3,1},{4,6},{5,7},{6,4},{7,5},{8,10},{9,11},{10,... | collective-permute-start | bytes 589832 | tf_op jit(solution)/shard_map/ppermute | solution.py:241
  72.7 16.7 %collective-permute-start.59 = (bf16[2,2,96,256]{3,2,1,0:T(8,128)(2,1)S(1)}, bf16[2,2,96,256]{3,2,1,0:T(8,128)(2,1)S(1)}, u32[]{:S(2)}, u32[]{:S(2)}) collective-permute-start(bf16[2,2,96,256]{3,2,1,0:T(8,128)(2,1)S(1)} %get-tuple-element.164), channel_id=1, source_target_pairs={{0,3},{1,2},{2,1},{3,0},{4,7},{5,6},{6,5},{7,4},{8,11},{9,10},{10,... | collective-permute-start | bytes 589832 | tf_op jit(solution)/shard_map/ppermute | solution.py:241
  73.4 16.0 %collective-permute-start.60 = (bf16[2,2,96,256]{3,2,1,0:T(8,128)(2,1)S(1)}, bf16[2,2,96,256]{3,2,1,0:T(8,128)(2,1)S(1)}, u32[]{:S(2)}, u32[]{:S(2)}) collective-permute-start(bf16[2,2,96,256]{3,2,1,0:T(8,128)(2,1)S(1)} %get-tuple-element.165), channel_id=1, source_target_pairs={{0,4},{1,5},{2,6},{3,7},{4,0},{5,1},{6,2},{7,3},{8,12},{9,13},{10,... | collective-permute-start | bytes 589832 | tf_op jit(solution)/shard_map/ppermute | solution.py:241
  83.1 15.6 %collective-permute-start.61 = (bf16[2,2,96,256]{3,2,1,0:T(8,128)(2,1)S(1)}, bf16[2,2,96,256]{3,2,1,0:T(8,128)(2,1)S(1)}, u32[]{:S(2)}, u32[]{:S(2)}) collective-permute-start(bf16[2,2,96,256]{3,2,1,0:T(8,128)(2,1)S(1)} %get-tuple-element.166), channel_id=1, source_target_pairs={{0,5},{1,4},{2,7},{3,6},{4,1},{5,0},{6,3},{7,2},{8,13},{9,12},{10,... | collective-permute-start | bytes 589832 | tf_op jit(solution)/shard_map/ppermute | solution.py:241
  84.4 15.4 %collective-permute-start.62 = (bf16[2,2,96,256]{3,2,1,0:T(8,128)(2,1)S(1)}, bf16[2,2,96,256]{3,2,1,0:T(8,128)(2,1)S(1)}, u32[]{:S(2)}, u32[]{:S(2)}) collective-permute-start(bf16[2,2,96,256]{3,2,1,0:T(8,128)(2,1)S(1)} %get-tuple-element.167), channel_id=1, source_target_pairs={{0,6},{1,7},{2,4},{3,5},{4,2},{5,3},{6,0},{7,1},{8,14},{9,15},{10,... | collective-permute-start | bytes 589832 | tf_op jit(solution)/shard_map/ppermute | solution.py:241
  87.0 13.3 %collective-permute-start.63 = (bf16[2,2,96,256]{3,2,1,0:T(8,128)(2,1)S(1)}, bf16[2,2,96,256]{3,2,1,0:T(8,128)(2,1)S(1)}, u32[]{:S(2)}, u32[]{:S(2)}) collective-permute-start(bf16[2,2,96,256]{3,2,1,0:T(8,128)(2,1)S(1)} %get-tuple-element.168), channel_id=1, source_target_pairs={{0,7},{1,6},{2,5},{3,4},{4,3},{5,2},{6,1},{7,0},{8,15},{9,14},{10,... | collective-permute-start | bytes 589832 | tf_op jit(solution)/shard_map/ppermute | solution.py:241
  89.4 12.1 %collective-permute-start.50 = (bf16[2,2,96,256]{3,2,1,0:T(8,128)(2,1)S(1)}, bf16[2,2,96,256]{3,2,1,0:T(8,128)(2,1)S(1)}, u32[]{:S(2)}, u32[]{:S(2)}) collective-permute-start(bf16[2,2,96,256]{3,2,1,0:T(8,128)(2,1)S(1)} %get-tuple-element.154), channel_id=1, source_target_pairs={{0,1},{1,0},{2,3},{3,2},{4,5},{5,4},{6,7},{7,6},{8,9},{9,8},{10,11... | collective-permute-start | bytes 589832 | tf_op jit(solution)/shard_map/ppermute | solution.py:241
  89.4 13.2 %collective-permute-start.51 = (bf16[2,2,96,256]{3,2,1,0:T(8,128)(2,1)S(1)}, bf16[2,2,96,256]{3,2,1,0:T(8,128)(2,1)S(1)}, u32[]{:S(2)}, u32[]{:S(2)}) collective-permute-start(bf16[2,2,96,256]{3,2,1,0:T(8,128)(2,1)S(1)} %get-tuple-element.155), channel_id=1, source_target_pairs={{0,2},{1,3},{2,0},{3,1},{4,6},{5,7},{6,4},{7,5},{8,10},{9,11},{10,... | collective-permute-start | bytes 589832 | tf_op jit(solution)/shard_map/ppermute | solution.py:241
  98.6 11.3 %collective-permute-start.52 = (bf16[2,2,96,256]{3,2,1,0:T(8,128)(2,1)S(1)}, bf16[2,2,96,256]{3,2,1,0:T(8,128)(2,1)S(1)}, u32[]{:S(2)}, u32[]{:S(2)}) collective-permute-start(bf16[2,2,96,256]{3,2,1,0:T(8,128)(2,1)S(1)} %get-tuple-element.156), channel_id=1, source_target_pairs={{0,3},{1,2},{2,1},{3,0},{4,7},{5,6},{6,5},{7,4},{8,11},{9,10},{10,... | collective-permute-start | bytes 589832 | tf_op jit(solution)/shard_map/ppermute | solution.py:241
  99.8 18.3 %collective-permute-start.53 = (bf16[2,2,96,256]{3,2,1,0:T(8,128)(2,1)S(1)}, bf16[2,2,96,256]{3,2,1,0:T(8,128)(2,1)S(1)}, u32[]{:S(2)}, u32[]{:S(2)}) collective-permute-start(bf16[2,2,96,256]{3,2,1,0:T(8,128)(2,1)S(1)} %get-tuple-element.157), channel_id=1, source_target_pairs={{0,4},{1,5},{2,6},{3,7},{4,0},{5,1},{6,2},{7,3},{8,12},{9,13},{10,... | collective-permute-start | bytes 589832 | tf_op jit(solution)/shard_map/ppermute | solution.py:241
  101.5 19.0 %collective-permute-start.54 = (bf16[2,2,96,256]{3,2,1,0:T(8,128)(2,1)S(1)}, bf16[2,2,96,256]{3,2,1,0:T(8,128)(2,1)S(1)}, u32[]{:S(2)}, u32[]{:S(2)}) collective-permute-start(bf16[2,2,96,256]{3,2,1,0:T(8,128)(2,1)S(1)} %get-tuple-element.158), channel_id=1, source_target_pairs={{0,5},{1,4},{2,7},{3,6},{4,1},{5,0},{6,3},{7,2},{8,13},{9,12},{10,... | collective-permute-start | bytes 589832 | tf_op jit(solution)/shard_map/ppermute | solution.py:241
  102.6 19.1 %collective-permute-start.55 = (bf16[2,2,96,256]{3,2,1,0:T(8,128)(2,1)S(1)}, bf16[2,2,96,256]{3,2,1,0:T(8,128)(2,1)S(1)}, u32[]{:S(2)}, u32[]{:S(2)}) collective-permute-start(bf16[2,2,96,256]{3,2,1,0:T(8,128)(2,1)S(1)} %get-tuple-element.159), channel_id=1, source_target_pairs={{0,6},{1,7},{2,4},{3,5},{4,2},{5,3},{6,0},{7,1},{8,14},{9,15},{10,... | collective-permute-start | bytes 589832 | tf_op jit(solution)/shard_map/ppermute | solution.py:241
  103.8 19.5 %collective-permute-start.56 = (bf16[2,2,96,256]{3,2,1,0:T(8,128)(2,1)S(1)}, bf16[2,2,96,256]{3,2,1,0:T(8,128)(2,1)S(1)}, u32[]{:S(2)}, u32[]{:S(2)}) collective-permute-start(bf16[2,2,96,256]{3,2,1,0:T(8,128)(2,1)S(1)} %get-tuple-element.160), channel_id=1, source_target_pairs={{0,7},{1,6},{2,5},{3,4},{4,3},{5,2},{6,1},{7,0},{8,15},{9,14},{10,... | collective-permute-start | bytes 589832 | tf_op jit(solution)/shard_map/ppermute | solution.py:241
  110.6 14.0 %collective-permute-start.10 = (bf16[2,1,96,256]{3,2,1,0:T(8,128)(2,1)S(1)}, bf16[2,1,96,256]{3,2,1,0:T(8,128)(2,1)S(1)}, u32[]{:S(2)}, u32[]{:S(2)}) collective-permute-start(bf16[2,1,96,256]{3,2,1,0:T(8,128)(2,1)S(1)} %get-tuple-element.110), channel_id=1, source_target_pairs={{0,7},{1,6},{2,5},{3,4},{4,3},{5,2},{6,1},{7,0},{8,15},{9,14},{10,... | collective-permute-start | bytes 294920 | tf_op jit(solution)/shard_map/ppermute | solution.py:241
  118.1 12.7 %collective-permute-start.39 = (bf16[2,2,96,256]{3,2,1,0:T(8,128)(2,1)S(1)}, bf16[2,2,96,256]{3,2,1,0:T(8,128)(2,1)S(1)}, u32[]{:S(2)}, u32[]{:S(2)}) collective-permute-start(bf16[2,2,96,256]{3,2,1,0:T(8,128)(2,1)S(1)} %get-tuple-element.144), channel_id=1, source_target_pairs={{0,1},{1,0},{2,3},{3,2},{4,5},{5,4},{6,7},{7,6},{8,9},{9,8},{10,11... | collective-permute-start | bytes 589832 | tf_op jit(solution)/shard_map/ppermute | solution.py:241
  120.5 11.7 %collective-permute-start.40 = (bf16[2,2,96,256]{3,2,1,0:T(8,128)(2,1)S(1)}, bf16[2,2,96,256]{3,2,1,0:T(8,128)(2,1)S(1)}, u32[]{:S(2)}, u32[]{:S(2)}) collective-permute-start(bf16[2,2,96,256]{3,2,1,0:T(8,128)(2,1)S(1)} %get-tuple-element.145), channel_id=1, source_target_pairs={{0,2},{1,3},{2,0},{3,1},{4,6},{5,7},{6,4},{7,5},{8,10},{9,11},{10,... | collective-permute-start | bytes 589832 | tf_op jit(solution)/shard_map/ppermute | solution.py:241
  122.3 10.7 %collective-permute-start.41 = (bf16[2,2,96,256]{3,2,1,0:T(8,128)(2,1)S(1)}, bf16[2,2,96,256]{3,2,1,0:T(8,128)(2,1)S(1)}, u32[]{:S(2)}, u32[]{:S(2)}) collective-permute-start(bf16[2,2,96,256]{3,2,1,0:T(8,128)(2,1)S(1)} %get-tuple-element.146), channel_id=1, source_target_pairs={{0,3},{1,2},{2,1},{3,0},{4,7},{5,6},{6,5},{7,4},{8,11},{9,10},{10,... | collective-permute-start | bytes 589832 | tf_op jit(solution)/shard_map/ppermute | solution.py:241
  123.3 12.7 %collective-permute-start.42 = (bf16[2,2,96,256]{3,2,1,0:T(8,128)(2,1)S(1)}, bf16[2,2,96,256]{3,2,1,0:T(8,128)(2,1)S(1)}, u32[]{:S(2)}, u32[]{:S(2)}) collective-permute-start(bf16[2,2,96,256]{3,2,1,0:T(8,128)(2,1)S(1)} %get-tuple-element.147), channel_id=1, source_target_pairs={{0,4},{1,5},{2,6},{3,7},{4,0},{5,1},{6,2},{7,3},{8,12},{9,13},{10,... | collective-permute-start | bytes 589832 | tf_op jit(solution)/shard_map/ppermute | solution.py:241
  130.6 20.7 %collective-permute-start.11 = (bf16[2,3,96,256]{3,2,1,0:T(8,128)(2,1)S(1)}, bf16[2,3,96,256]{3,2,1,0:T(8,128)(2,1)S(1)}, u32[]{:S(2)}, u32[]{:S(2)}) collective-permute-start(bf16[2,3,96,256]{3,2,1,0:T(8,128)(2,1)S(1)} %get-tuple-element.112), channel_id=1, source_target_pairs={{0,1},{1,0},{2,3},{3,2},{4,5},{5,4},{6,7},{7,6},{8,9},{9,8},{10,11... | collective-permute-start | bytes 884744 | tf_op jit(solution)/shard_map/ppermute | solution.py:241
  131.4 21.6 %collective-permute-start.12 = (bf16[2,3,96,256]{3,2,1,0:T(8,128)(2,1)S(1)}, bf16[2,3,96,256]{3,2,1,0:T(8,128)(2,1)S(1)}, u32[]{:S(2)}, u32[]{:S(2)}) collective-permute-start(bf16[2,3,96,256]{3,2,1,0:T(8,128)(2,1)S(1)} %get-tuple-element.113), channel_id=1, source_target_pairs={{0,2},{1,3},{2,0},{3,1},{4,6},{5,7},{6,4},{7,5},{8,10},{9,11},{10,... | collective-permute-start | bytes 884744 | tf_op jit(solution)/shard_map/ppermute | solution.py:241
  133.7 11.9 %collective-permute-start.44 = (bf16[2,2,96,256]{3,2,1,0:T(8,128)(2,1)S(1)}, bf16[2,2,96,256]{3,2,1,0:T(8,128)(2,1)S(1)}, u32[]{:S(2)}, u32[]{:S(2)}) collective-permute-start(bf16[2,2,96,256]{3,2,1,0:T(8,128)(2,1)S(1)} %get-tuple-element.149), channel_id=1, source_target_pairs={{0,6},{1,7},{2,4},{3,5},{4,2},{5,3},{6,0},{7,1},{8,14},{9,15},{10,... | collective-permute-start | bytes 589832 | tf_op jit(solution)/shard_map/ppermute | solution.py:241
  136.6 11.4 %collective-permute-start.45 = (bf16[2,2,96,256]{3,2,1,0:T(8,128)(2,1)S(1)}, bf16[2,2,96,256]{3,2,1,0:T(8,128)(2,1)S(1)}, u32[]{:S(2)}, u32[]{:S(2)}) collective-permute-start(bf16[2,2,96,256]{3,2,1,0:T(8,128)(2,1)S(1)} %get-tuple-element.150), channel_id=1, source_target_pairs={{0,7},{1,6},{2,5},{3,4},{4,3},{5,2},{6,1},{7,0},{8,15},{9,14},{10,... | collective-permute-start | bytes 589832 | tf_op jit(solution)/shard_map/ppermute | solution.py:241
  140.9 17.8 %collective-permute-start.13 = (bf16[2,3,96,256]{3,2,1,0:T(8,128)(2,1)S(1)}, bf16[2,3,96,256]{3,2,1,0:T(8,128)(2,1)S(1)}, u32[]{:S(2)}, u32[]{:S(2)}) collective-permute-start(bf16[2,3,96,256]{3,2,1,0:T(8,128)(2,1)S(1)} %get-tuple-element.114), channel_id=1, source_target_pairs={{0,3},{1,2},{2,1},{3,0},{4,7},{5,6},{6,5},{7,4},{8,11},{9,10},{10,... | collective-permute-start | bytes 884744 | tf_op jit(solution)/shard_map/ppermute | solution.py:241
  146.3 22.2 %collective-permute-start.14 = (bf16[2,3,96,256]{3,2,1,0:T(8,128)(2,1)S(1)}, bf16[2,3,96,256]{3,2,1,0:T(8,128)(2,1)S(1)}, u32[]{:S(2)}, u32[]{:S(2)}) collective-permute-start(bf16[2,3,96,256]{3,2,1,0:T(8,128)(2,1)S(1)} %get-tuple-element.115), channel_id=1, source_target_pairs={{0,4},{1,5},{2,6},{3,7},{4,0},{5,1},{6,2},{7,3},{8,12},{9,13},{10,... | collective-permute-start | bytes 884744 | tf_op jit(solution)/shard_map/ppermute | solution.py:241
  148.7 24.7 %collective-permute-start.15 = (bf16[2,3,96,256]{3,2,1,0:T(8,128)(2,1)S(1)}, bf16[2,3,96,256]{3,2,1,0:T(8,128)(2,1)S(1)}, u32[]{:S(2)}, u32[]{:S(2)}) collective-permute-start(bf16[2,3,96,256]{3,2,1,0:T(8,128)(2,1)S(1)} %get-tuple-element.116), channel_id=1, source_target_pairs={{0,5},{1,4},{2,7},{3,6},{4,1},{5,0},{6,3},{7,2},{8,13},{9,12},{10,... | collective-permute-start | bytes 884744 | tf_op jit(solution)/shard_map/ppermute | solution.py:241
  152.0 23.5 %collective-permute-start.16 = (bf16[2,3,96,256]{3,2,1,0:T(8,128)(2,1)S(1)}, bf16[2,3,96,256]{3,2,1,0:T(8,128)(2,1)S(1)}, u32[]{:S(2)}, u32[]{:S(2)}) collective-permute-start(bf16[2,3,96,256]{3,2,1,0:T(8,128)(2,1)S(1)} %get-tuple-element.117), channel_id=1, source_target_pairs={{0,6},{1,7},{2,4},{3,5},{4,2},{5,3},{6,0},{7,1},{8,14},{9,15},{10,... | collective-permute-start | bytes 884744 | tf_op jit(solution)/shard_map/ppermute | solution.py:241
  153.7 24.0 %collective-permute-start.17 = (bf16[2,3,96,256]{3,2,1,0:T(8,128)(2,1)S(1)}, bf16[2,3,96,256]{3,2,1,0:T(8,128)(2,1)S(1)}, u32[]{:S(2)}, u32[]{:S(2)}) collective-permute-start(bf16[2,3,96,256]{3,2,1,0:T(8,128)(2,1)S(1)} %get-tuple-element.118), channel_id=1, source_target_pairs={{0,7},{1,6},{2,5},{3,4},{4,3},{5,2},{6,1},{7,0},{8,15},{9,14},{10,... | collective-permute-start | bytes 884744 | tf_op jit(solution)/shard_map/ppermute | solution.py:241
  159.5 18.9 %collective-permute-start.32 = (bf16[2,4,96,256]{3,2,1,0:T(8,128)(2,1)S(1)}, bf16[2,4,96,256]{3,2,1,0:T(8,128)(2,1)S(1)}, u32[]{:S(2)}, u32[]{:S(2)}) collective-permute-start(bf16[2,4,96,256]{3,2,1,0:T(8,128)(2,1)S(1)} %get-tuple-element.136), channel_id=1, source_target_pairs={{0,1},{1,0},{2,3},{3,2},{4,5},{5,4},{6,7},{7,6},{8,9},{9,8},{10,11... | collective-permute-start | bytes 1179656 | tf_op jit(solution)/shard_map/ppermute | solution.py:241
  169.3 19.0 %collective-permute-start.33 = (bf16[2,4,96,256]{3,2,1,0:T(8,128)(2,1)S(1)}, bf16[2,4,96,256]{3,2,1,0:T(8,128)(2,1)S(1)}, u32[]{:S(2)}, u32[]{:S(2)}) collective-permute-start(bf16[2,4,96,256]{3,2,1,0:T(8,128)(2,1)S(1)} %get-tuple-element.137), channel_id=1, source_target_pairs={{0,2},{1,3},{2,0},{3,1},{4,6},{5,7},{6,4},{7,5},{8,10},{9,11},{10,... | collective-permute-start | bytes 1179656 | tf_op jit(solution)/shard_map/ppermute | solution.py:241
  174.1 15.7 %collective-permute-start.34 = (bf16[2,4,96,256]{3,2,1,0:T(8,128)(2,1)S(1)}, bf16[2,4,96,256]{3,2,1,0:T(8,128)(2,1)S(1)}, u32[]{:S(2)}, u32[]{:S(2)}) collective-permute-start(bf16[2,4,96,256]{3,2,1,0:T(8,128)(2,1)S(1)} %get-tuple-element.138), channel_id=1, source_target_pairs={{0,3},{1,2},{2,1},{3,0},{4,7},{5,6},{6,5},{7,4},{8,11},{9,10},{10,... | collective-permute-start | bytes 1179656 | tf_op jit(solution)/shard_map/ppermute | solution.py:241
  176.2 20.4 %collective-permute-start.35 = (bf16[2,4,96,256]{3,2,1,0:T(8,128)(2,1)S(1)}, bf16[2,4,96,256]{3,2,1,0:T(8,128)(2,1)S(1)}, u32[]{:S(2)}, u32[]{:S(2)}) collective-permute-start(bf16[2,4,96,256]{3,2,1,0:T(8,128)(2,1)S(1)} %get-tuple-element.139), channel_id=1, source_target_pairs={{0,4},{1,5},{2,6},{3,7},{4,0},{5,1},{6,2},{7,3},{8,12},{9,13},{10,... | collective-permute-start | bytes 1179656 | tf_op jit(solution)/shard_map/ppermute | solution.py:241
  178.4 24.4 %collective-permute-start.36 = (bf16[2,4,96,256]{3,2,1,0:T(8,128)(2,1)S(1)}, bf16[2,4,96,256]{3,2,1,0:T(8,128)(2,1)S(1)}, u32[]{:S(2)}, u32[]{:S(2)}) collective-permute-start(bf16[2,4,96,256]{3,2,1,0:T(8,128)(2,1)S(1)} %get-tuple-element.140), channel_id=1, source_target_pairs={{0,5},{1,4},{2,7},{3,6},{4,1},{5,0},{6,3},{7,2},{8,13},{9,12},{10,... | collective-permute-start | bytes 1179656 | tf_op jit(solution)/shard_map/ppermute | solution.py:241
  178.4 25.6 %collective-permute-start.37 = (bf16[2,4,96,256]{3,2,1,0:T(8,128)(2,1)S(1)}, bf16[2,4,96,256]{3,2,1,0:T(8,128)(2,1)S(1)}, u32[]{:S(2)}, u32[]{:S(2)}) collective-permute-start(bf16[2,4,96,256]{3,2,1,0:T(8,128)(2,1)S(1)} %get-tuple-element.141), channel_id=1, source_target_pairs={{0,6},{1,7},{2,4},{3,5},{4,2},{5,3},{6,0},{7,1},{8,14},{9,15},{10,... | collective-permute-start | bytes 1179656 | tf_op jit(solution)/shard_map/ppermute | solution.py:241
  189.1 48.7 %collective-permute-start.25 = (bf16[2,8,96,256]{3,2,1,0:T(8,128)(2,1)S(1)}, bf16[2,8,96,256]{3,2,1,0:T(8,128)(2,1)S(1)}, u32[]{:S(2)}, u32[]{:S(2)}) collective-permute-start(bf16[2,8,96,256]{3,2,1,0:T(8,128)(2,1)S(1)} %get-tuple-element.128), channel_id=1, source_target_pairs={{0,1},{1,0},{2,3},{3,2},{4,5},{5,4},{6,7},{7,6},{8,9},{9,8},{10,11... | collective-permute-start | bytes 2359304 | tf_op jit(solution)/shard_map/ppermute | solution.py:241
  190.5 49.2 %collective-permute-start.26 = (bf16[2,8,96,256]{3,2,1,0:T(8,128)(2,1)S(1)}, bf16[2,8,96,256]{3,2,1,0:T(8,128)(2,1)S(1)}, u32[]{:S(2)}, u32[]{:S(2)}) collective-permute-start(bf16[2,8,96,256]{3,2,1,0:T(8,128)(2,1)S(1)} %get-tuple-element.129), channel_id=1, source_target_pairs={{0,2},{1,3},{2,0},{3,1},{4,6},{5,7},{6,4},{7,5},{8,10},{9,11},{10,... | collective-permute-start | bytes 2359304 | tf_op jit(solution)/shard_map/ppermute | solution.py:241
  196.7 43.6 %collective-permute-start.27 = (bf16[2,8,96,256]{3,2,1,0:T(8,128)(2,1)S(1)}, bf16[2,8,96,256]{3,2,1,0:T(8,128)(2,1)S(1)}, u32[]{:S(2)}, u32[]{:S(2)}) collective-permute-start(bf16[2,8,96,256]{3,2,1,0:T(8,128)(2,1)S(1)} %get-tuple-element.130), channel_id=1, source_target_pairs={{0,3},{1,2},{2,1},{3,0},{4,7},{5,6},{6,5},{7,4},{8,11},{9,10},{10,... | collective-permute-start | bytes 2359304 | tf_op jit(solution)/shard_map/ppermute | solution.py:241
  202.8 38.0 %collective-permute-start.28 = (bf16[2,8,96,256]{3,2,1,0:T(8,128)(2,1)S(1)}, bf16[2,8,96,256]{3,2,1,0:T(8,128)(2,1)S(1)}, u32[]{:S(2)}, u32[]{:S(2)}) collective-permute-start(bf16[2,8,96,256]{3,2,1,0:T(8,128)(2,1)S(1)} %get-tuple-element.131), channel_id=1, source_target_pairs={{0,4},{1,5},{2,6},{3,7},{4,0},{5,1},{6,2},{7,3},{8,12},{9,13},{10,... | collective-permute-start | bytes 2359304 | tf_op jit(solution)/shard_map/ppermute | solution.py:241
  204.0 32.5 %collective-permute-start.38 = (bf16[2,4,96,256]{3,2,1,0:T(8,128)(2,1)S(1)}, bf16[2,4,96,256]{3,2,1,0:T(8,128)(2,1)S(1)}, u32[]{:S(2)}, u32[]{:S(2)}) collective-permute-start(bf16[2,4,96,256]{3,2,1,0:T(8,128)(2,1)S(1)} %get-tuple-element.142), channel_id=1, source_target_pairs={{0,7},{1,6},{2,5},{3,4},{4,3},{5,2},{6,1},{7,0},{8,15},{9,14},{10,... | collective-permute-start | bytes 1179656 | tf_op jit(solution)/shard_map/ppermute | solution.py:241
  237.3 52.7 %collective-permute-start.29 = (bf16[2,8,96,256]{3,2,1,0:T(8,128)(2,1)S(1)}, bf16[2,8,96,256]{3,2,1,0:T(8,128)(2,1)S(1)}, u32[]{:S(2)}, u32[]{:S(2)}) collective-permute-start(bf16[2,8,96,256]{3,2,1,0:T(8,128)(2,1)S(1)} %get-tuple-element.132), channel_id=1, source_target_pairs={{0,5},{1,4},{2,7},{3,6},{4,1},{5,0},{6,3},{7,2},{8,13},{9,12},{10,... | collective-permute-start | bytes 2359304 | tf_op jit(solution)/shard_map/ppermute | solution.py:241
  237.8 54.2 %collective-permute-start.30 = (bf16[2,8,96,256]{3,2,1,0:T(8,128)(2,1)S(1)}, bf16[2,8,96,256]{3,2,1,0:T(8,128)(2,1)S(1)}, u32[]{:S(2)}, u32[]{:S(2)}) collective-permute-start(bf16[2,8,96,256]{3,2,1,0:T(8,128)(2,1)S(1)} %get-tuple-element.133), channel_id=1, source_target_pairs={{0,6},{1,7},{2,4},{3,5},{4,2},{5,3},{6,0},{7,1},{8,14},{9,15},{10,... | collective-permute-start | bytes 2359304 | tf_op jit(solution)/shard_map/ppermute | solution.py:241
  239.7 53.9 %collective-permute-start.31 = (bf16[2,8,96,256]{3,2,1,0:T(8,128)(2,1)S(1)}, bf16[2,8,96,256]{3,2,1,0:T(8,128)(2,1)S(1)}, u32[]{:S(2)}, u32[]{:S(2)}) collective-permute-start(bf16[2,8,96,256]{3,2,1,0:T(8,128)(2,1)S(1)} %get-tuple-element.134), channel_id=1, source_target_pairs={{0,7},{1,6},{2,5},{3,4},{4,3},{5,2},{6,1},{7,0},{8,15},{9,14},{10,... | collective-permute-start | bytes 2359304 | tf_op jit(solution)/shard_map/ppermute | solution.py:241
  240.3 54.8 %collective-permute-start.18 = (bf16[2,8,96,256]{3,2,1,0:T(8,128)(2,1)S(1)}, bf16[2,8,96,256]{3,2,1,0:T(8,128)(2,1)S(1)}, u32[]{:S(2)}, u32[]{:S(2)}) collective-permute-start(bf16[2,8,96,256]{3,2,1,0:T(8,128)(2,1)S(1)} %get-tuple-element.120), channel_id=1, source_target_pairs={{0,1},{1,0},{2,3},{3,2},{4,5},{5,4},{6,7},{7,6},{8,9},{9,8},{10,11... | collective-permute-start | bytes 2359304 | tf_op jit(solution)/shard_map/ppermute | solution.py:241
  241.8 55.9 %collective-permute-start.19 = (bf16[2,8,96,256]{3,2,1,0:T(8,128)(2,1)S(1)}, bf16[2,8,96,256]{3,2,1,0:T(8,128)(2,1)S(1)}, u32[]{:S(2)}, u32[]{:S(2)}) collective-permute-start(bf16[2,8,96,256]{3,2,1,0:T(8,128)(2,1)S(1)} %get-tuple-element.121), channel_id=1, source_target_pairs={{0,2},{1,3},{2,0},{3,1},{4,6},{5,7},{6,4},{7,5},{8,10},{9,11},{10,... | collective-permute-start | bytes 2359304 | tf_op jit(solution)/shard_map/ppermute | solution.py:241
  290.9 32.1 %collective-permute-start.20 = (bf16[2,8,96,256]{3,2,1,0:T(8,128)(2,1)}, bf16[2,8,96,256]{3,2,1,0:T(8,128)(2,1)}, u32[]{:S(2)}, u32[]{:S(2)}) collective-permute-start(bf16[2,8,96,256]{3,2,1,0:T(8,128)(2,1)} %get-tuple-element.122), channel_id=1, source_target_pairs={{0,3},{1,2},{2,1},{3,0},{4,7},{5,6},{6,5},{7,4},{8,11},{9,10},{10,... | collective-permute-start | bytes 2359304 | tf_op jit(solution)/shard_map/ppermute | solution.py:241
  292.9 54.4 %collective-permute-start.21 = (bf16[2,8,96,256]{3,2,1,0:T(8,128)(2,1)}, bf16[2,8,96,256]{3,2,1,0:T(8,128)(2,1)}, u32[]{:S(2)}, u32[]{:S(2)}) collective-permute-start(bf16[2,8,96,256]{3,2,1,0:T(8,128)(2,1)} %get-tuple-element.123), channel_id=1, source_target_pairs={{0,4},{1,5},{2,6},{3,7},{4,0},{5,1},{6,2},{7,3},{8,12},{9,13},{10,... | collective-permute-start | bytes 2359304 | tf_op jit(solution)/shard_map/ppermute | solution.py:241
  294.5 67.5 %collective-permute-start.22 = (bf16[2,8,96,256]{3,2,1,0:T(8,128)(2,1)}, bf16[2,8,96,256]{3,2,1,0:T(8,128)(2,1)}, u32[]{:S(2)}, u32[]{:S(2)}) collective-permute-start(bf16[2,8,96,256]{3,2,1,0:T(8,128)(2,1)} %get-tuple-element.124), channel_id=1, source_target_pairs={{0,5},{1,4},{2,7},{3,6},{4,1},{5,0},{6,3},{7,2},{8,13},{9,12},{10,... | collective-permute-start | bytes 2359304 | tf_op jit(solution)/shard_map/ppermute | solution.py:241
  295.9 66.7 %collective-permute-start.23 = (bf16[2,8,96,256]{3,2,1,0:T(8,128)(2,1)}, bf16[2,8,96,256]{3,2,1,0:T(8,128)(2,1)}, u32[]{:S(2)}, u32[]{:S(2)}) collective-permute-start(bf16[2,8,96,256]{3,2,1,0:T(8,128)(2,1)} %get-tuple-element.125), channel_id=1, source_target_pairs={{0,6},{1,7},{2,4},{3,5},{4,2},{5,3},{6,0},{7,1},{8,14},{9,15},{10,... | collective-permute-start | bytes 2359304 | tf_op jit(solution)/shard_map/ppermute | solution.py:241
  298.6 65.7 %collective-permute-start.24 = (bf16[2,8,96,256]{3,2,1,0:T(8,128)(2,1)}, bf16[2,8,96,256]{3,2,1,0:T(8,128)(2,1)}, u32[]{:S(2)}, u32[]{:S(2)}) collective-permute-start(bf16[2,8,96,256]{3,2,1,0:T(8,128)(2,1)} %get-tuple-element.126), channel_id=1, source_target_pairs={{0,7},{1,6},{2,5},{3,4},{4,3},{5,2},{6,1},{7,0},{8,15},{9,14},{10,... | collective-permute-start | bytes 2359304 | tf_op jit(solution)/shard_map/ppermute | solution.py:241
  322.9 63.4 %collective-permute-start.5 = (bf16[2,1,96,256]{3,2,1,0:T(8,128)(2,1)S(1)}, bf16[2,1,96,256]{3,2,1,0:T(8,128)(2,1)S(1)}, u32[]{:S(2)}, u32[]{:S(2)}) collective-permute-start(bf16[2,1,96,256]{3,2,1,0:T(8,128)(2,1)S(1)} %copy-done.128), channel_id=1, source_target_pairs={{0,2},{1,3},{2,0},{3,1},{4,6},{5,7},{6,4},{7,5},{8,10},{9,11},{10,... | collective-permute-start | bytes 294920 | tf_op jit(solution)/shard_map/ppermute | solution.py:241
  347.3 39.0 %collective-permute-start.6 = (bf16[2,1,96,256]{3,2,1,0:T(8,128)(2,1)S(1)}, bf16[2,1,96,256]{3,2,1,0:T(8,128)(2,1)S(1)}, u32[]{:S(2)}, u32[]{:S(2)}) collective-permute-start(bf16[2,1,96,256]{3,2,1,0:T(8,128)(2,1)S(1)} %copy-done.126), channel_id=1, source_target_pairs={{0,3},{1,2},{2,1},{3,0},{4,7},{5,6},{6,5},{7,4},{8,11},{9,10},{10,... | collective-permute-start | bytes 294920 | tf_op jit(solution)/shard_map/ppermute | solution.py:241
  362.0 24.3 %collective-permute-start.7 = (bf16[2,1,96,256]{3,2,1,0:T(8,128)(2,1)S(1)}, bf16[2,1,96,256]{3,2,1,0:T(8,128)(2,1)S(1)}, u32[]{:S(2)}, u32[]{:S(2)}) collective-permute-start(bf16[2,1,96,256]{3,2,1,0:T(8,128)(2,1)S(1)} %copy-done.124), channel_id=1, source_target_pairs={{0,4},{1,5},{2,6},{3,7},{4,0},{5,1},{6,2},{7,3},{8,12},{9,13},{10,... | collective-permute-start | bytes 294920 | tf_op jit(solution)/shard_map/ppermute | solution.py:241
  362.7 23.7 %collective-permute-start.8 = (bf16[2,1,96,256]{3,2,1,0:T(8,128)(2,1)S(1)}, bf16[2,1,96,256]{3,2,1,0:T(8,128)(2,1)S(1)}, u32[]{:S(2)}, u32[]{:S(2)}) collective-permute-start(bf16[2,1,96,256]{3,2,1,0:T(8,128)(2,1)S(1)} %copy-done.122), channel_id=1, source_target_pairs={{0,5},{1,4},{2,7},{3,6},{4,1},{5,0},{6,3},{7,2},{8,13},{9,12},{10,... | collective-permute-start | bytes 294920 | tf_op jit(solution)/shard_map/ppermute | solution.py:241
  364.3 22.0 %collective-permute-start.9 = (bf16[2,1,96,256]{3,2,1,0:T(8,128)(2,1)S(1)}, bf16[2,1,96,256]{3,2,1,0:T(8,128)(2,1)S(1)}, u32[]{:S(2)}, u32[]{:S(2)}) collective-permute-start(bf16[2,1,96,256]{3,2,1,0:T(8,128)(2,1)S(1)} %copy-done.120), channel_id=1, source_target_pairs={{0,6},{1,7},{2,4},{3,5},{4,2},{5,3},{6,0},{7,1},{8,14},{9,15},{10,... | collective-permute-start | bytes 294920 | tf_op jit(solution)/shard_map/ppermute | solution.py:241
  (163 other events, 1178.0 us)

commit v5 on v4

--- a/solution.py
+++ b/solution.py
@@ -139,26 +139,37 @@
     _, count, width, rows = pieces[0].shape
 
     def kernel(*refs):
-        ins, outs, left = refs[:size], refs[-3:-1], refs[-1]
-        me = lax.axis_index("zero")
-        copies = []
-        for k in range(size):
+        ins, outs, (held, arrived, left) = refs[:size], refs[-5:-3], refs[-3:]
+        me = lax.axis_index("zero")
+        places = [(side, k) for side in range(2) for k in range(size)]
+
+        def arrival(side, k):
+            return pltpu.make_async_copy(ins[k].at[side], held.at[k, side], arrived.at[k, side])
+
+        def departure(side, k):
             offset = pl.multiple_of(lax.bitwise_xor(me, k) * rows, rows)
-            for side in range(2):
-                place = outs[side].at[pl.ds(first, count), :, pl.ds(offset, rows)]
-                copies.append(pltpu.make_async_copy(ins[k].at[side], place, left.at[k, side]))
-        for copy in copies:
-            copy.start()
-        for copy in copies:
-            copy.wait()
-
-    return pl.pallas_call(
-        kernel,
-        in_specs=[pl.BlockSpec(memory_space=pltpu.VMEM)] * size + [pl.BlockSpec(memory_space=pl.ANY)] * 2,
+            place = outs[side].at[pl.ds(first, count), :, pl.ds(offset, rows)]
+            return pltpu.make_async_copy(held.at[k, side], place, left.at[k, side])
+
+        for place in places:
+            arrival(*place).start()
+        for place in places:
+            arrival(*place).wait()
+            departure(*place).start()
+        for place in places:
+            departure(*place).wait()
+
+    return pl.pallas_call(
+        kernel,
+        in_specs=[pl.BlockSpec(memory_space=pl.ANY)] * (size + 2),
         out_specs=[pl.BlockSpec(memory_space=pl.ANY)] * 2,
         out_shape=[jax.ShapeDtypeStruct(x.shape, x.dtype) for x in outputs],
         input_output_aliases={size + n: n for n in range(2)},
-        scratch_shapes=[pltpu.SemaphoreType.DMA((size, 2))],
+        scratch_shapes=[
+            pltpu.VMEM((size, 2, count, width, rows), jnp.bfloat16),
+            pltpu.SemaphoreType.DMA((size, 2)),
+            pltpu.SemaphoreType.DMA((size, 2)),
+        ],
         compiler_params=granted(44),
         cost_estimate=cost(count * width * rows * size, 8 * count * width * rows * size),
     )(*pieces, *outputs)

time: 391 us -> 392 us (level)
  no operation moved by 1% of the time
where the time goes in v5:
time: 392 us; the launch traced here: 389 us
  waiting for transfers between devices  167 us (43%)
  starting transfers between devices  81.5 us (21%)
  Pallas kernels  77.1 us (20%)
  local copies, waits for them, and re-layouts  58.8 us (15%)
    ppermute x85, waiting for transfers between devices, send(): return lax.ppermute(x, axis, xor_pairs(count, k))  167 us
    ppermute x85, starting transfers between devices, send(): return lax.ppermute(x, axis, xor_pairs(count, k))  81.5 us
    unnamed x284, local copies, waits for them, and re-layouts  58.2 us
    pallas_call x6, Pallas kernels, scaled_pieces(): pl.pallas_call(kernel, grid=(count,), in_specs=[weights, weights] + [pl.B...  28.9 us
    pallas_call x8, Pallas kernels, assembled(): pl.pallas_call(kernel, grid=(count,), in_specs=[piece] * size + [pl.Block...  22.6 us
    pallas_call x3, Pallas kernels, square_sums(): pl.pallas_call(kernel, in_specs=[pl.BlockSpec(memory_space=pl.ANY)] * 2,...  18.1 us
  transfers between devices with their start and end apart: 85, of which 20 were waited for; matrix products, arithmetic and copies ran while one was open for 1% of the time, Pallas kernels for 19%

profile of v5, /device:TPU:0, one launch (start us, length us, event | category | flops | bytes accessed | tf_op | source)
XLA Modules:
  0.0 388.7 jit_solution(12606500184525531383)
XLA Ops:
  0.6 2.0 shard_map.93
  3.2 13.2 %shard_map.83 = (f32[2,13,768]{2,1,0:T(8,128)S(1)}, f32[2,13,768]{2,1,0:T(8,128)S(1)}) custom-call(f32[32,256,768]{2,1,0:T(8,128)} %refs_0_.5, f32[32,256,768]{2,1,0:T(8,128)} %refs_1_.5), custom_call_target="tpu_custom_call" | custom-call | flops 20447232 | bytes 40894464 | tf_op jit(solution)/shard_map/pallas_call | solution.py:66
  16.5 3.0 collective-permute-start.76
  19.5 1.5 collective-permute-start.78
  21.1 2.9 shard_map.90
  24.1 2.7 copy-done
  28.5 1.9 collective-permute-start.65
  31.6 1.5 shard_map.104.refs_0_
  33.1 1.6 collective-permute-start.82
  35.3 1.5 collective-permute-start.66
  36.9 1.4 collective-permute-start.67
  38.3 1.5 collective-permute-start.48
  41.5 2.6 collective-permute-start.83
  44.1 1.4 collective-permute-start.49
  46.7 2.1 collective-permute-done.49.refs_3_
  48.8 1.6 collective-permute-start.69
  51.7 5.7 %collective-permute-done.84.refs_3_ = bf16[32,2048]{1,0:T(8,128)(2,1)S(1)} collective-permute-done((bf16[32,2048]{1,0:T(8,128)(2,1)}, bf16[32,2048]{1,0:T(8,128)(2,1)S(1)}, u32[]{:S(2)}, u32[]{:S(2)}) %collective-permute-start.84) | collective-permute-done | bytes 131104 | tf_op jit(solution)/shard_map/ppermute | solution.py:252
  60.0 2.2 collective-permute-start.74
  62.3 2.8 copy-done.1
  68.3 4.4 %collective-permute-done.72.refs_5_ = bf16[2,2,96,256]{3,2,1,0:T(8,128)(2,1)S(1)} collective-permute-done((bf16[2,2,96,256]{3,2,1,0:T(8,128)(2,1)S(1)}, bf16[2,2,96,256]{3,2,1,0:T(8,128)(2,1)S(1)}, u32[]{:S(2)}, u32[]{:S(2)}) %collective-permute-start.72) | collective-permute-done | bytes 196640 | tf_op jit(solution)/shard_map/ppermute | solution.py:252
  73.4 1.5 collective-permute-start.60
  76.1 6.9 %collective-permute-done.2 = f32[2,13,768]{2,1,0:T(8,128)S(1)} collective-permute-done((f32[2,13,768]{2,1,0:T(8,128)S(1)}, f32[2,13,768]{2,1,0:T(8,128)S(1)}, u32[]{:S(2)}, u32[]{:S(2)}) %collective-permute-start.2) | collective-permute-done | bytes 79904 | tf_op jit(solution)/shard_map/ppermute | solution.py:252
  84.4 1.9 collective-permute-start.62
  90.8 7.8 %collective-permute-done.61.refs_5_ = bf16[2,2,96,256]{3,2,1,0:T(8,128)(2,1)S(1)} collective-permute-done((bf16[2,2,96,256]{3,2,1,0:T(8,128)(2,1)S(1)}, bf16[2,2,96,256]{3,2,1,0:T(8,128)(2,1)S(1)}, u32[]{:S(2)}, u32[]{:S(2)}) %collective-permute-start.61) | collective-permute-done | bytes 196640 | tf_op jit(solution)/shard_map/ppermute | solution.py:252
  104.9 1.7 shard_map.84
  110.6 1.5 collective-permute-start.10
  112.0 2.3 shard_map.89
  115.0 3.1 collective-permute-done.53.refs_4_
  118.1 2.5 collective-permute-done.54.refs_5_
  125.6 3.6 shard_map.85
  133.7 2.2 collective-permute-start.44
  137.4 2.9 collective-permute-done.43.refs_5_
  140.9 1.6 collective-permute-start.13
  142.5 3.1 collective-permute-done.44.refs_6_
  148.7 2.5 collective-permute-start.15
  154.6 4.1 %shard_map.88 = (bf16[2,4,96,256]{3,2,1,0:T(8,128)(2,1)S(1)}, bf16[2,4,96,256]{3,2,1,0:T(8,128)(2,1)S(1)}, bf16[2,4,96,256]{3,2,1,0:T(8,128)(2,1)S(1)}, bf16[2,4...) custom-call(f32[32,256,768]{2,1,0:T(8,128)} %refs_0_.5, ...), custom_call_target="tpu_custom_call" | custom-call | flops 3145728 | bytes 9437184 | tf_op jit(solution)/shard_map/pallas_call | solution.py:98
  160.6 7.9 %collective-permute-done.14.refs_4_ = bf16[2,3,96,256]{3,2,1,0:T(8,128)(2,1)S(1)} collective-permute-done((bf16[2,3,96,256]{3,2,1,0:T(8,128)(2,1)S(1)}, bf16[2,3,96,256]{3,2,1,0:T(8,128)(2,1)S(1)}, u32[]{:S(2)}, u32[]{:S(2)}) %collective-permute-start.14) | collective-permute-done | bytes 294944 | tf_op jit(solution)/shard_map/ppermute | solution.py:252
  170.2 3.2 collective-permute-done.15.refs_5_
  176.2 1.5 collective-permute-start.35
  178.4 1.9 collective-permute-start.37
  180.3 7.9 %shard_map.87 = (bf16[2,8,96,256]{3,2,1,0:T(8,128)(2,1)S(1)}, bf16[2,8,96,256]{3,2,1,0:T(8,128)(2,1)S(1)}, bf16[2,8,96,256]{3,2,1,0:T(8,128)(2,1)S(1)}, bf16[2,8...) custom-call(f32[32,256,768]{2,1,0:T(8,128)} %refs_0_.5, ...), custom_call_target="tpu_custom_call" | custom-call | flops 6291456 | bytes 18874368 | tf_op jit(solution)/shard_map/pallas_call | solution.py:98
  191.2 5.5 %collective-permute-done.35.refs_4_ = bf16[2,4,96,256]{3,2,1,0:T(8,128)(2,1)S(1)} collective-permute-done((bf16[2,4,96,256]{3,2,1,0:T(8,128)(2,1)S(1)}, bf16[2,4,96,256]{3,2,1,0:T(8,128)(2,1)S(1)}, u32[]{:S(2)}, u32[]{:S(2)}) %collective-permute-start.35) | collective-permute-done | bytes 393248 | tf_op jit(solution)/shard_map/ppermute | solution.py:252
  196.7 6.2 %collective-permute-done.36.refs_5_ = bf16[2,4,96,256]{3,2,1,0:T(8,128)(2,1)S(1)} collective-permute-done((bf16[2,4,96,256]{3,2,1,0:T(8,128)(2,1)S(1)}, bf16[2,4,96,256]{3,2,1,0:T(8,128)(2,1)S(1)}, u32[]{:S(2)}, u32[]{:S(2)}) %collective-permute-start.36) | collective-permute-done | bytes 393248 | tf_op jit(solution)/shard_map/ppermute | solution.py:252
  204.0 1.9 collective-permute-start.38
  206.0 9.4 %shard_map.86 = (bf16[2,8,96,256]{3,2,1,0:T(8,128)(2,1)S(1)}, bf16[2,8,96,256]{3,2,1,0:T(8,128)(2,1)S(1)}, bf16[2,8,96,256]{3,2,1,0:T(8,128)(2,1)S(1)}, bf16[2,8...) custom-call(f32[32,256,768]{2,1,0:T(8,128)} %refs_0_.5, ...), custom_call_target="tpu_custom_call" | custom-call | flops 6291456 | bytes 18874368 | tf_op jit(solution)/shard_map/pallas_call | solution.py:98
  216.2 20.3 %collective-permute-done.38.refs_7_ = bf16[2,4,96,256]{3,2,1,0:T(8,128)(2,1)S(1)} collective-permute-done((bf16[2,4,96,256]{3,2,1,0:T(8,128)(2,1)S(1)}, bf16[2,4,96,256]{3,2,1,0:T(8,128)(2,1)S(1)}, u32[]{:S(2)}, u32[]{:S(2)}) %collective-permute-start.38) | collective-permute-done | bytes 393248 | tf_op jit(solution)/shard_map/ppermute | solution.py:252
  237.8 1.9 collective-permute-start.30
  242.7 47.3 %collective-permute-done.29.refs_5_ = bf16[2,8,96,256]{3,2,1,0:T(8,128)(2,1)S(1)} collective-permute-done((bf16[2,8,96,256]{3,2,1,0:T(8,128)(2,1)S(1)}, bf16[2,8,96,256]{3,2,1,0:T(8,128)(2,1)S(1)}, u32[]{:S(2)}, u32[]{:S(2)}) %collective-permute-start.29) | collective-permute-done | bytes 786464 | tf_op jit(solution)/shard_map/ppermute | solution.py:252
  295.9 1.7 collective-permute-start.23
  298.6 1.4 collective-permute-start.24
  300.9 2.1 shard_map.105
  319.4 1.4 shard_map.96
  321.4 1.4 shard_map.97
  322.9 1.6 collective-permute-start.5
  324.5 22.8 %collective-permute-done.21.refs_4_ = bf16[2,8,96,256]{3,2,1,0:T(8,128)(2,1)} collective-permute-done((bf16[2,8,96,256]{3,2,1,0:T(8,128)(2,1)}, bf16[2,8,96,256]{3,2,1,0:T(8,128)(2,1)}, u32[]{:S(2)}, u32[]{:S(2)}) %collective-permute-start.21) | collective-permute-done | bytes 786464 | tf_op jit(solution)/shard_map/ppermute | solution.py:252
  347.3 14.7 %collective-permute-done.22.refs_5_ = bf16[2,8,96,256]{3,2,1,0:T(8,128)(2,1)} collective-permute-done((bf16[2,8,96,256]{3,2,1,0:T(8,128)(2,1)}, bf16[2,8,96,256]{3,2,1,0:T(8,128)(2,1)}, u32[]{:S(2)}, u32[]{:S(2)}) %collective-permute-start.22) | collective-permute-done | bytes 786464 | tf_op jit(solution)/shard_map/ppermute | solution.py:252
  362.7 1.6 collective-permute-start.8
  364.3 1.6 collective-permute-start.9
  366.7 1.4 shard_map.98
  369.0 2.5 shard_map.99
  371.7 4.5 %shard_map.100 = (bf16[32,96,2048]{2,1,0:T(8,128)(2,1)}, bf16[32,96,2048]{2,1,0:T(8,128)(2,1)}) custom-call(bf16[2,8,96,256]{3,2,1,0:T(8,128)(2,1)S(1)} %get-tuple-element.127.refs_0_, bf16[2,8,96,256]{3,2,1,0:T(8,128)(2,1)S(1)} %collective-permute-done.25.refs_1_, ...), custom_call_target="tpu_custom_call", output_to_operand_aliasing={{0}: (8, {}), {1}: (9, {})} | custom-call | flops 1572864 | bytes 12582912 | tf_op jit(solution)/shard_map/pallas_call | solution.py:193
  376.3 7.7 %shard_map.101 = (bf16[32,96,2048]{2,1,0:T(8,128)(2,1)}, bf16[32,96,2048]{2,1,0:T(8,128)(2,1)}) custom-call(bf16[2,8,96,256]{3,2,1,0:T(8,128)(2,1)S(1)} %copy-done.5, bf16[2,8,96,256]{3,2,1,0:T(8,128)(2,1)S(1)} %copy-done.11, bf16[2,8,96,256]{3,2,1,0:T(8,128)(2,1)S(1)} %copy-done.15, ...), custom_call_target="tpu_custom_call", output_to_operand_aliasing={{0}: (8, {}), {1}: (9, {})} | custom-call | flops 1572864 | bytes 12582912 | tf_op jit(solution)/shard_map/pallas_call | solution.py:193
  384.2 2.1 shard_map.102
  386.4 2.2 shard_map.103
  (424 shorter events, 94.1 us)
Async XLA Ops:
  2.6 18.5 %collective-permute-start.64 = (f32[2,2,768]{2,1,0:T(2,128)S(1)}, f32[2,2,768]{2,1,0:T(2,128)S(1)}, u32[]{:S(2)}, u32[]{:S(2)}) collective-permute-start(f32[2,2,768]{2,1,0:T(2,128)S(1)} %get-tuple-element.170), channel_id=1, source_target_pairs={{0,1},{1,0},{2,3},{3,2},{4,5},{5,4},{6,7},{7,6},{8,9},{9,8},{10,11... | collective-permute-start | bytes 36872 | tf_op jit(solution)/shard_map/ppermute | solution.py:252
  16.4 21.9 %collective-permute-start = (f32[2,13,768]{2,1,0:T(8,128)S(1)}, f32[2,13,768]{2,1,0:T(8,128)}, u32[]{:S(2)}, u32[]{:S(2)}) collective-permute-start(f32[2,13,768]{2,1,0:T(8,128)S(1)} %get-tuple-element.102), channel_id=1, source_target_pairs={{0,1},{1,0},{2,3},{3,2},{4,5},{5,4},{6,7},{7,6},{8,9},{9,8},{10,11... | collective-permute-start | bytes 239624 | tf_op jit(solution)/shard_map/ppermute | solution.py:252
  33.1 17.5 %collective-permute-start.82 = (bf16[32,2048]{1,0:T(8,128)(2,1)}, bf16[32,2048]{1,0:T(8,128)(2,1)S(1)}, u32[]{:S(2)}, u32[]{:S(2)}) collective-permute-start(bf16[32,2048]{1,0:T(8,128)(2,1)} %shard_map.104.refs_0_), channel_id=1, source_target_pairs={{0,8},{8,0},{16,24},{24,16},{1,9},{9,1},{17,25},{25,17},{2,10},{10... | collective-permute-start | bytes 393224 | tf_op jit(solution)/shard_map/ppermute | solution.py:252
  46.7 11.3 %collective-permute-start.68 = (bf16[2,2,96,256]{3,2,1,0:T(8,128)(2,1)S(1)}, bf16[2,2,96,256]{3,2,1,0:T(8,128)(2,1)S(1)}, u32[]{:S(2)}, u32[]{:S(2)}) collective-permute-start(bf16[2,2,96,256]{3,2,1,0:T(8,128)(2,1)S(1)} %get-tuple-element.172), channel_id=1, source_target_pairs={{0,1},{1,0},{2,3},{3,2},{4,5},{5,4},{6,7},{7,6},{8,9},{9,8},{10,11... | collective-permute-start | bytes 589832 | tf_op jit(solution)/shard_map/ppermute | solution.py:252
  48.8 10.5 %collective-permute-start.69 = (bf16[2,2,96,256]{3,2,1,0:T(8,128)(2,1)S(1)}, bf16[2,2,96,256]{3,2,1,0:T(8,128)(2,1)S(1)}, u32[]{:S(2)}, u32[]{:S(2)}) collective-permute-start(bf16[2,2,96,256]{3,2,1,0:T(8,128)(2,1)S(1)} %get-tuple-element.173), channel_id=1, source_target_pairs={{0,2},{1,3},{2,0},{3,1},{4,6},{5,7},{6,4},{7,5},{8,10},{9,11},{10,... | collective-permute-start | bytes 589832 | tf_op jit(solution)/shard_map/ppermute | solution.py:252
  50.6 15.6 %collective-permute-start.70 = (bf16[2,2,96,256]{3,2,1,0:T(8,128)(2,1)S(1)}, bf16[2,2,96,256]{3,2,1,0:T(8,128)(2,1)S(1)}, u32[]{:S(2)}, u32[]{:S(2)}) collective-permute-start(bf16[2,2,96,256]{3,2,1,0:T(8,128)(2,1)S(1)} %get-tuple-element.174), channel_id=1, source_target_pairs={{0,3},{1,2},{2,1},{3,0},{4,7},{5,6},{6,5},{7,4},{8,11},{9,10},{10,... | collective-permute-start | bytes 589832 | tf_op jit(solution)/shard_map/ppermute | solution.py:252
  51.3 15.8 %collective-permute-start.71 = (bf16[2,2,96,256]{3,2,1,0:T(8,128)(2,1)S(1)}, bf16[2,2,96,256]{3,2,1,0:T(8,128)(2,1)S(1)}, u32[]{:S(2)}, u32[]{:S(2)}) collective-permute-start(bf16[2,2,96,256]{3,2,1,0:T(8,128)(2,1)S(1)} %get-tuple-element.175), channel_id=1, source_target_pairs={{0,4},{1,5},{2,6},{3,7},{4,0},{5,1},{6,2},{7,3},{8,12},{9,13},{10,... | collective-permute-start | bytes 589832 | tf_op jit(solution)/shard_map/ppermute | solution.py:252
  58.0 14.6 %collective-permute-start.72 = (bf16[2,2,96,256]{3,2,1,0:T(8,128)(2,1)S(1)}, bf16[2,2,96,256]{3,2,1,0:T(8,128)(2,1)S(1)}, u32[]{:S(2)}, u32[]{:S(2)}) collective-permute-start(bf16[2,2,96,256]{3,2,1,0:T(8,128)(2,1)S(1)} %get-tuple-element.176), channel_id=1, source_target_pairs={{0,5},{1,4},{2,7},{3,6},{4,1},{5,0},{6,3},{7,2},{8,13},{9,12},{10,... | collective-permute-start | bytes 589832 | tf_op jit(solution)/shard_map/ppermute | solution.py:252
  58.7 13.9 %collective-permute-start.73 = (bf16[2,2,96,256]{3,2,1,0:T(8,128)(2,1)S(1)}, bf16[2,2,96,256]{3,2,1,0:T(8,128)(2,1)S(1)}, u32[]{:S(2)}, u32[]{:S(2)}) collective-permute-start(bf16[2,2,96,256]{3,2,1,0:T(8,128)(2,1)S(1)} %get-tuple-element.177), channel_id=1, source_target_pairs={{0,6},{1,7},{2,4},{3,5},{4,2},{5,3},{6,0},{7,1},{8,14},{9,15},{10,... | collective-permute-start | bytes 589832 | tf_op jit(solution)/shard_map/ppermute | solution.py:252
  60.0 15.0 %collective-permute-start.74 = (bf16[2,2,96,256]{3,2,1,0:T(8,128)(2,1)S(1)}, bf16[2,2,96,256]{3,2,1,0:T(8,128)(2,1)S(1)}, u32[]{:S(2)}, u32[]{:S(2)}) collective-permute-start(bf16[2,2,96,256]{3,2,1,0:T(8,128)(2,1)S(1)} %get-tuple-element.178), channel_id=1, source_target_pairs={{0,7},{1,6},{2,5},{3,4},{4,3},{5,2},{6,1},{7,0},{8,15},{9,14},{10,... | collective-permute-start | bytes 589832 | tf_op jit(solution)/shard_map/ppermute | solution.py:252
  66.9 16.7 %collective-permute-start.57 = (bf16[2,2,96,256]{3,2,1,0:T(8,128)(2,1)S(1)}, bf16[2,2,96,256]{3,2,1,0:T(8,128)(2,1)S(1)}, u32[]{:S(2)}, u32[]{:S(2)}) collective-permute-start(bf16[2,2,96,256]{3,2,1,0:T(8,128)(2,1)S(1)} %get-tuple-element.162), channel_id=1, source_target_pairs={{0,1},{1,0},{2,3},{3,2},{4,5},{5,4},{6,7},{7,6},{8,9},{9,8},{10,11... | collective-permute-start | bytes 589832 | tf_op jit(solution)/shard_map/ppermute | solution.py:252
  67.8 18.4 %collective-permute-start.58 = (bf16[2,2,96,256]{3,2,1,0:T(8,128)(2,1)S(1)}, bf16[2,2,96,256]{3,2,1,0:T(8,128)(2,1)S(1)}, u32[]{:S(2)}, u32[]{:S(2)}) collective-permute-start(bf16[2,2,96,256]{3,2,1,0:T(8,128)(2,1)S(1)} %get-tuple-element.163), channel_id=1, source_target_pairs={{0,2},{1,3},{2,0},{3,1},{4,6},{5,7},{6,4},{7,5},{8,10},{9,11},{10,... | collective-permute-start | bytes 589832 | tf_op jit(solution)/shard_map/ppermute | solution.py:252
  72.7 16.7 %collective-permute-start.59 = (bf16[2,2,96,256]{3,2,1,0:T(8,128)(2,1)S(1)}, bf16[2,2,96,256]{3,2,1,0:T(8,128)(2,1)S(1)}, u32[]{:S(2)}, u32[]{:S(2)}) collective-permute-start(bf16[2,2,96,256]{3,2,1,0:T(8,128)(2,1)S(1)} %get-tuple-element.164), channel_id=1, source_target_pairs={{0,3},{1,2},{2,1},{3,0},{4,7},{5,6},{6,5},{7,4},{8,11},{9,10},{10,... | collective-permute-start | bytes 589832 | tf_op jit(solution)/shard_map/ppermute | solution.py:252
  73.4 16.0 %collective-permute-start.60 = (bf16[2,2,96,256]{3,2,1,0:T(8,128)(2,1)S(1)}, bf16[2,2,96,256]{3,2,1,0:T(8,128)(2,1)S(1)}, u32[]{:S(2)}, u32[]{:S(2)}) collective-permute-start(bf16[2,2,96,256]{3,2,1,0:T(8,128)(2,1)S(1)} %get-tuple-element.165), channel_id=1, source_target_pairs={{0,4},{1,5},{2,6},{3,7},{4,0},{5,1},{6,2},{7,3},{8,12},{9,13},{10,... | collective-permute-start | bytes 589832 | tf_op jit(solution)/shard_map/ppermute | solution.py:252
  83.1 15.6 %collective-permute-start.61 = (bf16[2,2,96,256]{3,2,1,0:T(8,128)(2,1)S(1)}, bf16[2,2,96,256]{3,2,1,0:T(8,128)(2,1)S(1)}, u32[]{:S(2)}, u32[]{:S(2)}) collective-permute-start(bf16[2,2,96,256]{3,2,1,0:T(8,128)(2,1)S(1)} %get-tuple-element.166), channel_id=1, source_target_pairs={{0,5},{1,4},{2,7},{3,6},{4,1},{5,0},{6,3},{7,2},{8,13},{9,12},{10,... | collective-permute-start | bytes 589832 | tf_op jit(solution)/shard_map/ppermute | solution.py:252
  84.4 15.4 %collective-permute-start.62 = (bf16[2,2,96,256]{3,2,1,0:T(8,128)(2,1)S(1)}, bf16[2,2,96,256]{3,2,1,0:T(8,128)(2,1)S(1)}, u32[]{:S(2)}, u32[]{:S(2)}) collective-permute-start(bf16[2,2,96,256]{3,2,1,0:T(8,128)(2,1)S(1)} %get-tuple-element.167), channel_id=1, source_target_pairs={{0,6},{1,7},{2,4},{3,5},{4,2},{5,3},{6,0},{7,1},{8,14},{9,15},{10,... | collective-permute-start | bytes 589832 | tf_op jit(solution)/shard_map/ppermute | solution.py:252
  87.0 13.3 %collective-permute-start.63 = (bf16[2,2,96,256]{3,2,1,0:T(8,128)(2,1)S(1)}, bf16[2,2,96,256]{3,2,1,0:T(8,128)(2,1)S(1)}, u32[]{:S(2)}, u32[]{:S(2)}) collective-permute-start(bf16[2,2,96,256]{3,2,1,0:T(8,128)(2,1)S(1)} %get-tuple-element.168), channel_id=1, source_target_pairs={{0,7},{1,6},{2,5},{3,4},{4,3},{5,2},{6,1},{7,0},{8,15},{9,14},{10,... | collective-permute-start | bytes 589832 | tf_op jit(solution)/shard_map/ppermute | solution.py:252
  89.4 12.1 %collective-permute-start.50 = (bf16[2,2,96,256]{3,2,1,0:T(8,128)(2,1)S(1)}, bf16[2,2,96,256]{3,2,1,0:T(8,128)(2,1)S(1)}, u32[]{:S(2)}, u32[]{:S(2)}) collective-permute-start(bf16[2,2,96,256]{3,2,1,0:T(8,128)(2,1)S(1)} %get-tuple-element.154), channel_id=1, source_target_pairs={{0,1},{1,0},{2,3},{3,2},{4,5},{5,4},{6,7},{7,6},{8,9},{9,8},{10,11... | collective-permute-start | bytes 589832 | tf_op jit(solution)/shard_map/ppermute | solution.py:252
  89.4 13.2 %collective-permute-start.51 = (bf16[2,2,96,256]{3,2,1,0:T(8,128)(2,1)S(1)}, bf16[2,2,96,256]{3,2,1,0:T(8,128)(2,1)S(1)}, u32[]{:S(2)}, u32[]{:S(2)}) collective-permute-start(bf16[2,2,96,256]{3,2,1,0:T(8,128)(2,1)S(1)} %get-tuple-element.155), channel_id=1, source_target_pairs={{0,2},{1,3},{2,0},{3,1},{4,6},{5,7},{6,4},{7,5},{8,10},{9,11},{10,... | collective-permute-start | bytes 589832 | tf_op jit(solution)/shard_map/ppermute | solution.py:252
  98.6 11.3 %collective-permute-start.52 = (bf16[2,2,96,256]{3,2,1,0:T(8,128)(2,1)S(1)}, bf16[2,2,96,256]{3,2,1,0:T(8,128)(2,1)S(1)}, u32[]{:S(2)}, u32[]{:S(2)}) collective-permute-start(bf16[2,2,96,256]{3,2,1,0:T(8,128)(2,1)S(1)} %get-tuple-element.156), channel_id=1, source_target_pairs={{0,3},{1,2},{2,1},{3,0},{4,7},{5,6},{6,5},{7,4},{8,11},{9,10},{10,... | collective-permute-start | bytes 589832 | tf_op jit(solution)/shard_map/ppermute | solution.py:252
  99.8 18.3 %collective-permute-start.53 = (bf16[2,2,96,256]{3,2,1,0:T(8,128)(2,1)S(1)}, bf16[2,2,96,256]{3,2,1,0:T(8,128)(2,1)S(1)}, u32[]{:S(2)}, u32[]{:S(2)}) collective-permute-start(bf16[2,2,96,256]{3,2,1,0:T(8,128)(2,1)S(1)} %get-tuple-element.157), channel_id=1, source_target_pairs={{0,4},{1,5},{2,6},{3,7},{4,0},{5,1},{6,2},{7,3},{8,12},{9,13},{10,... | collective-permute-start | bytes 589832 | tf_op jit(solution)/shard_map/ppermute | solution.py:252
  101.5 19.0 %collective-permute-start.54 = (bf16[2,2,96,256]{3,2,1,0:T(8,128)(2,1)S(1)}, bf16[2,2,96,256]{3,2,1,0:T(8,128)(2,1)S(1)}, u32[]{:S(2)}, u32[]{:S(2)}) collective-permute-start(bf16[2,2,96,256]{3,2,1,0:T(8,128)(2,1)S(1)} %get-tuple-element.158), channel_id=1, source_target_pairs={{0,5},{1,4},{2,7},{3,6},{4,1},{5,0},{6,3},{7,2},{8,13},{9,12},{10,... | collective-permute-start | bytes 589832 | tf_op jit(solution)/shard_map/ppermute | solution.py:252
  102.6 19.1 %collective-permute-start.55 = (bf16[2,2,96,256]{3,2,1,0:T(8,128)(2,1)S(1)}, bf16[2,2,96,256]{3,2,1,0:T(8,128)(2,1)S(1)}, u32[]{:S(2)}, u32[]{:S(2)}) collective-permute-start(bf16[2,2,96,256]{3,2,1,0:T(8,128)(2,1)S(1)} %get-tuple-element.159), channel_id=1, source_target_pairs={{0,6},{1,7},{2,4},{3,5},{4,2},{5,3},{6,0},{7,1},{8,14},{9,15},{10,... | collective-permute-start | bytes 589832 | tf_op jit(solution)/shard_map/ppermute | solution.py:252
  103.8 19.5 %collective-permute-start.56 = (bf16[2,2,96,256]{3,2,1,0:T(8,128)(2,1)S(1)}, bf16[2,2,96,256]{3,2,1,0:T(8,128)(2,1)S(1)}, u32[]{:S(2)}, u32[]{:S(2)}) collective-permute-start(bf16[2,2,96,256]{3,2,1,0:T(8,128)(2,1)S(1)} %get-tuple-element.160), channel_id=1, source_target_pairs={{0,7},{1,6},{2,5},{3,4},{4,3},{5,2},{6,1},{7,0},{8,15},{9,14},{10,... | collective-permute-start | bytes 589832 | tf_op jit(solution)/shard_map/ppermute | solution.py:252
  110.6 14.0 %collective-permute-start.10 = (bf16[2,1,96,256]{3,2,1,0:T(8,128)(2,1)S(1)}, bf16[2,1,96,256]{3,2,1,0:T(8,128)(2,1)S(1)}, u32[]{:S(2)}, u32[]{:S(2)}) collective-permute-start(bf16[2,1,96,256]{3,2,1,0:T(8,128)(2,1)S(1)} %get-tuple-element.110), channel_id=1, source_target_pairs={{0,7},{1,6},{2,5},{3,4},{4,3},{5,2},{6,1},{7,0},{8,15},{9,14},{10,... | collective-permute-start | bytes 294920 | tf_op jit(solution)/shard_map/ppermute | solution.py:252
  118.1 12.7 %collective-permute-start.39 = (bf16[2,2,96,256]{3,2,1,0:T(8,128)(2,1)S(1)}, bf16[2,2,96,256]{3,2,1,0:T(8,128)(2,1)S(1)}, u32[]{:S(2)}, u32[]{:S(2)}) collective-permute-start(bf16[2,2,96,256]{3,2,1,0:T(8,128)(2,1)S(1)} %get-tuple-element.144), channel_id=1, source_target_pairs={{0,1},{1,0},{2,3},{3,2},{4,5},{5,4},{6,7},{7,6},{8,9},{9,8},{10,11... | collective-permute-start | bytes 589832 | tf_op jit(solution)/shard_map/ppermute | solution.py:252
  120.5 11.7 %collective-permute-start.40 = (bf16[2,2,96,256]{3,2,1,0:T(8,128)(2,1)S(1)}, bf16[2,2,96,256]{3,2,1,0:T(8,128)(2,1)S(1)}, u32[]{:S(2)}, u32[]{:S(2)}) collective-permute-start(bf16[2,2,96,256]{3,2,1,0:T(8,128)(2,1)S(1)} %get-tuple-element.145), channel_id=1, source_target_pairs={{0,2},{1,3},{2,0},{3,1},{4,6},{5,7},{6,4},{7,5},{8,10},{9,11},{10,... | collective-permute-start | bytes 589832 | tf_op jit(solution)/shard_map/ppermute | solution.py:252
  122.3 10.7 %collective-permute-start.41 = (bf16[2,2,96,256]{3,2,1,0:T(8,128)(2,1)S(1)}, bf16[2,2,96,256]{3,2,1,0:T(8,128)(2,1)S(1)}, u32[]{:S(2)}, u32[]{:S(2)}) collective-permute-start(bf16[2,2,96,256]{3,2,1,0:T(8,128)(2,1)S(1)} %get-tuple-element.146), channel_id=1, source_target_pairs={{0,3},{1,2},{2,1},{3,0},{4,7},{5,6},{6,5},{7,4},{8,11},{9,10},{10,... | collective-permute-start | bytes 589832 | tf_op jit(solution)/shard_map/ppermute | solution.py:252
  123.3 12.7 %collective-permute-start.42 = (bf16[2,2,96,256]{3,2,1,0:T(8,128)(2,1)S(1)}, bf16[2,2,96,256]{3,2,1,0:T(8,128)(2,1)S(1)}, u32[]{:S(2)}, u32[]{:S(2)}) collective-permute-start(bf16[2,2,96,256]{3,2,1,0:T(8,128)(2,1)S(1)} %get-tuple-element.147), channel_id=1, source_target_pairs={{0,4},{1,5},{2,6},{3,7},{4,0},{5,1},{6,2},{7,3},{8,12},{9,13},{10,... | collective-permute-start | bytes 589832 | tf_op jit(solution)/shard_map/ppermute | solution.py:252
  130.6 20.7 %collective-permute-start.11 = (bf16[2,3,96,256]{3,2,1,0:T(8,128)(2,1)S(1)}, bf16[2,3,96,256]{3,2,1,0:T(8,128)(2,1)S(1)}, u32[]{:S(2)}, u32[]{:S(2)}) collective-permute-start(bf16[2,3,96,256]{3,2,1,0:T(8,128)(2,1)S(1)} %get-tuple-element.112), channel_id=1, source_target_pairs={{0,1},{1,0},{2,3},{3,2},{4,5},{5,4},{6,7},{7,6},{8,9},{9,8},{10,11... | collective-permute-start | bytes 884744 | tf_op jit(solution)/shard_map/ppermute | solution.py:252
  131.4 21.6 %collective-permute-start.12 = (bf16[2,3,96,256]{3,2,1,0:T(8,128)(2,1)S(1)}, bf16[2,3,96,256]{3,2,1,0:T(8,128)(2,1)S(1)}, u32[]{:S(2)}, u32[]{:S(2)}) collective-permute-start(bf16[2,3,96,256]{3,2,1,0:T(8,128)(2,1)S(1)} %get-tuple-element.113), channel_id=1, source_target_pairs={{0,2},{1,3},{2,0},{3,1},{4,6},{5,7},{6,4},{7,5},{8,10},{9,11},{10,... | collective-permute-start | bytes 884744 | tf_op jit(solution)/shard_map/ppermute | solution.py:252
  133.7 11.9 %collective-permute-start.44 = (bf16[2,2,96,256]{3,2,1,0:T(8,128)(2,1)S(1)}, bf16[2,2,96,256]{3,2,1,0:T(8,128)(2,1)S(1)}, u32[]{:S(2)}, u32[]{:S(2)}) collective-permute-start(bf16[2,2,96,256]{3,2,1,0:T(8,128)(2,1)S(1)} %get-tuple-element.149), channel_id=1, source_target_pairs={{0,6},{1,7},{2,4},{3,5},{4,2},{5,3},{6,0},{7,1},{8,14},{9,15},{10,... | collective-permute-start | bytes 589832 | tf_op jit(solution)/shard_map/ppermute | solution.py:252
  136.6 11.4 %collective-permute-start.45 = (bf16[2,2,96,256]{3,2,1,0:T(8,128)(2,1)S(1)}, bf16[2,2,96,256]{3,2,1,0:T(8,128)(2,1)S(1)}, u32[]{:S(2)}, u32[]{:S(2)}) collective-permute-start(bf16[2,2,96,256]{3,2,1,0:T(8,128)(2,1)S(1)} %get-tuple-element.150), channel_id=1, source_target_pairs={{0,7},{1,6},{2,5},{3,4},{4,3},{5,2},{6,1},{7,0},{8,15},{9,14},{10,... | collective-permute-start | bytes 589832 | tf_op jit(solution)/shard_map/ppermute | solution.py:252
  140.9 17.8 %collective-permute-start.13 = (bf16[2,3,96,256]{3,2,1,0:T(8,128)(2,1)S(1)}, bf16[2,3,96,256]{3,2,1,0:T(8,128)(2,1)S(1)}, u32[]{:S(2)}, u32[]{:S(2)}) collective-permute-start(bf16[2,3,96,256]{3,2,1,0:T(8,128)(2,1)S(1)} %get-tuple-element.114), channel_id=1, source_target_pairs={{0,3},{1,2},{2,1},{3,0},{4,7},{5,6},{6,5},{7,4},{8,11},{9,10},{10,... | collective-permute-start | bytes 884744 | tf_op jit(solution)/shard_map/ppermute | solution.py:252
  146.3 22.2 %collective-permute-start.14 = (bf16[2,3,96,256]{3,2,1,0:T(8,128)(2,1)S(1)}, bf16[2,3,96,256]{3,2,1,0:T(8,128)(2,1)S(1)}, u32[]{:S(2)}, u32[]{:S(2)}) collective-permute-start(bf16[2,3,96,256]{3,2,1,0:T(8,128)(2,1)S(1)} %get-tuple-element.115), channel_id=1, source_target_pairs={{0,4},{1,5},{2,6},{3,7},{4,0},{5,1},{6,2},{7,3},{8,12},{9,13},{10,... | collective-permute-start | bytes 884744 | tf_op jit(solution)/shard_map/ppermute | solution.py:252
  148.7 24.7 %collective-permute-start.15 = (bf16[2,3,96,256]{3,2,1,0:T(8,128)(2,1)S(1)}, bf16[2,3,96,256]{3,2,1,0:T(8,128)(2,1)S(1)}, u32[]{:S(2)}, u32[]{:S(2)}) collective-permute-start(bf16[2,3,96,256]{3,2,1,0:T(8,128)(2,1)S(1)} %get-tuple-element.116), channel_id=1, source_target_pairs={{0,5},{1,4},{2,7},{3,6},{4,1},{5,0},{6,3},{7,2},{8,13},{9,12},{10,... | collective-permute-start | bytes 884744 | tf_op jit(solution)/shard_map/ppermute | solution.py:252
  152.0 23.5 %collective-permute-start.16 = (bf16[2,3,96,256]{3,2,1,0:T(8,128)(2,1)S(1)}, bf16[2,3,96,256]{3,2,1,0:T(8,128)(2,1)S(1)}, u32[]{:S(2)}, u32[]{:S(2)}) collective-permute-start(bf16[2,3,96,256]{3,2,1,0:T(8,128)(2,1)S(1)} %get-tuple-element.117), channel_id=1, source_target_pairs={{0,6},{1,7},{2,4},{3,5},{4,2},{5,3},{6,0},{7,1},{8,14},{9,15},{10,... | collective-permute-start | bytes 884744 | tf_op jit(solution)/shard_map/ppermute | solution.py:252
  153.7 24.0 %collective-permute-start.17 = (bf16[2,3,96,256]{3,2,1,0:T(8,128)(2,1)S(1)}, bf16[2,3,96,256]{3,2,1,0:T(8,128)(2,1)S(1)}, u32[]{:S(2)}, u32[]{:S(2)}) collective-permute-start(bf16[2,3,96,256]{3,2,1,0:T(8,128)(2,1)S(1)} %get-tuple-element.118), channel_id=1, source_target_pairs={{0,7},{1,6},{2,5},{3,4},{4,3},{5,2},{6,1},{7,0},{8,15},{9,14},{10,... | collective-permute-start | bytes 884744 | tf_op jit(solution)/shard_map/ppermute | solution.py:252
  159.5 18.9 %collective-permute-start.32 = (bf16[2,4,96,256]{3,2,1,0:T(8,128)(2,1)S(1)}, bf16[2,4,96,256]{3,2,1,0:T(8,128)(2,1)S(1)}, u32[]{:S(2)}, u32[]{:S(2)}) collective-permute-start(bf16[2,4,96,256]{3,2,1,0:T(8,128)(2,1)S(1)} %get-tuple-element.136), channel_id=1, source_target_pairs={{0,1},{1,0},{2,3},{3,2},{4,5},{5,4},{6,7},{7,6},{8,9},{9,8},{10,11... | collective-permute-start | bytes 1179656 | tf_op jit(solution)/shard_map/ppermute | solution.py:252
  169.3 19.0 %collective-permute-start.33 = (bf16[2,4,96,256]{3,2,1,0:T(8,128)(2,1)S(1)}, bf16[2,4,96,256]{3,2,1,0:T(8,128)(2,1)S(1)}, u32[]{:S(2)}, u32[]{:S(2)}) collective-permute-start(bf16[2,4,96,256]{3,2,1,0:T(8,128)(2,1)S(1)} %get-tuple-element.137), channel_id=1, source_target_pairs={{0,2},{1,3},{2,0},{3,1},{4,6},{5,7},{6,4},{7,5},{8,10},{9,11},{10,... | collective-permute-start | bytes 1179656 | tf_op jit(solution)/shard_map/ppermute | solution.py:252
  174.1 15.7 %collective-permute-start.34 = (bf16[2,4,96,256]{3,2,1,0:T(8,128)(2,1)S(1)}, bf16[2,4,96,256]{3,2,1,0:T(8,128)(2,1)S(1)}, u32[]{:S(2)}, u32[]{:S(2)}) collective-permute-start(bf16[2,4,96,256]{3,2,1,0:T(8,128)(2,1)S(1)} %get-tuple-element.138), channel_id=1, source_target_pairs={{0,3},{1,2},{2,1},{3,0},{4,7},{5,6},{6,5},{7,4},{8,11},{9,10},{10,... | collective-permute-start | bytes 1179656 | tf_op jit(solution)/shard_map/ppermute | solution.py:252
  176.2 20.4 %collective-permute-start.35 = (bf16[2,4,96,256]{3,2,1,0:T(8,128)(2,1)S(1)}, bf16[2,4,96,256]{3,2,1,0:T(8,128)(2,1)S(1)}, u32[]{:S(2)}, u32[]{:S(2)}) collective-permute-start(bf16[2,4,96,256]{3,2,1,0:T(8,128)(2,1)S(1)} %get-tuple-element.139), channel_id=1, source_target_pairs={{0,4},{1,5},{2,6},{3,7},{4,0},{5,1},{6,2},{7,3},{8,12},{9,13},{10,... | collective-permute-start | bytes 1179656 | tf_op jit(solution)/shard_map/ppermute | solution.py:252
  178.4 24.4 %collective-permute-start.36 = (bf16[2,4,96,256]{3,2,1,0:T(8,128)(2,1)S(1)}, bf16[2,4,96,256]{3,2,1,0:T(8,128)(2,1)S(1)}, u32[]{:S(2)}, u32[]{:S(2)}) collective-permute-start(bf16[2,4,96,256]{3,2,1,0:T(8,128)(2,1)S(1)} %get-tuple-element.140), channel_id=1, source_target_pairs={{0,5},{1,4},{2,7},{3,6},{4,1},{5,0},{6,3},{7,2},{8,13},{9,12},{10,... | collective-permute-start | bytes 1179656 | tf_op jit(solution)/shard_map/ppermute | solution.py:252
  178.4 25.6 %collective-permute-start.37 = (bf16[2,4,96,256]{3,2,1,0:T(8,128)(2,1)S(1)}, bf16[2,4,96,256]{3,2,1,0:T(8,128)(2,1)S(1)}, u32[]{:S(2)}, u32[]{:S(2)}) collective-permute-start(bf16[2,4,96,256]{3,2,1,0:T(8,128)(2,1)S(1)} %get-tuple-element.141), channel_id=1, source_target_pairs={{0,6},{1,7},{2,4},{3,5},{4,2},{5,3},{6,0},{7,1},{8,14},{9,15},{10,... | collective-permute-start | bytes 1179656 | tf_op jit(solution)/shard_map/ppermute | solution.py:252
  189.1 48.7 %collective-permute-start.25 = (bf16[2,8,96,256]{3,2,1,0:T(8,128)(2,1)S(1)}, bf16[2,8,96,256]{3,2,1,0:T(8,128)(2,1)S(1)}, u32[]{:S(2)}, u32[]{:S(2)}) collective-permute-start(bf16[2,8,96,256]{3,2,1,0:T(8,128)(2,1)S(1)} %get-tuple-element.128), channel_id=1, source_target_pairs={{0,1},{1,0},{2,3},{3,2},{4,5},{5,4},{6,7},{7,6},{8,9},{9,8},{10,11... | collective-permute-start | bytes 2359304 | tf_op jit(solution)/shard_map/ppermute | solution.py:252
  190.5 49.2 %collective-permute-start.26 = (bf16[2,8,96,256]{3,2,1,0:T(8,128)(2,1)S(1)}, bf16[2,8,96,256]{3,2,1,0:T(8,128)(2,1)S(1)}, u32[]{:S(2)}, u32[]{:S(2)}) collective-permute-start(bf16[2,8,96,256]{3,2,1,0:T(8,128)(2,1)S(1)} %get-tuple-element.129), channel_id=1, source_target_pairs={{0,2},{1,3},{2,0},{3,1},{4,6},{5,7},{6,4},{7,5},{8,10},{9,11},{10,... | collective-permute-start | bytes 2359304 | tf_op jit(solution)/shard_map/ppermute | solution.py:252
  196.7 43.6 %collective-permute-start.27 = (bf16[2,8,96,256]{3,2,1,0:T(8,128)(2,1)S(1)}, bf16[2,8,96,256]{3,2,1,0:T(8,128)(2,1)S(1)}, u32[]{:S(2)}, u32[]{:S(2)}) collective-permute-start(bf16[2,8,96,256]{3,2,1,0:T(8,128)(2,1)S(1)} %get-tuple-element.130), channel_id=1, source_target_pairs={{0,3},{1,2},{2,1},{3,0},{4,7},{5,6},{6,5},{7,4},{8,11},{9,10},{10,... | collective-permute-start | bytes 2359304 | tf_op jit(solution)/shard_map/ppermute | solution.py:252
  202.8 38.0 %collective-permute-start.28 = (bf16[2,8,96,256]{3,2,1,0:T(8,128)(2,1)S(1)}, bf16[2,8,96,256]{3,2,1,0:T(8,128)(2,1)S(1)}, u32[]{:S(2)}, u32[]{:S(2)}) collective-permute-start(bf16[2,8,96,256]{3,2,1,0:T(8,128)(2,1)S(1)} %get-tuple-element.131), channel_id=1, source_target_pairs={{0,4},{1,5},{2,6},{3,7},{4,0},{5,1},{6,2},{7,3},{8,12},{9,13},{10,... | collective-permute-start | bytes 2359304 | tf_op jit(solution)/shard_map/ppermute | solution.py:252
  204.0 32.5 %collective-permute-start.38 = (bf16[2,4,96,256]{3,2,1,0:T(8,128)(2,1)S(1)}, bf16[2,4,96,256]{3,2,1,0:T(8,128)(2,1)S(1)}, u32[]{:S(2)}, u32[]{:S(2)}) collective-permute-start(bf16[2,4,96,256]{3,2,1,0:T(8,128)(2,1)S(1)} %get-tuple-element.142), channel_id=1, source_target_pairs={{0,7},{1,6},{2,5},{3,4},{4,3},{5,2},{6,1},{7,0},{8,15},{9,14},{10,... | collective-permute-start | bytes 1179656 | tf_op jit(solution)/shard_map/ppermute | solution.py:252
  237.3 52.7 %collective-permute-start.29 = (bf16[2,8,96,256]{3,2,1,0:T(8,128)(2,1)S(1)}, bf16[2,8,96,256]{3,2,1,0:T(8,128)(2,1)S(1)}, u32[]{:S(2)}, u32[]{:S(2)}) collective-permute-start(bf16[2,8,96,256]{3,2,1,0:T(8,128)(2,1)S(1)} %get-tuple-element.132), channel_id=1, source_target_pairs={{0,5},{1,4},{2,7},{3,6},{4,1},{5,0},{6,3},{7,2},{8,13},{9,12},{10,... | collective-permute-start | bytes 2359304 | tf_op jit(solution)/shard_map/ppermute | solution.py:252
  237.8 54.2 %collective-permute-start.30 = (bf16[2,8,96,256]{3,2,1,0:T(8,128)(2,1)S(1)}, bf16[2,8,96,256]{3,2,1,0:T(8,128)(2,1)S(1)}, u32[]{:S(2)}, u32[]{:S(2)}) collective-permute-start(bf16[2,8,96,256]{3,2,1,0:T(8,128)(2,1)S(1)} %get-tuple-element.133), channel_id=1, source_target_pairs={{0,6},{1,7},{2,4},{3,5},{4,2},{5,3},{6,0},{7,1},{8,14},{9,15},{10,... | collective-permute-start | bytes 2359304 | tf_op jit(solution)/shard_map/ppermute | solution.py:252
  239.7 53.9 %collective-permute-start.31 = (bf16[2,8,96,256]{3,2,1,0:T(8,128)(2,1)S(1)}, bf16[2,8,96,256]{3,2,1,0:T(8,128)(2,1)S(1)}, u32[]{:S(2)}, u32[]{:S(2)}) collective-permute-start(bf16[2,8,96,256]{3,2,1,0:T(8,128)(2,1)S(1)} %get-tuple-element.134), channel_id=1, source_target_pairs={{0,7},{1,6},{2,5},{3,4},{4,3},{5,2},{6,1},{7,0},{8,15},{9,14},{10,... | collective-permute-start | bytes 2359304 | tf_op jit(solution)/shard_map/ppermute | solution.py:252
  240.3 54.8 %collective-permute-start.18 = (bf16[2,8,96,256]{3,2,1,0:T(8,128)(2,1)S(1)}, bf16[2,8,96,256]{3,2,1,0:T(8,128)(2,1)S(1)}, u32[]{:S(2)}, u32[]{:S(2)}) collective-permute-start(bf16[2,8,96,256]{3,2,1,0:T(8,128)(2,1)S(1)} %get-tuple-element.120), channel_id=1, source_target_pairs={{0,1},{1,0},{2,3},{3,2},{4,5},{5,4},{6,7},{7,6},{8,9},{9,8},{10,11... | collective-permute-start | bytes 2359304 | tf_op jit(solution)/shard_map/ppermute | solution.py:252
  241.8 55.9 %collective-permute-start.19 = (bf16[2,8,96,256]{3,2,1,0:T(8,128)(2,1)S(1)}, bf16[2,8,96,256]{3,2,1,0:T(8,128)(2,1)S(1)}, u32[]{:S(2)}, u32[]{:S(2)}) collective-permute-start(bf16[2,8,96,256]{3,2,1,0:T(8,128)(2,1)S(1)} %get-tuple-element.121), channel_id=1, source_target_pairs={{0,2},{1,3},{2,0},{3,1},{4,6},{5,7},{6,4},{7,5},{8,10},{9,11},{10,... | collective-permute-start | bytes 2359304 | tf_op jit(solution)/shard_map/ppermute | solution.py:252
  290.9 32.1 %collective-permute-start.20 = (bf16[2,8,96,256]{3,2,1,0:T(8,128)(2,1)}, bf16[2,8,96,256]{3,2,1,0:T(8,128)(2,1)}, u32[]{:S(2)}, u32[]{:S(2)}) collective-permute-start(bf16[2,8,96,256]{3,2,1,0:T(8,128)(2,1)} %get-tuple-element.122), channel_id=1, source_target_pairs={{0,3},{1,2},{2,1},{3,0},{4,7},{5,6},{6,5},{7,4},{8,11},{9,10},{10,... | collective-permute-start | bytes 2359304 | tf_op jit(solution)/shard_map/ppermute | solution.py:252
  292.9 54.4 %collective-permute-start.21 = (bf16[2,8,96,256]{3,2,1,0:T(8,128)(2,1)}, bf16[2,8,96,256]{3,2,1,0:T(8,128)(2,1)}, u32[]{:S(2)}, u32[]{:S(2)}) collective-permute-start(bf16[2,8,96,256]{3,2,1,0:T(8,128)(2,1)} %get-tuple-element.123), channel_id=1, source_target_pairs={{0,4},{1,5},{2,6},{3,7},{4,0},{5,1},{6,2},{7,3},{8,12},{9,13},{10,... | collective-permute-start | bytes 2359304 | tf_op jit(solution)/shard_map/ppermute | solution.py:252
  294.5 67.5 %collective-permute-start.22 = (bf16[2,8,96,256]{3,2,1,0:T(8,128)(2,1)}, bf16[2,8,96,256]{3,2,1,0:T(8,128)(2,1)}, u32[]{:S(2)}, u32[]{:S(2)}) collective-permute-start(bf16[2,8,96,256]{3,2,1,0:T(8,128)(2,1)} %get-tuple-element.124), channel_id=1, source_target_pairs={{0,5},{1,4},{2,7},{3,6},{4,1},{5,0},{6,3},{7,2},{8,13},{9,12},{10,... | collective-permute-start | bytes 2359304 | tf_op jit(solution)/shard_map/ppermute | solution.py:252
  295.9 66.7 %collective-permute-start.23 = (bf16[2,8,96,256]{3,2,1,0:T(8,128)(2,1)}, bf16[2,8,96,256]{3,2,1,0:T(8,128)(2,1)}, u32[]{:S(2)}, u32[]{:S(2)}) collective-permute-start(bf16[2,8,96,256]{3,2,1,0:T(8,128)(2,1)} %get-tuple-element.125), channel_id=1, source_target_pairs={{0,6},{1,7},{2,4},{3,5},{4,2},{5,3},{6,0},{7,1},{8,14},{9,15},{10,... | collective-permute-start | bytes 2359304 | tf_op jit(solution)/shard_map/ppermute | solution.py:252
  298.6 65.7 %collective-permute-start.24 = (bf16[2,8,96,256]{3,2,1,0:T(8,128)(2,1)}, bf16[2,8,96,256]{3,2,1,0:T(8,128)(2,1)}, u32[]{:S(2)}, u32[]{:S(2)}) collective-permute-start(bf16[2,8,96,256]{3,2,1,0:T(8,128)(2,1)} %get-tuple-element.126), channel_id=1, source_target_pairs={{0,7},{1,6},{2,5},{3,4},{4,3},{5,2},{6,1},{7,0},{8,15},{9,14},{10,... | collective-permute-start | bytes 2359304 | tf_op jit(solution)/shard_map/ppermute | solution.py:252
  322.9 63.4 %collective-permute-start.5 = (bf16[2,1,96,256]{3,2,1,0:T(8,128)(2,1)S(1)}, bf16[2,1,96,256]{3,2,1,0:T(8,128)(2,1)S(1)}, u32[]{:S(2)}, u32[]{:S(2)}) collective-permute-start(bf16[2,1,96,256]{3,2,1,0:T(8,128)(2,1)S(1)} %copy-done.128), channel_id=1, source_target_pairs={{0,2},{1,3},{2,0},{3,1},{4,6},{5,7},{6,4},{7,5},{8,10},{9,11},{10,... | collective-permute-start | bytes 294920 | tf_op jit(solution)/shard_map/ppermute | solution.py:252
  347.3 39.0 %collective-permute-start.6 = (bf16[2,1,96,256]{3,2,1,0:T(8,128)(2,1)S(1)}, bf16[2,1,96,256]{3,2,1,0:T(8,128)(2,1)S(1)}, u32[]{:S(2)}, u32[]{:S(2)}) collective-permute-start(bf16[2,1,96,256]{3,2,1,0:T(8,128)(2,1)S(1)} %copy-done.126), channel_id=1, source_target_pairs={{0,3},{1,2},{2,1},{3,0},{4,7},{5,6},{6,5},{7,4},{8,11},{9,10},{10,... | collective-permute-start | bytes 294920 | tf_op jit(solution)/shard_map/ppermute | solution.py:252
  362.0 24.3 %collective-permute-start.7 = (bf16[2,1,96,256]{3,2,1,0:T(8,128)(2,1)S(1)}, bf16[2,1,96,256]{3,2,1,0:T(8,128)(2,1)S(1)}, u32[]{:S(2)}, u32[]{:S(2)}) collective-permute-start(bf16[2,1,96,256]{3,2,1,0:T(8,128)(2,1)S(1)} %copy-done.124), channel_id=1, source_target_pairs={{0,4},{1,5},{2,6},{3,7},{4,0},{5,1},{6,2},{7,3},{8,12},{9,13},{10,... | collective-permute-start | bytes 294920 | tf_op jit(solution)/shard_map/ppermute | solution.py:252
  362.7 23.7 %collective-permute-start.8 = (bf16[2,1,96,256]{3,2,1,0:T(8,128)(2,1)S(1)}, bf16[2,1,96,256]{3,2,1,0:T(8,128)(2,1)S(1)}, u32[]{:S(2)}, u32[]{:S(2)}) collective-permute-start(bf16[2,1,96,256]{3,2,1,0:T(8,128)(2,1)S(1)} %copy-done.122), channel_id=1, source_target_pairs={{0,5},{1,4},{2,7},{3,6},{4,1},{5,0},{6,3},{7,2},{8,13},{9,12},{10,... | collective-permute-start | bytes 294920 | tf_op jit(solution)/shard_map/ppermute | solution.py:252
  364.3 22.0 %collective-permute-start.9 = (bf16[2,1,96,256]{3,2,1,0:T(8,128)(2,1)S(1)}, bf16[2,1,96,256]{3,2,1,0:T(8,128)(2,1)S(1)}, u32[]{:S(2)}, u32[]{:S(2)}) collective-permute-start(bf16[2,1,96,256]{3,2,1,0:T(8,128)(2,1)S(1)} %copy-done.120), channel_id=1, source_target_pairs={{0,6},{1,7},{2,4},{3,5},{4,2},{5,3},{6,0},{7,1},{8,14},{9,15},{10,... | collective-permute-start | bytes 294920 | tf_op jit(solution)/shard_map/ppermute | solution.py:252
  (163 other events, 1178.0 us)
